TPU v7x, 32 devices: a whole 2x2x4 slice. The times are simulated.
32 devices in a mesh: pb: 4 (over y, core), an: 8 (over z, x).
Axes of the slice: x: 2, y: 2, z: 4, core: 2. Of those that a mesh axis runs over, the one named last changes fastest.
Arguments:
- child_ids: int32 [512, 256], P(('pb', 'an')), may hold values from 0 to 262143, as said below
- history_ids: int32 [512, 69], P(('pb', 'an')), may hold values from 0 to 262143, as said below
- node_table: bfloat16 [262144, 128], P(('pb', 'an')), may hold values from -6 to 6
- w_first: bfloat16 [256, 512], replicated, may hold values from -0.375 to 0.375
- b_first: float32 [512], replicated, may hold values from -3 to 3
- w_second: bfloat16 [512, 512], replicated, may hold values from -0.25 to 0.25
- b_second: float32 [512], replicated, may hold values from -3 to 3
- w_out: bfloat16 [512], replicated, may hold values from -0.25 to 0.25
Outputs:
- scores: float32 [512, 256], P(('pb', 'an'))
Inputs may be any that keep to these rules, and one draw needn't show every extreme that they name: `child_ids`: in each aligned block of 16 queries (the queries of one device), at most 320 of the child ids lie in any one aligned range of 8192 node ids; some range holds exactly 320 in every block. `history_ids`: in each aligned block of 16 queries, at most 35 of the history ids lie in any one aligned range of 8192 node ids, and some range holds exactly 35.
All inputs are finite; a program needn't handle non-finite values.
Results may differ from a plain program's by a relative error of at most 0.0034.
Values may be sent and summed in bfloat16 or wider, within the bound.
No kernel may reach another device: no remote copies, remote signals or barrier semaphores. Data moves between devices by JAX's collectives and lax.ppermute only.
A program may use at most 64 MiB of HBM per device.

v0:
```python
import jax
import jax.numpy as jnp
from jax import lax
from jax.sharding import PartitionSpec as P


def rank_within(owners, groups):
    total = owners.shape[0]
    block = 128
    padding = -total % block
    padded = jnp.concatenate([owners, jnp.full((padding,), -1, jnp.int32)])
    hits = (padded[:, None] == jnp.arange(groups, dtype=jnp.int32)[None, :]).astype(jnp.float32)
    hits = hits.reshape((total + padding) // block, block, groups)
    lower = (jnp.arange(block)[:, None] > jnp.arange(block)[None, :]).astype(jnp.float32)
    inside = jnp.einsum("ij,bjc->bic", lower, hits)
    totals = jnp.sum(hits, axis=1)
    before = jnp.cumsum(totals, axis=0) - totals
    ranking = jnp.sum((inside + before[:, None, :]) * hits, axis=2).reshape(total + padding)
    return ranking[:total].astype(jnp.int32)


def body(child_ids, history_ids, node_table, w_first, b_first, w_second, b_second, w_out):
    queries, children = child_ids.shape
    history = history_ids.shape[1]
    shard_rows, width = node_table.shape
    peers = lax.axis_size(("pb", "an"))
    row_count = queries * children
    past_count = queries * history
    capacity = 5 * row_count // (2 * peers)
    past_cap = (past_count + peers - 1) // peers
    slots = capacity + past_cap
    table_slots = peers * slots
    kid_flat = child_ids.reshape(row_count)
    past_flat = history_ids.reshape(past_count)
    kid_owner = kid_flat // shard_rows
    past_owner = past_flat // shard_rows
    kid_slot = kid_owner * slots + rank_within(kid_owner, peers)
    past_slot = past_owner * slots + capacity + rank_within(past_owner, peers)
    total = row_count + past_count
    all_slots = jnp.concatenate([kid_slot, past_slot])
    all_offsets = jnp.concatenate([kid_flat % shard_rows, past_flat % shard_rows])
    wanted = (
        jnp.zeros((table_slots,), jnp.int32).at[all_slots].set(all_offsets).reshape(peers, slots)
    )
    fetched = lax.all_to_all(
        jnp.take(
            node_table,
            lax.all_to_all(wanted, ("pb", "an"), split_axis=0, concat_axis=0, tiled=True),
            axis=0,
        ),
        ("pb", "an"),
        split_axis=0,
        concat_axis=0,
        tiled=True,
    )
    fetched = fetched.reshape(table_slots, width)
    picked = jnp.take(fetched, all_slots, axis=0)
    child_rows = picked[:row_count].reshape(queries, children, width)
    past_rows = picked[row_count:total].reshape(queries, history, width)
    logits = jnp.einsum(
        "qhe,qke->qhk", past_rows, child_rows, preferred_element_type=jnp.float32
    ) * width ** (-0.5)
    attend = (jax.nn.sigmoid(logits) * history ** (-0.5)).astype(jnp.bfloat16)
    pooled = jnp.einsum(
        "qhk,qhe->qke", attend, past_rows, preferred_element_type=jnp.float32
    ).astype(jnp.bfloat16)
    joined = jnp.concatenate([child_rows, pooled], axis=-1).reshape(row_count, 2 * width)
    first = jax.nn.relu(
        jnp.dot(joined, w_first, preferred_element_type=jnp.float32) + b_first
    ).astype(jnp.bfloat16)
    second = jax.nn.relu(
        jnp.dot(first, w_second, preferred_element_type=jnp.float32) + b_second
    ).astype(jnp.bfloat16)
    result = jnp.dot(second, w_out, preferred_element_type=jnp.float32)
    return result.reshape(queries, children)


def solution(mesh):
    placed = (
        P(("pb", "an"), None),
        P(("pb", "an"), None),
        P(("pb", "an"), None),
        P(),
        P(),
        P(),
        P(),
        P(),
    )
    return jax.shard_map(
        body, mesh=mesh, in_specs=placed, out_specs=P(("pb", "an"), None), check_vma=False
    )
```

profile of v0, /device:TPU:0, one launch (start us, length us, event | category | flops | bytes accessed | tf_op | source)
XLA Modules:
  0.0 183.9 jit_solution(13975592773965441702)
XLA Ops:
  0.0 0.0 copy-start
  0.0 0.9 reshape.250
  1.0 0.1 convert_reduce_fusion.1
  1.1 0.2 fusion.15
  1.4 0.7 reshape.249
  2.1 0.2 convert_reduce_fusion
  2.3 0.1 reduce_window_sum.22
  2.4 0.3 fusion.12
  2.7 0.7 copy.10
  3.4 0.1 fusion.27
  3.5 25.3 %scatter_custom_fusion = s32[11360]{0:T(1024)S(1)} fusion(s32[5200]{0:T(1024)S(1)} %fusion.27, s32[5200]{0:T(1024)S(1)} %pad_add_fusion, s32[]{:T(128)} %constant.86.clone.1), kind=kCustom, calls=%fused_computation.48 | custom fusion | bytes 45444 | tf_op jit(solution)/shard_map/scatter | solution.py:43
  28.8 0.2 all_to_all.13
  29.0 14.4 %all_to_all.20 = s32[32,1,355]{2,1,0:T(1,128)S(1)} all-to-all(s32[32,1,355]{2,1,0:T(1,128)S(1)} %all_to_all.13), channel_id=1, replica_groups=mesh['pb'=4,'an'=8] {'pb','an'}, dimensions={0} | all-to-all | bytes 90880 | tf_op jit(solution)/shard_map/all_to_all | solution.py:48
  43.3 0.2 fusion.24
  43.5 0.1 reshape.258
  43.7 0.0 copy-done
  43.7 23.8 %gather_fusion = bf16[11360,128]{1,0:T(8,128)(2,1)} fusion(bf16[8192,128]{1,0:T(8,128)(2,1)S(1)} %copy-done, s32[12288]{0:T(1024)S(1)} %pad_clamp_fusion), kind=kCustom, calls=%fused_computation | custom fusion | bytes 5861760 | tf_op jit(solution)/shard_map/jit(_take)/gather | solution.py:46
  67.5 4.5 %reshape.257 = bf16[32,355,128]{2,1,0:T(8,128)(2,1)} reshape(bf16[11360,128]{1,0:T(8,128)(2,1)} %gather_fusion) | data formatting | bytes 5816320 | tf_op jit(solution)/shard_map/jit(_take)/gather | solution.py:46
  71.9 6.9 %broadcast_select_fusion = bf16[32,355,128]{2,1,0:T(8,128)(2,1)} fusion(bf16[32,355,128]{2,1,0:T(8,128)(2,1)} %reshape.257, pred[32,355]{1,0:T(8,128)(4,1)S(1)} %compare_and_fusion), kind=kLoop, calls=%fused_computation.5 | loop fusion | flops 1454080 | bytes 5827680 | tf_op jit(solution)/shard_map/jit(_take)/select_n | solution.py:46
  78.8 0.0 copy-start.1
  78.8 3.6 %all-to-all-start.1 = ((bf16[32,355,128]{2,1,0:T(8,128)(2,1)}), bf16[32,355,128]{2,1,0:T(8,128)(2,1)}, u32[]{:S(2)}, u32[]{:S(2)}) async-start(bf16[32,355,128]{2,1,0:T(8,128)(2,1)} %broadcast_select_fusion), calls=%async_computation.1 | async-start | bytes 5898240 | tf_op jit(solution)/shard_map/all_to_all | solution.py:45
  82.5 0.0 copy-done.1
  82.6 68.2 %all-to-all-done.1 = bf16[32,355,128]{2,1,0:T(8,128)(2,1)} async-done(((bf16[32,355,128]{2,1,0:T(8,128)(2,1)}), bf16[32,355,128]{2,1,0:T(8,128)(2,1)}, u32[]{:S(2)}, u32[]{:S(2)}) %all-to-all-start.1) | async-done | bytes 2908192 | tf_op jit(solution)/shard_map/all_to_all | solution.py:45
  150.8 4.5 %reshape.252 = bf16[11360,128]{1,0:T(8,128)(2,1)} reshape(bf16[32,355,128]{2,1,0:T(8,128)(2,1)} %all-to-all-done.1) | data formatting | bytes 5816320 | tf_op jit(solution)/shard_map/reshape | solution.py:56
  155.3 11.2 %gather_fusion.1 = bf16[5200,128]{1,0:T(8,128)(2,1)S(1)} fusion(bf16[11360,128]{1,0:T(8,128)(2,1)} %reshape.252, s32[6144]{0:T(1024)S(1)} %pad_clamp_fusion.1), kind=kCustom, calls=%fused_computation.1 | custom fusion | bytes 2683200 | tf_op jit(solution)/shard_map/jit(_take)/gather | solution.py:57
  166.4 2.7 %broadcast_select_fusion.1 = bf16[5200,128]{1,0:T(8,128)(2,1)S(1)} fusion(bf16[5200,128]{1,0:T(8,128)(2,1)S(1)} %gather_fusion.1, pred[5200]{0:T(1024)(128)(4,1)S(1)} %compare_and_fusion.1), kind=kLoop, calls=%fused_computation.17 | loop fusion | flops 665600 | bytes 2667600 | tf_op jit(solution)/shard_map/jit(_take)/select_n | solution.py:57
  169.2 0.1 slice.17
  169.3 0.8 reshape.253
  170.1 0.0 copy-start.2
  170.1 0.0 copy-start.3
  170.1 3.1 %convolution_convert_fusion = bf16[16,256,128]{2,1,0:T(8,128)(2,1)} fusion(bf16[16,69,128]{2,1,0:T(8,128)(2,1)} %reshape.253, bf16[16,256,128]{2,1,0:T(8,128)(2,1)S(1)} %bitcast.40), kind=kOutput, calls=%fused_computation.10 | convolution fusion | flops 146923520 | bytes 2379776 | tf_op jit(solution)/shard_map/qhk,qhe->qke/dot_general | solution.py:64
  173.2 0.0 copy-done.2
  173.2 0.0 copy-done.3
  173.2 0.0 copy-start.4
  173.2 4.4 %maximum_convert_fusion.1 = bf16[4096,512]{1,0:T(8,128)(2,1)} fusion(bf16[256,512]{1,0:T(8,128)(2,1)S(1)} %copy-done.2, f32[512]{0:T(512)S(1)} %copy-done.3, bf16[4096,128]{1,0:T(8,128)(2,1)} %bitcast.46, bf16[4096,128]{1,0:T(8,128)(2,1)S(1)} %slice.17), kind=kOutput, calls=%fused_computation.4 | convolution fusion | flops 1084227584 | bytes 6555648 | tf_op jit(solution)/shard_map/dot_general | solution.py:69
  177.7 0.0 copy-done.4
  177.7 5.6 %fusion.3 = f32[1,4096]{1,0:T(1,128)S(1)} fusion(bf16[512,1]{0,1:T(2,128)(2,1)S(1)} %reshape.282, bf16[4096,512]{1,0:T(8,128)(2,1)} %maximum_convert_fusion.1, bf16[512,512]{1,0:T(8,128)(2,1)} %param.13, f32[512]{0:T(512)S(1)} %copy-done.4), kind=kOutput, calls=%fused_computation.9 | convolution fusion | flops 2157969408 | bytes 4738048 | tf_op jit(solution)/shard_map/dot_general | solution.py:74
  183.3 0.6 reshape.255
  (16 shorter events, 0.2 us)
Async XLA Ops:
  0.0 43.7 %copy-start = (bf16[8192,128]{1,0:T(8,128)(2,1)S(1)}, bf16[8192,128]{1,0:T(8,128)(2,1)}, u32[]{:S(2)}) copy-start(bf16[8192,128]{1,0:T(8,128)(2,1)} %param.10) | copy-start | bytes 6291460
  78.8 3.7 %copy-start.1 = (bf16[512]{0:T(512)(128)(2,1)S(1)}, bf16[512]{0:T(512)(128)(2,1)}, u32[]{:S(2)}) copy-start(bf16[512]{0:T(512)(128)(2,1)} %param.15) | copy-start | bytes 3076
  78.8 71.9 %all-to-all-start.1 = ((bf16[32,355,128]{2,1,0:T(8,128)(2,1)}), bf16[32,355,128]{2,1,0:T(8,128)(2,1)}, u32[]{:S(2)}, u32[]{:S(2)}) async-start(bf16[32,355,128]{2,1,0:T(8,128)(2,1)} %broadcast_select_fusion), calls=%async_computation.1 | async-start | bytes 5898240 | tf_op jit(solution)/shard_map/all_to_all | solution.py:45
  170.1 3.1 %copy-start.2 = (bf16[256,512]{1,0:T(8,128)(2,1)S(1)}, bf16[256,512]{1,0:T(8,128)(2,1)}, u32[]{:S(2)}) copy-start(bf16[256,512]{1,0:T(8,128)(2,1)} %param.11) | copy-start | bytes 786436
  170.1 3.1 %copy-start.3 = (f32[512]{0:T(512)S(1)}, f32[512]{0:T(512)}, u32[]{:S(2)}) copy-start(f32[512]{0:T(512)} %param.12) | copy-start | bytes 6148
  173.2 4.4 %copy-start.4 = (f32[512]{0:T(512)S(1)}, f32[512]{0:T(512)}, u32[]{:S(2)}) copy-start(f32[512]{0:T(512)} %param.14) | copy-start | bytes 6148
where the time goes:
time: 185 us; the launch traced here: 184 us
  local copies, waits for them, and re-layouts  73.4 us (40%)
  waiting for transfers between devices  68.2 us (37%)
  blocking collectives  14.4 us (8%)
  matrix products  13.7 us (7%)
  other arithmetic  10.4 us (6%)
  starting transfers between devices  3.65 us (2%)
    all_to_all x1, waiting for transfers between devices, body(): lax.all_to_all(jnp.take(node_table, lax.all_to_all(wanted, ('pb', 'an'),...  68.2 us
    gather x2, local copies, waits for them, and re-layouts, body(): jnp.take(node_table, lax.all_to_all(wanted, ('pb', 'an'), split_axis=0, c...  28.3 us
    scatter x1, local copies, waits for them, and re-layouts, body(): jnp.zeros((table_slots,), jnp.int32).at[all_slots].set(all_offsets)  25.3 us
    all_to_all x1, blocking collectives, body(): lax.all_to_all(wanted, ('pb', 'an'), split_axis=0, concat_axis=0, tiled=T...  14.4 us
    gather x1, local copies, waits for them, and re-layouts, body(): picked = jnp.take(fetched, all_slots, axis=0)  11.2 us
    select_n x2, other arithmetic, body(): jnp.take(node_table, lax.all_to_all(wanted, ('pb', 'an'), split_axis=0, c...  7.05 us
    dot_general x1, matrix products, body(): result = jnp.dot(second, w_out, preferred_element_type=jnp.float32)  5.63 us
    reshape x1, local copies, waits for them, and re-layouts, body(): fetched = fetched.reshape(table_slots, width)  4.47 us
  transfers between devices with their start and end apart: 1, of which 1 were waited for; matrix products, arithmetic and copies ran while one was open for 0% of the time, Pallas kernels for 0%

commit v1 on v0

--- a/solution.py
+++ b/solution.py
@@ -19,6 +19,15 @@
     return ranking[:total].astype(jnp.int32)
 
 
+def place(owners, ranks, offsets, groups, slots):
+    hit = owners[:, None] == jnp.arange(groups, dtype=jnp.int32)[None, :]
+    high = jnp.where(hit, (offsets // 256)[:, None], 0).astype(jnp.bfloat16)
+    low = jnp.where(hit, (offsets % 256)[:, None], 0).astype(jnp.bfloat16)
+    spot = (ranks[:, None] == jnp.arange(slots, dtype=jnp.int32)[None, :]).astype(jnp.bfloat16)
+    digits = jnp.einsum("io,is->os", jnp.concatenate([high, low], axis=1), spot, preferred_element_type=jnp.float32)
+    return digits[:groups].astype(jnp.int32) * 256 + digits[groups:].astype(jnp.int32)
+
+
 def body(child_ids, history_ids, node_table, w_first, b_first, w_second, b_second, w_out):
     queries, children = child_ids.shape
     history = history_ids.shape[1]
@@ -28,33 +37,33 @@
     past_count = queries * history
     capacity = 5 * row_count // (2 * peers)
     past_cap = (past_count + peers - 1) // peers
+    past_cap += -(capacity + past_cap) % 8
     slots = capacity + past_cap
     table_slots = peers * slots
     kid_flat = child_ids.reshape(row_count)
     past_flat = history_ids.reshape(past_count)
     kid_owner = kid_flat // shard_rows
     past_owner = past_flat // shard_rows
-    kid_slot = kid_owner * slots + rank_within(kid_owner, peers)
-    past_slot = past_owner * slots + capacity + rank_within(past_owner, peers)
+    kid_rank = rank_within(kid_owner, peers)
+    past_rank = rank_within(past_owner, peers)
+    kid_slot = kid_owner * slots + kid_rank
+    past_slot = past_owner * slots + capacity + past_rank
     total = row_count + past_count
     all_slots = jnp.concatenate([kid_slot, past_slot])
-    all_offsets = jnp.concatenate([kid_flat % shard_rows, past_flat % shard_rows])
-    wanted = (
-        jnp.zeros((table_slots,), jnp.int32).at[all_slots].set(all_offsets).reshape(peers, slots)
+    wanted = jnp.concatenate(
+        [
+            place(kid_owner, kid_rank, kid_flat % shard_rows, peers, capacity),
+            place(past_owner, past_rank, past_flat % shard_rows, peers, past_cap),
+        ],
+        axis=1,
     )
+    asked = lax.all_to_all(wanted, ("pb", "an"), split_axis=0, concat_axis=0, tiled=True)
+    rows = node_table.at[asked.reshape(table_slots)].get(mode="promise_in_bounds")
     fetched = lax.all_to_all(
-        jnp.take(
-            node_table,
-            lax.all_to_all(wanted, ("pb", "an"), split_axis=0, concat_axis=0, tiled=True),
-            axis=0,
-        ),
-        ("pb", "an"),
-        split_axis=0,
-        concat_axis=0,
-        tiled=True,
+        rows.reshape(peers, slots, width), ("pb", "an"), split_axis=0, concat_axis=0, tiled=True
     )
     fetched = fetched.reshape(table_slots, width)
-    picked = jnp.take(fetched, all_slots, axis=0)
+    picked = fetched.at[all_slots].get(mode="promise_in_bounds")
     child_rows = picked[:row_count].reshape(queries, children, width)
     past_rows = picked[row_count:total].reshape(queries, history, width)
     logits = jnp.einsum(

time: 185 us -> 146 us (0.79)
  local copies, waits for them, and re-layouts: 73.4 us -> 41 us
  other arithmetic: 10.4 us -> 1.84 us
  matrix products: 13.7 us -> 15.8 us
    scatter x1 -> x0, local copies, waits for them, and re-layouts: 25.3 us -> none  [body(): jnp.zeros((table_slots,), jnp.int32).at[all_slots].set(all_offsets)]
    select_n x6 -> x2, other arithmetic: 9.89 us -> 0.21 us  [the longest x1 0.14 us: body(): node_table.at[asked.reshape(table_slots)].get(mode='promise_in_bounds')]
    gather x3 -> x2, local copies, waits for them, and re-layouts: 39.4 us -> 35 us  [the longest x1 23.8 us: body(): node_table.at[asked.reshape(table_slots)].get(mode='promise_in_bounds')]
    reshape x1, local copies, waits for them, and re-layouts: 4.47 us -> 0.13 us  [body(): asked.reshape(table_slots)]
    dot_general x0 -> x2, matrix products: none -> 1.85 us  [place(): jnp.einsum('io,is->os', jnp.concatenate([high, low], axis=1), spot, prefe...]
where the time goes in v1:
time: 146 us; the launch traced here: 145 us
  waiting for transfers between devices  68.2 us (47%)
  local copies, waits for them, and re-layouts  41 us (28%)
  matrix products  15.8 us (11%)
  blocking collectives  14.4 us (10%)
  starting transfers between devices  3.65 us (2%)
  other arithmetic  1.84 us (1%)
    all_to_all x1, waiting for transfers between devices, body(): lax.all_to_all(rows.reshape(peers, slots, width), ('pb', 'an'), split_axi...  68.2 us
    gather x1, local copies, waits for them, and re-layouts, body(): node_table.at[asked.reshape(table_slots)].get(mode='promise_in_bounds')  23.8 us
    all_to_all x1, blocking collectives, body(): lax.all_to_all(wanted, ('pb', 'an'), split_axis=0, concat_axis=0, tiled=T...  14.4 us
    gather x1, local copies, waits for them, and re-layouts, body(): picked = fetched.at[all_slots].get(mode='promise_in_bounds')  11.2 us
    dot_general x1, matrix products, body(): result = jnp.dot(second, w_out, preferred_element_type=jnp.float32)  5.64 us
    dot_general x1, matrix products, body(): jnp.dot(joined, w_first, preferred_element_type=jnp.float32) + b_first  4.46 us
    all_to_all x1, starting transfers between devices, body(): lax.all_to_all(rows.reshape(peers, slots, width), ('pb', 'an'), split_axi...  3.65 us
    dot_general x1, matrix products, body(): jnp.einsum('qhk,qhe->qke', attend, past_rows, preferred_element_type=jnp....  3.36 us
  transfers between devices with their start and end apart: 1, of which 1 were waited for; matrix products, arithmetic and copies ran while one was open for 0% of the time, Pallas kernels for 0%

profile of v1, /device:TPU:0, one launch (start us, length us, event | category | flops | bytes accessed | tf_op | source)
XLA Modules:
  0.0 145.1 jit_solution(10664567140895448151)
XLA Ops:
  0.0 0.0 copy-start
  0.0 0.9 reshape.385
  1.0 0.1 convert_reduce_fusion.1
  1.1 0.2 fusion.17
  1.4 0.8 select_convert_fusion.1
  2.2 0.5 fusion.21
  2.7 0.7 reshape.384
  3.4 0.2 convert_reduce_fusion
  3.6 0.1 reduce_window_sum.22
  3.7 0.3 fusion.14
  4.0 0.7 copy.20
  4.8 0.1 select_convert_fusion.3
  4.9 1.4 fusion
  6.3 0.1 add_bitcast_fusion
  6.4 0.1 copy.18
  6.4 14.4 %all_to_all.14 = s32[32,1,360]{2,1,0:T(1,128)S(1)} all-to-all(s32[32,1,360]{2,1,0:T(1,128)S(1)} %copy.18), channel_id=1, replica_groups=mesh['pb'=4,'an'=8] {'pb','an'}, dimensions={0} | all-to-all | bytes 92160 | tf_op jit(solution)/shard_map/all_to_all | solution.py:60
  20.8 0.1 reduce
  20.9 0.1 reshape.387
  21.0 0.1 fusion.36
  21.2 0.0 copy-done
  21.2 23.8 %gather_fusion = bf16[11520,128]{1,0:T(8,128)(2,1)} fusion(bf16[8192,128]{1,0:T(8,128)(2,1)S(1)} %copy-done, s32[12288]{0:T(1024)S(1)} %pad_clamp_fusion), kind=kCustom, calls=%fused_computation | custom fusion | bytes 5944320 | tf_op jit(solution)/shard_map/gather | solution.py:61
  45.0 0.0 copy-start.2
  45.0 3.6 %all-to-all-start.1 = ((bf16[32,360,128]{2,1,0:T(8,128)(2,1)}), bf16[32,360,128]{2,1,0:T(8,128)(2,1)}, u32[]{:S(2)}, u32[]{:S(2)}) async-start(bf16[32,360,128]{2,1,0:T(8,128)(2,1)} %bitcast.40), calls=%async_computation.1 | async-start | bytes 5898240 | tf_op jit(solution)/shard_map/all_to_all | solution.py:62
  48.7 0.0 copy-done.2
  48.7 0.1 fusion.37
  48.8 68.2 %all-to-all-done.1 = bf16[32,360,128]{2,1,0:T(8,128)(2,1)} async-done(((bf16[32,360,128]{2,1,0:T(8,128)(2,1)}), bf16[32,360,128]{2,1,0:T(8,128)(2,1)}, u32[]{:S(2)}, u32[]{:S(2)}) %all-to-all-start.1) | async-done | bytes 2949152 | tf_op jit(solution)/shard_map/all_to_all | solution.py:62
  116.9 11.2 %gather_fusion.1 = bf16[5200,128]{1,0:T(8,128)(2,1)S(1)} fusion(bf16[11520,128]{1,0:T(8,128)(2,1)} %bitcast.8, s32[6144]{0:T(1024)S(1)} %pad_clamp_fusion.1), kind=kCustom, calls=%fused_computation.1 | custom fusion | bytes 2683200 | tf_op jit(solution)/shard_map/gather | solution.py:66
  128.1 1.1 slice.37
  129.2 0.7 slice.38
  129.9 1.1 reshape.390
  131.0 0.0 copy-start.1
  131.0 0.0 copy-start.3
  131.0 3.4 %convolution_convert_fusion = bf16[16,256,128]{2,1,0:T(8,128)(2,1)} fusion(bf16[16,69,128]{2,1,0:T(8,128)(2,1)S(1)} %reshape.390, bf16[16,256,128]{2,1,0:T(8,128)(2,1)} %bitcast.41), kind=kOutput, calls=%fused_computation.11 | convolution fusion | flops 146923520 | bytes 2379776 | tf_op jit(solution)/shard_map/qhk,qhe->qke/dot_general | solution.py:73
  134.4 0.0 copy-done.1
  134.4 0.0 copy-done.3
  134.4 0.0 copy-start.4
  134.4 4.5 %maximum_convert_fusion.1 = bf16[4096,512]{1,0:T(8,128)(2,1)} fusion(bf16[256,512]{1,0:T(8,128)(2,1)} %param.11, f32[512]{0:T(512)S(1)} %copy-done.3, bf16[4096,128]{1,0:T(8,128)(2,1)} %bitcast.48, bf16[4096,128]{1,0:T(8,128)(2,1)S(1)} %copy-done.1), kind=kOutput, calls=%fused_computation.3 | convolution fusion | flops 1084227584 | bytes 6555648 | tf_op jit(solution)/shard_map/dot_general | solution.py:78
  138.8 0.0 copy-done.4
  138.8 5.6 %fusion.5 = f32[1,4096]{1,0:T(1,128)S(1)} fusion(bf16[512,1]{0,1:T(2,128)(2,1)S(1)} %reshape.410, bf16[4096,512]{1,0:T(8,128)(2,1)} %maximum_convert_fusion.1, bf16[512,512]{1,0:T(8,128)(2,1)} %param.13, f32[512]{0:T(512)S(1)} %copy-done.4), kind=kOutput, calls=%fused_computation.10 | convolution fusion | flops 2157969408 | bytes 4738048 | tf_op jit(solution)/shard_map/dot_general | solution.py:83
  144.5 0.6 reshape.392
  (16 shorter events, 0.2 us)
Async XLA Ops:
  0.0 21.2 %copy-start = (bf16[8192,128]{1,0:T(8,128)(2,1)S(1)}, bf16[8192,128]{1,0:T(8,128)(2,1)}, u32[]{:S(2)}) copy-start(bf16[8192,128]{1,0:T(8,128)(2,1)} %param.10) | copy-start | bytes 6291460
  45.0 3.7 %copy-start.2 = (bf16[512]{0:T(512)(128)(2,1)S(1)}, bf16[512]{0:T(512)(128)(2,1)}, u32[]{:S(2)}) copy-start(bf16[512]{0:T(512)(128)(2,1)} %param.15) | copy-start | bytes 3076
  45.0 71.9 %all-to-all-start.1 = ((bf16[32,360,128]{2,1,0:T(8,128)(2,1)}), bf16[32,360,128]{2,1,0:T(8,128)(2,1)}, u32[]{:S(2)}, u32[]{:S(2)}) async-start(bf16[32,360,128]{2,1,0:T(8,128)(2,1)} %bitcast.40), calls=%async_computation.1 | async-start | bytes 5898240 | tf_op jit(solution)/shard_map/all_to_all | solution.py:62
  131.0 3.4 %copy-start.1 = (bf16[4096,128]{1,0:T(8,128)(2,1)S(1)}, bf16[4096,128]{1,0:T(8,128)(2,1)}, u32[]{:S(2)}) copy-start(bf16[4096,128]{1,0:T(8,128)(2,1)} %slice.37) | copy-start | bytes 3145732
  131.0 3.4 %copy-start.3 = (f32[512]{0:T(512)S(1)}, f32[512]{0:T(512)}, u32[]{:S(2)}) copy-start(f32[512]{0:T(512)} %param.12) | copy-start | bytes 6148
  134.4 4.5 %copy-start.4 = (f32[512]{0:T(512)S(1)}, f32[512]{0:T(512)}, u32[]{:S(2)}) copy-start(f32[512]{0:T(512)} %param.14) | copy-start | bytes 6148

commit v2 on v1

v2 whole, which is shorter than its diff:
```python
import jax
import jax.numpy as jnp
from jax import lax
from jax.experimental import pallas as pl
from jax.experimental.pallas import tpu as pltpu
from jax.sharding import Mesh
from jax.sharding import PartitionSpec as P

AXES = ("pb", "ah", "al")
HALF = ("pb", "al")
BLOCK = 512


def rounded(n, m):
    return -(-n // m) * m


def unroll_of(n, most=64):
    return max(u for u in range(1, most + 1) if n % u == 0)


def rank_within(owners, groups):
    total = owners.shape[0]
    block = 128
    padding = -total % block
    padded = jnp.concatenate([owners, jnp.full((padding,), -1, jnp.int32)])
    hits = (padded[:, None] == jnp.arange(groups, dtype=jnp.int32)[None, :]).astype(jnp.float32)
    hits = hits.reshape((total + padding) // block, block, groups)
    lower = (jnp.arange(block)[:, None] > jnp.arange(block)[None, :]).astype(jnp.float32)
    inside = jnp.einsum("ij,bjc->bic", lower, hits)
    totals = jnp.sum(hits, axis=1)
    before = jnp.cumsum(totals, axis=0) - totals
    ranking = jnp.sum((inside + before[:, None, :]) * hits, axis=2).reshape(total + padding)
    return ranking[:total].astype(jnp.int32)


def place(owners, ranks, offsets, groups, slots):
    hit = owners[:, None] == jnp.arange(groups, dtype=jnp.int32)[None, :]
    high = jnp.where(hit, (offsets // 256)[:, None], 0).astype(jnp.bfloat16)
    low = jnp.where(hit, (offsets % 256)[:, None], 0).astype(jnp.bfloat16)
    spot = (ranks[:, None] == jnp.arange(slots, dtype=jnp.int32)[None, :]).astype(jnp.bfloat16)
    digits = jnp.einsum("io,is->os", jnp.concatenate([high, low], axis=1), spot, preferred_element_type=jnp.float32)
    return digits[:groups].astype(jnp.int32) * 256 + digits[groups:].astype(jnp.int32)


VMEM = pl.BlockSpec(memory_space=pltpu.VMEM)
SMEM = pl.BlockSpec(memory_space=pltpu.SMEM)


def widen(src, dst, rows, at=0, step=128):
    def go(i, c):
        dst[pl.ds(at + i * step, step), :] = src[pl.ds(i * step, step), :].astype(jnp.float32)
        return c

    step = unroll_of(rows // 8, step // 8) * 8
    lax.fori_loop(0, rows // step, go, 0)


def narrow(src, dst, rows, step=128):
    def go(i, c):
        dst[pl.ds(i * step, step), :] = src[pl.ds(i * step, step), :].astype(jnp.bfloat16)
        return c

    step = unroll_of(rows // 8, step // 8) * 8
    lax.fori_loop(0, rows // step, go, 0)


def gather_slabs(asked, order, table, shifts, capacity, stride, past_half, peers, al_n):
    width = table.shape[1]
    slab = 2 * capacity
    unroll = unroll_of(capacity)
    per = capacity // unroll

    def kernel(order_ref, asked_ref, table_ref, *rest):
        outs, wide, spare = rest[:-2], rest[-2], rest[-1]
        widen(table_ref, wide, table_ref.shape[0])
        if past_half:
            pasts, outs = outs[0], outs[1:]

            def past(d, c):
                at = d * stride + capacity
                rows = [wide[pl.ds(asked_ref[at + i], 1), :] for i in range(past_half)]
                mate = d + al_n * (1 - 2 * ((d // al_n) % 2))
                for i, row in enumerate(rows):
                    spare[pl.ds(d * 2 * past_half + i, 1), :] = row
                for i, row in enumerate(rows):
                    spare[pl.ds((mate * 2 + 1) * past_half + i, 1), :] = row
                return c

            lax.fori_loop(0, peers, past, 0)
            narrow(spare, pasts, peers * 2 * past_half)
        for out, shift in zip(outs, shifts):

            def child(t, c, shift=shift):
                at = order_ref[2 * shift + t // per] + (t % per) * unroll
                rows = [wide[pl.ds(asked_ref[at + i], 1), :] for i in range(unroll)]
                for i, row in enumerate(rows):
                    spare[pl.ds(t * unroll + i, 1), :] = row
                return c

            lax.fori_loop(0, 2 * per, child, 0)
            narrow(spare, out, slab)

    shapes = [jax.ShapeDtypeStruct((slab, width), table.dtype)] * len(shifts)
    spare_rows = slab
    if past_half:
        shapes = [jax.ShapeDtypeStruct((peers * 2 * past_half, width), table.dtype)] + shapes
        spare_rows = max(slab, peers * 2 * past_half)
    return pl.pallas_call(
        kernel,
        out_shape=shapes,
        in_specs=[SMEM, SMEM, VMEM],
        out_specs=[VMEM] * len(shapes),
        scratch_shapes=[
            pltpu.VMEM(table.shape, jnp.float32),
            pltpu.VMEM((spare_rows, width), jnp.float32),
        ],
        name="gather_past" if past_half else "gather_slabs",
    )(order, asked, table)


def arrange_past(slots, fetched, queries, history, lanes):
    rows, width = fetched.shape

    def kernel(slot_ref, in_ref, out_ref, wide, spare):
        widen(in_ref, wide, rows)
        spare[...] = jnp.zeros(spare.shape, jnp.float32)

        def one(q, c):
            for lo in range(0, history, 35):
                part = range(lo, min(lo + 35, history))
                vals = [wide[pl.ds(slot_ref[q * history + h], 1), :] for h in part]
                for h, val in zip(part, vals):
                    spare[pl.ds(h, 1), :] = val
            out_ref[pl.ds(pl.multiple_of(q * lanes, lanes), lanes), :] = spare[...].astype(jnp.bfloat16)
            return c

        lax.fori_loop(0, queries, one, 0)

    return pl.pallas_call(
        kernel,
        out_shape=jax.ShapeDtypeStruct((queries * lanes, width), fetched.dtype),
        in_specs=[SMEM, VMEM],
        out_specs=VMEM,
        scratch_shapes=[pltpu.VMEM((rows, width), jnp.float32), pltpu.VMEM((lanes, width), jnp.float32)],
        name="arrange_past",
    )(slots, fetched)


def score_rows(segments, bases, rel, slabs, past, w_first, b_first, w_second, b_second, w_out, history, lanes):
    queries, children = rel.shape
    slab, width = slabs[0].shape
    parts = len(slabs)
    hidden = w_second.shape[0]
    longest = queries * children // 2 + children
    longest = rounded(queries * children + queries * 8, BLOCK)
    per_block = BLOCK // 128
    quick = 3
    group = 4

    def kernel(seg_ref, base_ref, rel_ref, past_ref, w1, b1, w2, b2, wo, *rest):
        slab_refs, out_ref = rest[:parts], rest[parts]
        wide, rows, pool, line, g0, g1, g2 = rest[parts + 1 :]
        for i, ref in enumerate(slab_refs):
            widen(ref, wide, slab, at=i * slab)
        spots = lax.broadcasted_iota(jnp.int32, (8, width), 0)

        def segment(t, c):
            src = seg_ref[t]
            dst = seg_ref[queries * parts + t]
            count = seg_ref[2 * queries * parts + t]
            chunks = [wide[pl.ds(src + 8 * i, 8), :] for i in range(quick)]
            for i, chunk in enumerate(chunks):
                pltpu.store(rows.at[pl.ds(dst + 8 * i, 8), :], chunk, mask=spots < count - 8 * i)

            def more(i, c):
                pltpu.store(
                    rows.at[pl.ds(dst + 8 * i, 8), :],
                    wide[pl.ds(src + 8 * i, 8), :],
                    mask=spots < count - 8 * i,
                )
                return c

            lax.fori_loop(quick, (count + 7) // 8, more, 0)
            return c

        lax.fori_loop(0, queries * parts, segment, 0)

        def attend(g, c):
            for i in range(group):
                q = g * group + i
                base = pl.multiple_of(base_ref[q], 8)
                kids = rows[pl.ds(base, children), :].astype(jnp.bfloat16)
                own = past_ref[pl.ds(pl.multiple_of(q * lanes, lanes), lanes), :]
                logits = lax.dot_general(kids, own, (((1,), (1,)), ((), ())), preferred_element_type=jnp.float32)
                logits = logits * width ** (-0.5)
                share = (jax.nn.sigmoid(logits) * history ** (-0.5)).astype(jnp.bfloat16)
                pool[pl.ds(base, children), :] = jnp.dot(share, own, preferred_element_type=jnp.float32)
            return c

        lax.fori_loop(0, queries // group, attend, 0)

        def dense(b, c):
            at = pl.multiple_of(b * BLOCK, BLOCK)
            kids = rows[pl.ds(at, BLOCK), :].astype(jnp.bfloat16)
            pooled = pool[pl.ds(at, BLOCK), :].astype(jnp.bfloat16)
            joined = jnp.concatenate([kids, pooled], axis=1)
            first = jnp.dot(joined, w1[...], preferred_element_type=jnp.float32) + b1[...]
            first = jnp.maximum(first, 0.0).astype(jnp.bfloat16)
            second = jnp.dot(first, w2[...], preferred_element_type=jnp.float32) + b2[...]
            second = jnp.maximum(second, 0.0).astype(jnp.bfloat16)
            out = lax.dot_general(wo[...], second, (((1,), (1,)), ((), ())), preferred_element_type=jnp.float32)
            for i in range(per_block):
                line[pl.ds(b * per_block + i, 1), :] = out[0:1, i * 128 : (i + 1) * 128]
            return c

        lax.fori_loop(0, (base_ref[queries] + BLOCK - 1) // BLOCK, dense, 0)
        for q in range(queries):
            at = base_ref[q] // 128
            for i, ref in enumerate((g0, g1, g2)):
                ref[q : q + 1, :] = line[pl.ds(at + i, 1), :]
        for q in range(0, queries, 8):
            for k in range(0, children, 128):
                spot = rel_ref[q : q + 8, k : k + 128]
                lane = spot & 127
                took = [jnp.take_along_axis(ref[q : q + 8, :], lane, axis=1) for ref in (g0, g1, g2)]
                out_ref[q : q + 8, k : k + 128] = jnp.where(
                    spot < 128, took[0], jnp.where(spot < 256, took[1], took[2])
                )

    wide_rows = parts * slab + 8 * quick
    return pl.pallas_call(
        kernel,
        out_shape=jax.ShapeDtypeStruct((queries, children), jnp.float32),
        in_specs=[SMEM, SMEM] + [VMEM] * (7 + parts),
        out_specs=VMEM,
        scratch_shapes=[
            pltpu.VMEM((wide_rows, width), jnp.float32),
            pltpu.VMEM((longest + children, width), jnp.float32),
            pltpu.VMEM((longest + children, width), jnp.float32),
            pltpu.VMEM((rounded(longest // 128 + 3, 8), 128), jnp.float32),
        ]
        + [pltpu.VMEM((queries, 128), jnp.float32)] * 3,
        name="score_rows",
    )(
        segments,
        bases,
        rel,
        past,
        w_first,
        b_first.reshape(1, hidden),
        w_second,
        b_second.reshape(1, hidden),
        jnp.broadcast_to(w_out[None, :], (8, hidden)),
        *slabs,
    )


def body(child_ids, history_ids, node_table, w_first, b_first, w_second, b_second, w_out):
    queries, children = child_ids.shape
    history = history_ids.shape[1]
    shard_rows, width = node_table.shape
    pb_n, al_n = lax.axis_size("pb"), lax.axis_size("al")
    peers, near = 2 * pb_n * al_n, pb_n * al_n
    pb, ah, al = (lax.axis_index(a) for a in AXES)
    here = pb * al_n + al
    row_count = queries * children
    past_count = queries * history
    capacity = 5 * row_count // (2 * peers)
    past_cap = (past_count + peers - 1) // peers
    past_half = rounded(past_cap, 4)
    stride = rounded(capacity + past_half, 128)
    power = near & (near - 1) == 0

    kid_flat = child_ids.reshape(row_count)
    past_flat = history_ids.reshape(past_count)
    kid_owner = kid_flat // shard_rows
    past_owner = past_flat // shard_rows
    kid_rank = rank_within(kid_owner, peers)
    past_rank = rank_within(past_owner, peers)
    wanted = jnp.concatenate(
        [
            place(kid_owner, kid_rank, kid_flat % shard_rows, peers, capacity),
            place(past_owner, past_rank, past_flat % shard_rows, peers, stride - capacity),
        ],
        axis=1,
    )
    asked = lax.all_to_all(wanted.reshape(peers, 1, stride), AXES, split_axis=0, concat_axis=0, tiled=True)
    asked = asked.reshape(peers * stride)

    shifts = jnp.arange(near, dtype=jnp.int32)
    target = (here ^ shifts) if power else (here + shifts) % near
    lists = (target // al_n) * (2 * al_n) + target % al_n
    order = jnp.stack([lists + ah * al_n, lists + (1 - ah) * al_n], axis=1).reshape(2 * near) * stride

    pairs = [(i, (i ^ s) if power else (i + s) % near) for s in range(near) for i in range(near)]
    steps = sorted(range(near), key=lambda s: (s == 0, -bin(s).count("1"), -s))
    first_cut = max(1, near // 8)
    second_cut = near // 2
    waves = [steps[:first_cut], steps[first_cut:second_cut], steps[second_cut:]]
    slabs = [None] * near
    for number, wave in enumerate(waves):
        outs = gather_slabs(
            asked, order, node_table, wave, capacity, stride, past_half if number == 0 else 0, peers, al_n
        )
        if number == 0:
            past_out, outs = outs[0], outs[1:]
            past_in = lax.all_to_all(
                past_out.reshape(peers, 2 * past_half, width), AXES, split_axis=0, concat_axis=0, tiled=True
            ).reshape(peers * 2 * past_half, width)
        for shift, out in zip(wave, outs):
            slabs[shift] = lax.ppermute(out, HALF, pairs[shift * near : (shift + 1) * near]) if shift else out

    ids = jnp.concatenate([child_ids, past_owner.reshape(queries, history), past_rank.reshape(queries, history)], axis=1)
    swap = [(0, 1), (1, 0)]
    mate_ids = lax.ppermute(ids, "ah", swap)
    both = jnp.stack([ids, mate_ids])
    kids = both[:, :, :children]
    owner = kids // shard_rows
    local = (owner // (2 * al_n)) * al_n + owner % al_n
    inside_half = (owner // al_n) % 2 == ah
    part = (local ^ here) if power else (here - local) % near
    part = jnp.where(inside_half, part, near)
    hits = (part.reshape(2 * queries, children)[:, :, None] == jnp.arange(near, dtype=jnp.int32)).astype(jnp.bfloat16)
    lower = (jnp.arange(children)[:, None] > jnp.arange(children)[None, :]).astype(jnp.bfloat16)
    before = jnp.einsum("kj,qjx->qkx", lower, hits, preferred_element_type=jnp.float32)
    counts = jnp.sum(hits.astype(jnp.float32), axis=1).astype(jnp.int32)
    blocked = counts.reshape(2, queries, near)
    starts = (jnp.cumsum(blocked, axis=1) - blocked).reshape(2 * queries, near)
    offsets = jnp.cumsum(counts, axis=1) - counts
    lengths = (jnp.sum(counts, axis=1) + 7) // 8 * 8
    ends = jnp.cumsum(lengths)
    bases = ends - lengths
    spot = jnp.sum((before + offsets.astype(jnp.float32)[:, None, :]) * hits.astype(jnp.float32), axis=2).astype(jnp.int32)
    rel = spot + (bases % 128)[:, None]
    which = (jnp.arange(2 * queries, dtype=jnp.int32) // queries)[:, None]
    source = jnp.arange(near, dtype=jnp.int32)[None, :] * (2 * capacity) + which * capacity + starts
    segments = jnp.concatenate([source.reshape(-1), (bases[:, None] + offsets).reshape(-1), counts.reshape(-1)])
    bases = jnp.concatenate([bases, ends[-1:]])
    own_past, own_rank = both[:, :, children : children + history], both[:, :, children + history :]
    past_slot = own_past * (2 * past_half) + jnp.arange(2, dtype=jnp.int32)[:, None, None] * past_half + own_rank

    lanes = rounded(history, 128)
    past = arrange_past(past_slot.reshape(-1), past_in, 2 * queries, history, lanes)
    scores = score_rows(segments, bases, rel, slabs, past, w_first, b_first, w_second, b_second, w_out, history, lanes)
    back = lax.ppermute(scores[queries:], "ah", swap)
    return jnp.where(inside_half[0], scores[:queries], back)


def solution(mesh):
    pb_n, an_n = mesh.shape["pb"], mesh.shape["an"]
    fine = Mesh(mesh.devices.reshape(pb_n, 2, an_n // 2), AXES)
    rows = P(AXES, None)
    return jax.shard_map(
        body, mesh=fine, in_specs=(rows, rows, rows, P(), P(), P(), P(), P()), out_specs=rows, check_vma=False
    )
```

time: 146 us -> 128 us (0.88)
  Pallas kernels: 0 us -> 54.5 us
  waiting for transfers between devices: 68.2 us -> 23.9 us
  local copies, waits for them, and re-layouts: 41 us -> 8.32 us
  starting transfers between devices: 3.65 us -> 29.9 us
  blocking collectives: 14.4 us -> 0 us
  matrix products: 15.8 us -> 2.68 us
  other arithmetic: 1.84 us -> 7.81 us
    all_to_all x1 -> x2, waiting for transfers between devices: 68.2 us -> 5.53 us  [the longest x1 5.53 us: body(): lax.all_to_all(wanted.reshape(peers, 1, stride), AXES, split_axis=0, conc...]
    pallas_call x0 -> x5, Pallas kernels: none -> 54.5 us  [the longest x1 27.1 us: score_rows(): pl.pallas_call(kernel, out_shape=jax.ShapeDtypeStruct((queries, children)...]
    gather x2 -> x0, local copies, waits for them, and re-layouts: 35 us -> none  [the longest x1 23.8 us: body(): node_table.at[asked.reshape(table_slots)].get(mode='promise_in_bounds')]
    ppermute x0 -> x17, starting transfers between devices: none -> 23.5 us  [the longest x15 18.4 us: body(): lax.ppermute(out, HALF, pairs[shift * near:(shift + 1) * near])]
    ppermute x0 -> x17, waiting for transfers between devices: none -> 18.3 us  [the longest x15 14.6 us: body(): lax.ppermute(out, HALF, pairs[shift * near:(shift + 1) * near])]
    all_to_all x1 -> x0, blocking collectives: 14.4 us -> none  [body(): lax.all_to_all(wanted, ('pb', 'an'), split_axis=0, concat_axis=0, tiled=T...]
    dot_general x3 -> x1, matrix products: 13.5 us -> 0.34 us  [body(): jnp.einsum('kj,qjx->qkx', lower, hits, preferred_element_type=jnp.float32)]
    all_to_all x1 -> x2, starting transfers between devices: 3.65 us -> 6.43 us  [the longest x1 3.82 us: body(): lax.all_to_all(wanted.reshape(peers, 1, stride), AXES, split_axis=0, conc...]
  transfers between devices with their start and end apart: 1 -> 19, of which waited for: 1 -> 5; matrix products, arithmetic and copies ran while one was open for 0% -> 9% of each run, Pallas kernels for 0% -> 17%
where the time goes in v2:
time: 128 us; the launch traced here: 127 us
  Pallas kernels  54.5 us (43%)
  starting transfers between devices  29.9 us (23%)
  waiting for transfers between devices  23.9 us (19%)
  local copies, waits for them, and re-layouts  8.32 us (6%)
  other arithmetic  7.81 us (6%)
  matrix products  2.68 us (2%)
    pallas_call x1, Pallas kernels, score_rows(): pl.pallas_call(kernel, out_shape=jax.ShapeDtypeStruct((queries, children)...  27.1 us
    pallas_call x3, Pallas kernels, gather_slabs(): pl.pallas_call(kernel, out_shape=shapes, in_specs=[SMEM, SMEM, VMEM], out...  22.7 us
    ppermute x15, starting transfers between devices, body(): lax.ppermute(out, HALF, pairs[shift * near:(shift + 1) * near])  18.4 us
    ppermute x15, waiting for transfers between devices, body(): lax.ppermute(out, HALF, pairs[shift * near:(shift + 1) * near])  14.6 us
    all_to_all x1, waiting for transfers between devices, body(): lax.all_to_all(wanted.reshape(peers, 1, stride), AXES, split_axis=0, conc...  5.53 us
    pallas_call x1, Pallas kernels, arrange_past(): pl.pallas_call(kernel, out_shape=jax.ShapeDtypeStruct((queries * lanes, w...  4.58 us
    ppermute x1, starting transfers between devices, body(): mate_ids = lax.ppermute(ids, 'ah', swap)  4.07 us
    all_to_all x1, starting transfers between devices, body(): lax.all_to_all(wanted.reshape(peers, 1, stride), AXES, split_axis=0, conc...  3.82 us
  transfers between devices with their start and end apart: 19, of which 5 were waited for; matrix products, arithmetic and copies ran while one was open for 9% of the time, Pallas kernels for 17%

profile of v2, /device:TPU:0, one launch (start us, length us, event | category | flops | bytes accessed | tf_op | source)
XLA Modules:
  0.0 127.5 jit_solution(5072211663459180614)
XLA Ops:
  0.0 0.8 reshape.484
  0.8 0.7 add_select_fusion.14
  2.0 0.8 fusion.68
  2.8 4.1 %collective-permute-start = (s32[16,394]{1,0:T(8,128)S(1)}, s32[16,394]{1,0:T(8,128)S(1)}, u32[]{:S(2)}, u32[]{:S(2)}) collective-permute-start(s32[16,394]{1,0:T(8,128)S(1)} %get-tuple-element.44), channel_id=1, source_target_pairs={{0,4},{4,0},{1,5},{5,1},{2,6},{6,2},{3,7},{7,3},{8,12},{12,8},{9,1... | collective-permute-start | bytes 75656 | tf_op jit(solution)/shard_map/ppermute | solution.py:316
  6.8 0.7 reshape.489
  7.6 0.8 select_convert_fusion.1
  8.3 0.5 fusion.11
  8.9 0.7 copy.17
  9.9 0.3 fusion.7
  10.3 1.4 %fusion = f32[64,320]{1,0:T(8,128)S(1)} fusion(s32[4096]{0:T(1024)S(1)} %convert_bitcast_fusion, bf16[4096,32]{0,1:T(8,128)(2,1)S(1)} %get-tuple-element.46, bf16[4096,32]{0,1:T(8,128)(2,1)S(1)} %get-tuple-element.45), kind=kOutput, calls=%fused_computation.1 | convolution fusion | flops 170131456 | bytes 622592 | tf_op jit(solution)/shard_map/io,is->os/dot_general | solution.py:42
  11.8 0.7 copy.16
  12.5 3.8 %all-to-all-start = ((s32[32,1,384]{2,1,0:T(1,128)}), s32[32,1,384]{2,1,0:T(1,128)S(1)}, u32[]{:S(2)}, u32[]{:S(2)}) async-start(s32[32,1,384]{2,1,0:T(1,128)} %copy.16), calls=%async_computation | async-start | bytes 98304 | tf_op jit(solution)/shard_map/all_to_all | solution.py:288
  16.6 0.6 mul.125.order_ref
  18.0 5.5 %all-to-all-done = s32[32,1,384]{2,1,0:T(1,128)S(1)} async-done(((s32[32,1,384]{2,1,0:T(1,128)}), s32[32,1,384]{2,1,0:T(1,128)S(1)}, u32[]{:S(2)}, u32[]{:S(2)}) %all-to-all-start) | async-done | bytes 49184 | tf_op jit(solution)/shard_map/all_to_all | solution.py:288
  23.5 0.6 copy-done.1
  24.1 6.2 %gather_past.1 = (bf16[2304,128]{1,0:T(8,128)(2,1)}, bf16[640,128]{1,0:T(8,128)(2,1)}, bf16[640,128]{1,0:T(8,128)(2,1)}) custom-call(s32[32]{0:T(128)} %mul.125.order_ref, s32[12288]{0:T(1024)} %bitcast.60, bf16[8192,128]{1,0:T(8,128)(2,1)} %table_ref.5), custom_call_target="tpu_custom_call" | custom-call | tf_op jit(solution)/shard_map/gather_past/pallas_call | solution.py:109
  30.4 2.6 %all-to-all-start.1 = ((bf16[32,72,128]{2,1,0:T(8,128)(2,1)}), bf16[32,72,128]{2,1,0:T(8,128)(2,1)S(1)}, u32[]{:S(2)}, u32[]{:S(2)}) async-start(bf16[32,72,128]{2,1,0:T(8,128)(2,1)} %bitcast.63), calls=%async_computation.1 | async-start | bytes 1179648 | tf_op jit(solution)/shard_map/all_to_all | solution.py:308
  33.0 0.5 slice.56
  34.0 0.3 fusion.6
  34.3 0.7 convert_add_fusion.rel_ref
  35.0 9.1 %gather_slabs.2 = (bf16[640,128]{1,0:T(8,128)(2,1)}, bf16[640,128]{1,0:T(8,128)(2,1)}, bf16[640,128]{1,0:T(8,128)(2,1)}, bf16[640,128]{1,0:T(8,128)(2,1)}, bf16[...) custom-call(s32[32]{0:T(128)} %mul.125.order_ref, ...), custom_call_target="tpu_custom_call" | custom-call | tf_op jit(solution)/shard_map/gather_slabs/pallas_call | solution.py:109
  44.1 1.7 %collective-permute-start.1 = (bf16[640,128]{1,0:T(8,128)(2,1)}, bf16[640,128]{1,0:T(8,128)(2,1)S(1)}, u32[]{:S(2)}, u32[]{:S(2)}) collective-permute-start(bf16[640,128]{1,0:T(8,128)(2,1)} %get-tuple-element.24), channel_id=1, source_target_pairs={{0,1},{1,0},{2,3},{3,2},{8,9},{9,8},{10,11},{11,10},{16,17},{17,16... | collective-permute-start | bytes 491528 | tf_op jit(solution)/shard_map/ppermute | solution.py:312
  45.8 1.5 %collective-permute-start.2 = (bf16[640,128]{1,0:T(8,128)(2,1)}, bf16[640,128]{1,0:T(8,128)(2,1)S(1)}, u32[]{:S(2)}, u32[]{:S(2)}) collective-permute-start(bf16[640,128]{1,0:T(8,128)(2,1)} %get-tuple-element.25), channel_id=1, source_target_pairs={{0,2},{1,3},{2,0},{3,1},{8,10},{9,11},{10,8},{11,9},{16,18},{17,19... | collective-permute-start | bytes 491528 | tf_op jit(solution)/shard_map/ppermute | solution.py:312
  47.3 0.3 collective-permute-start.3
  47.6 1.7 %collective-permute-start.5 = (bf16[640,128]{1,0:T(8,128)(2,1)}, bf16[640,128]{1,0:T(8,128)(2,1)S(1)}, u32[]{:S(2)}, u32[]{:S(2)}) collective-permute-start(bf16[640,128]{1,0:T(8,128)(2,1)} %get-tuple-element.28), channel_id=1, source_target_pairs={{0,9},{1,8},{2,11},{3,10},{8,1},{9,0},{10,3},{11,2},{16,25},{17,24... | collective-permute-start | bytes 491528 | tf_op jit(solution)/shard_map/ppermute | solution.py:312
  49.5 7.4 %gather_slabs.3 = (bf16[640,128]{1,0:T(8,128)(2,1)}, bf16[640,128]{1,0:T(8,128)(2,1)}, bf16[640,128]{1,0:T(8,128)(2,1)}, bf16[640,128]{1,0:T(8,128)(2,1)}, bf16[...) custom-call(s32[32]{0:T(128)} %mul.125.order_ref, s32[12288]{0:T(1024)} %bitcast.62, bf16[8192,128]{1,0:T(8,128)(2,1)} %table_ref.5), custom_call_target="tpu_custom_call" | custom-call | tf_op jit(solution)/shard_map/gather_slabs/pallas_call | solution.py:109
  56.9 1.2 collective-permute-start.6
  58.1 1.6 %collective-permute-start.8 = (bf16[640,128]{1,0:T(8,128)(2,1)S(1)}, bf16[640,128]{1,0:T(8,128)(2,1)S(1)}, u32[]{:S(2)}, u32[]{:S(2)}) collective-permute-start(bf16[640,128]{1,0:T(8,128)(2,1)S(1)} %copy-done.20), channel_id=1, source_target_pairs={{0,16},{1,17},{2,18},{3,19},{8,24},{9,25},{10,26},{11,27},{16,0},{... | collective-permute-start | bytes 491528 | tf_op jit(solution)/shard_map/ppermute | solution.py:312
  59.7 0.5 collective-permute-start.10
  60.2 2.4 %collective-permute-start.11 = (bf16[640,128]{1,0:T(8,128)(2,1)}, bf16[640,128]{1,0:T(8,128)(2,1)S(1)}, u32[]{:S(2)}, u32[]{:S(2)}) collective-permute-start(bf16[640,128]{1,0:T(8,128)(2,1)} %get-tuple-element.34), channel_id=1, source_target_pairs={{0,19},{1,18},{2,17},{3,16},{8,27},{9,26},{10,25},{11,24},{16,3},{... | collective-permute-start | bytes 491528 | tf_op jit(solution)/shard_map/ppermute | solution.py:312
  62.6 0.7 collective-permute-done.6.rest_6_
  63.3 2.1 %collective-permute-start.13 = (bf16[640,128]{1,0:T(8,128)(2,1)}, bf16[640,128]{1,0:T(8,128)(2,1)S(1)}, u32[]{:S(2)}, u32[]{:S(2)}) collective-permute-start(bf16[640,128]{1,0:T(8,128)(2,1)} %get-tuple-element.36), channel_id=1, source_target_pairs={{0,25},{1,24},{2,27},{3,26},{8,17},{9,16},{10,19},{11,18},{16,9},{... | collective-permute-start | bytes 491528 | tf_op jit(solution)/shard_map/ppermute | solution.py:312
  65.4 10.3 %collective-permute-done.8.rest_8_ = bf16[640,128]{1,0:T(8,128)(2,1)S(1)} collective-permute-done((bf16[640,128]{1,0:T(8,128)(2,1)S(1)}, bf16[640,128]{1,0:T(8,128)(2,1)S(1)}, u32[]{:S(2)}, u32[]{:S(2)}) %collective-permute-start.8) | collective-permute-done | bytes 163872 | tf_op jit(solution)/shard_map/ppermute | solution.py:312
  75.7 1.7 %collective-permute-start.9 = (bf16[640,128]{1,0:T(8,128)(2,1)}, bf16[640,128]{1,0:T(8,128)(2,1)S(1)}, u32[]{:S(2)}, u32[]{:S(2)}) collective-permute-start(bf16[640,128]{1,0:T(8,128)(2,1)} %get-tuple-element.32), channel_id=1, source_target_pairs={{0,17},{1,16},{2,19},{3,18},{8,25},{9,24},{10,27},{11,26},{16,1},{... | collective-permute-start | bytes 491528 | tf_op jit(solution)/shard_map/ppermute | solution.py:312
  77.4 2.2 %collective-permute-start.14 = (bf16[640,128]{1,0:T(8,128)(2,1)S(1)}, bf16[640,128]{1,0:T(8,128)(2,1)S(1)}, u32[]{:S(2)}, u32[]{:S(2)}) collective-permute-start(bf16[640,128]{1,0:T(8,128)(2,1)S(1)} %copy-done.19), channel_id=1, source_target_pairs={{0,26},{1,27},{2,24},{3,25},{8,18},{9,19},{10,16},{11,17},{16,10},... | collective-permute-start | bytes 491528 | tf_op jit(solution)/shard_map/ppermute | solution.py:312
  79.5 1.5 %collective-permute-start.15 = (bf16[640,128]{1,0:T(8,128)(2,1)S(1)}, bf16[640,128]{1,0:T(8,128)(2,1)S(1)}, u32[]{:S(2)}, u32[]{:S(2)}) collective-permute-start(bf16[640,128]{1,0:T(8,128)(2,1)S(1)} %copy-done.18), channel_id=1, source_target_pairs={{0,27},{1,26},{2,25},{3,24},{8,19},{9,18},{10,17},{11,16},{16,11},... | collective-permute-start | bytes 491528 | tf_op jit(solution)/shard_map/ppermute | solution.py:312
  81.1 1.3 %pad_add_fusion.3.base_ref = s32[33]{0:T(128)} fusion(s32[1]{0:T(128)} %bitcast.10, s32[32]{0:T(128)S(1)} %get-tuple-element.40), kind=kLoop, calls=%fused_computation.175 | loop fusion | flops 33 | bytes 264 | tf_op jit(solution)/shard_map/concatenate | solution.py:339
  82.4 0.7 reshape.487.slot_ref
  83.1 0.6 pad_add_fusion.2.seg_ref
  83.7 0.8 copy-done
  84.5 4.6 %arrange_past.1.past_ref = bf16[4096,128]{1,0:T(8,128)(2,1)} custom-call(s32[2208]{0:T(1024)} %reshape.487.slot_ref, bf16[2304,128]{1,0:T(8,128)(2,1)} %bitcast.59), custom_call_target="tpu_custom_call" | custom-call | tf_op jit(solution)/shard_map/arrange_past/pallas_call | solution.py:140
  89.1 3.6 %collective-permute-done.9.rest_9_ = bf16[640,128]{1,0:T(8,128)(2,1)S(1)} collective-permute-done((bf16[640,128]{1,0:T(8,128)(2,1)}, bf16[640,128]{1,0:T(8,128)(2,1)S(1)}, u32[]{:S(2)}, u32[]{:S(2)}) %collective-permute-start.9) | collective-permute-done | bytes 163872 | tf_op jit(solution)/shard_map/ppermute | solution.py:312
  92.7 0.7 broadcast_in_dim.49.wo
  93.5 27.1 %score_rows.1 = f32[32,256]{1,0:T(8,128)} custom-call(s32[1536]{0:T(1024)} %pad_add_fusion.2.seg_ref, s32[33]{0:T(128)} %pad_add_fusion.3.base_ref, s32[32,256]{1,0:T(8,128)} %convert_add_fusion.rel_ref, bf16[4096,128]{1,0:T(8,128)(2,1)} %arrange_past.1.past_ref, bf16[256,512]{1,0:T(8,128)(2,1)} %w1.1, f32[1,512]{1,0:T(1,128)} %bitcast.72, ...), custom_call_target="tpu_custom_call" | custom-call | tf_op jit(solution)/shard_map/score_rows/pallas_call | solution.py:232
  120.7 0.7 slice.64
  121.4 0.9 collective-permute-start.16
  122.4 3.8 %collective-permute-done.16 = f32[16,256]{1,0:T(8,128)S(1)} collective-permute-done((f32[16,256]{1,0:T(8,128)S(1)}, f32[16,256]{1,0:T(8,128)S(1)}, u32[]{:S(2)}, u32[]{:S(2)}) %collective-permute-start.16) | collective-permute-done | bytes 16416 | tf_op jit(solution)/shard_map/ppermute | solution.py:346
  126.1 1.3 %slice_select_fusion = f32[16,256]{1,0:T(8,128)} fusion(f32[16,256]{1,0:T(8,128)S(1)} %collective-permute-done.16, f32[32,256]{1,0:T(8,128)} %score_rows.1, pred[2,16,256]{2,1,0:T(8,128)(4,1)S(1)} %get-tuple-element.42), kind=kLoop, calls=%fused_computation.105 | loop fusion | flops 4096 | bytes 53248 | tf_op jit(solution)/shard_map/jit(_where)/select_n | solution.py:347
  (103 shorter events, 2.7 us)
Async XLA Ops:
  2.8 14.4 %collective-permute-start = (s32[16,394]{1,0:T(8,128)S(1)}, s32[16,394]{1,0:T(8,128)S(1)}, u32[]{:S(2)}, u32[]{:S(2)}) collective-permute-start(s32[16,394]{1,0:T(8,128)S(1)} %get-tuple-element.44), channel_id=1, source_target_pairs={{0,4},{4,0},{1,5},{5,1},{2,6},{6,2},{3,7},{7,3},{8,12},{12,8},{9,1... | collective-permute-start | bytes 75656 | tf_op jit(solution)/shard_map/ppermute | solution.py:316
  12.5 11.1 %all-to-all-start = ((s32[32,1,384]{2,1,0:T(1,128)}), s32[32,1,384]{2,1,0:T(1,128)S(1)}, u32[]{:S(2)}, u32[]{:S(2)}) async-start(s32[32,1,384]{2,1,0:T(1,128)} %copy.16), calls=%async_computation | async-start | bytes 98304 | tf_op jit(solution)/shard_map/all_to_all | solution.py:288
  23.5 0.6 copy-start.1
  30.4 53.3 %all-to-all-start.1 = ((bf16[32,72,128]{2,1,0:T(8,128)(2,1)}), bf16[32,72,128]{2,1,0:T(8,128)(2,1)S(1)}, u32[]{:S(2)}, u32[]{:S(2)}) async-start(bf16[32,72,128]{2,1,0:T(8,128)(2,1)} %bitcast.63), calls=%async_computation.1 | async-start | bytes 1179648 | tf_op jit(solution)/shard_map/all_to_all | solution.py:308
  35.0 42.4 %copy-start.19 = (bf16[640,128]{1,0:T(8,128)(2,1)S(1)}, bf16[640,128]{1,0:T(8,128)(2,1)}, u32[]{:S(2)}) copy-start(bf16[640,128]{1,0:T(8,128)(2,1)} %get-tuple-element.37) | copy-start | bytes 491524
  35.0 44.5 %copy-start.18 = (bf16[640,128]{1,0:T(8,128)(2,1)S(1)}, bf16[640,128]{1,0:T(8,128)(2,1)}, u32[]{:S(2)}) copy-start(bf16[640,128]{1,0:T(8,128)(2,1)} %get-tuple-element.38) | copy-start | bytes 491524
  44.1 12.8 %copy-start.21 = (bf16[640,128]{1,0:T(8,128)(2,1)S(1)}, bf16[640,128]{1,0:T(8,128)(2,1)}, u32[]{:S(2)}) copy-start(bf16[640,128]{1,0:T(8,128)(2,1)} %get-tuple-element.29) | copy-start | bytes 491524
  44.1 14.1 %copy-start.20 = (bf16[640,128]{1,0:T(8,128)(2,1)S(1)}, bf16[640,128]{1,0:T(8,128)(2,1)}, u32[]{:S(2)}) copy-start(bf16[640,128]{1,0:T(8,128)(2,1)} %get-tuple-element.31) | copy-start | bytes 491524
  44.1 48.7 %copy-start.17 = (bf16[512]{0:T(512)(128)(2,1)S(1)}, bf16[512]{0:T(512)(128)(2,1)}, u32[]{:S(2)}) copy-start(bf16[512]{0:T(512)(128)(2,1)} %param.15) | copy-start | bytes 3076
  44.1 12.8 %collective-permute-start.1 = (bf16[640,128]{1,0:T(8,128)(2,1)}, bf16[640,128]{1,0:T(8,128)(2,1)S(1)}, u32[]{:S(2)}, u32[]{:S(2)}) collective-permute-start(bf16[640,128]{1,0:T(8,128)(2,1)} %get-tuple-element.24), channel_id=1, source_target_pairs={{0,1},{1,0},{2,3},{3,2},{8,9},{9,8},{10,11},{11,10},{16,17},{17,16... | collective-permute-start | bytes 491528 | tf_op jit(solution)/shard_map/ppermute | solution.py:312
  45.8 12.3 %collective-permute-start.2 = (bf16[640,128]{1,0:T(8,128)(2,1)}, bf16[640,128]{1,0:T(8,128)(2,1)S(1)}, u32[]{:S(2)}, u32[]{:S(2)}) collective-permute-start(bf16[640,128]{1,0:T(8,128)(2,1)} %get-tuple-element.25), channel_id=1, source_target_pairs={{0,2},{1,3},{2,0},{3,1},{8,10},{9,11},{10,8},{11,9},{16,18},{17,19... | collective-permute-start | bytes 491528 | tf_op jit(solution)/shard_map/ppermute | solution.py:312
  47.3 12.4 %collective-permute-start.3 = (bf16[640,128]{1,0:T(8,128)(2,1)}, bf16[640,128]{1,0:T(8,128)(2,1)S(1)}, u32[]{:S(2)}, u32[]{:S(2)}) collective-permute-start(bf16[640,128]{1,0:T(8,128)(2,1)} %get-tuple-element.26), channel_id=1, source_target_pairs={{0,3},{1,2},{2,1},{3,0},{8,11},{9,10},{10,9},{11,8},{16,19},{17,18... | collective-permute-start | bytes 491528 | tf_op jit(solution)/shard_map/ppermute | solution.py:312
  47.6 12.5 %collective-permute-start.4 = (bf16[640,128]{1,0:T(8,128)(2,1)}, bf16[640,128]{1,0:T(8,128)(2,1)S(1)}, u32[]{:S(2)}, u32[]{:S(2)}) collective-permute-start(bf16[640,128]{1,0:T(8,128)(2,1)} %get-tuple-element.27), channel_id=1, source_target_pairs={{0,8},{1,9},{2,10},{3,11},{8,0},{9,1},{10,2},{11,3},{16,24},{17,25... | collective-permute-start | bytes 491528 | tf_op jit(solution)/shard_map/ppermute | solution.py:312
  47.6 15.0 %collective-permute-start.5 = (bf16[640,128]{1,0:T(8,128)(2,1)}, bf16[640,128]{1,0:T(8,128)(2,1)S(1)}, u32[]{:S(2)}, u32[]{:S(2)}) collective-permute-start(bf16[640,128]{1,0:T(8,128)(2,1)} %get-tuple-element.28), channel_id=1, source_target_pairs={{0,9},{1,8},{2,11},{3,10},{8,1},{9,0},{10,3},{11,2},{16,25},{17,24... | collective-permute-start | bytes 491528 | tf_op jit(solution)/shard_map/ppermute | solution.py:312
  56.9 36.5 %copy-start.2 = (bf16[640,128]{1,0:T(8,128)(2,1)}, bf16[640,128]{1,0:T(8,128)(2,1)S(1)}, u32[]{:S(2)}) copy-start(bf16[640,128]{1,0:T(8,128)(2,1)S(1)} %collective-permute-done.1.rest_1_) | copy-start | bytes 491524
  56.9 6.4 %collective-permute-start.6 = (bf16[640,128]{1,0:T(8,128)(2,1)S(1)}, bf16[640,128]{1,0:T(8,128)(2,1)S(1)}, u32[]{:S(2)}, u32[]{:S(2)}) collective-permute-start(bf16[640,128]{1,0:T(8,128)(2,1)S(1)} %copy-done.21), channel_id=1, source_target_pairs={{0,10},{1,11},{2,8},{3,9},{8,2},{9,3},{10,0},{11,1},{16,26},{17,27... | collective-permute-start | bytes 491528 | tf_op jit(solution)/shard_map/ppermute | solution.py:312
  58.1 35.3 %copy-start.3 = (bf16[640,128]{1,0:T(8,128)(2,1)}, bf16[640,128]{1,0:T(8,128)(2,1)S(1)}, u32[]{:S(2)}) copy-start(bf16[640,128]{1,0:T(8,128)(2,1)S(1)} %collective-permute-done.2.rest_2_) | copy-start | bytes 491524
  58.1 17.5 %collective-permute-start.8 = (bf16[640,128]{1,0:T(8,128)(2,1)S(1)}, bf16[640,128]{1,0:T(8,128)(2,1)S(1)}, u32[]{:S(2)}, u32[]{:S(2)}) collective-permute-start(bf16[640,128]{1,0:T(8,128)(2,1)S(1)} %copy-done.20), channel_id=1, source_target_pairs={{0,16},{1,17},{2,18},{3,19},{8,24},{9,25},{10,26},{11,27},{16,0},{... | collective-permute-start | bytes 491528 | tf_op jit(solution)/shard_map/ppermute | solution.py:312
  59.7 33.7 %copy-start.4 = (bf16[640,128]{1,0:T(8,128)(2,1)}, bf16[640,128]{1,0:T(8,128)(2,1)S(1)}, u32[]{:S(2)}) copy-start(bf16[640,128]{1,0:T(8,128)(2,1)S(1)} %collective-permute-done.3.rest_3_) | copy-start | bytes 491524
  59.7 15.9 %collective-permute-start.10 = (bf16[640,128]{1,0:T(8,128)(2,1)}, bf16[640,128]{1,0:T(8,128)(2,1)S(1)}, u32[]{:S(2)}, u32[]{:S(2)}) collective-permute-start(bf16[640,128]{1,0:T(8,128)(2,1)} %get-tuple-element.33), channel_id=1, source_target_pairs={{0,18},{1,19},{2,16},{3,17},{8,26},{9,27},{10,24},{11,25},{16,2},{... | collective-permute-start | bytes 491528 | tf_op jit(solution)/shard_map/ppermute | solution.py:312
  60.2 33.3 %copy-start.5 = (bf16[640,128]{1,0:T(8,128)(2,1)}, bf16[640,128]{1,0:T(8,128)(2,1)S(1)}, u32[]{:S(2)}) copy-start(bf16[640,128]{1,0:T(8,128)(2,1)S(1)} %collective-permute-done.4.rest_4_) | copy-start | bytes 491524
  60.2 17.2 %collective-permute-start.11 = (bf16[640,128]{1,0:T(8,128)(2,1)}, bf16[640,128]{1,0:T(8,128)(2,1)S(1)}, u32[]{:S(2)}, u32[]{:S(2)}) collective-permute-start(bf16[640,128]{1,0:T(8,128)(2,1)} %get-tuple-element.34), channel_id=1, source_target_pairs={{0,19},{1,18},{2,17},{3,16},{8,27},{9,26},{10,25},{11,24},{16,3},{... | collective-permute-start | bytes 491528 | tf_op jit(solution)/shard_map/ppermute | solution.py:312
  62.6 30.8 %copy-start.6 = (bf16[640,128]{1,0:T(8,128)(2,1)}, bf16[640,128]{1,0:T(8,128)(2,1)S(1)}, u32[]{:S(2)}) copy-start(bf16[640,128]{1,0:T(8,128)(2,1)S(1)} %collective-permute-done.5.rest_5_) | copy-start | bytes 491524
  62.6 16.9 %collective-permute-start.12 = (bf16[640,128]{1,0:T(8,128)(2,1)}, bf16[640,128]{1,0:T(8,128)(2,1)S(1)}, u32[]{:S(2)}, u32[]{:S(2)}) collective-permute-start(bf16[640,128]{1,0:T(8,128)(2,1)} %get-tuple-element.35), channel_id=1, source_target_pairs={{0,24},{1,25},{2,26},{3,27},{8,16},{9,17},{10,18},{11,19},{16,8},{... | collective-permute-start | bytes 491528 | tf_op jit(solution)/shard_map/ppermute | solution.py:312
  63.3 30.1 %copy-start.7 = (bf16[640,128]{1,0:T(8,128)(2,1)}, bf16[640,128]{1,0:T(8,128)(2,1)S(1)}, u32[]{:S(2)}) copy-start(bf16[640,128]{1,0:T(8,128)(2,1)S(1)} %collective-permute-done.6.rest_6_) | copy-start | bytes 491524
  63.3 25.8 %collective-permute-start.13 = (bf16[640,128]{1,0:T(8,128)(2,1)}, bf16[640,128]{1,0:T(8,128)(2,1)S(1)}, u32[]{:S(2)}, u32[]{:S(2)}) collective-permute-start(bf16[640,128]{1,0:T(8,128)(2,1)} %get-tuple-element.36), channel_id=1, source_target_pairs={{0,25},{1,24},{2,27},{3,26},{8,17},{9,16},{10,19},{11,18},{16,9},{... | collective-permute-start | bytes 491528 | tf_op jit(solution)/shard_map/ppermute | solution.py:312
  75.6 17.8 %copy-start.8 = (bf16[640,128]{1,0:T(8,128)(2,1)}, bf16[640,128]{1,0:T(8,128)(2,1)S(1)}, u32[]{:S(2)}) copy-start(bf16[640,128]{1,0:T(8,128)(2,1)S(1)} %collective-permute-done.8.rest_8_) | copy-start | bytes 491524
  75.6 13.5 %collective-permute-start.7 = (bf16[640,128]{1,0:T(8,128)(2,1)}, bf16[640,128]{1,0:T(8,128)(2,1)S(1)}, u32[]{:S(2)}, u32[]{:S(2)}) collective-permute-start(bf16[640,128]{1,0:T(8,128)(2,1)} %get-tuple-element.30), channel_id=1, source_target_pairs={{0,11},{1,10},{2,9},{3,8},{8,3},{9,2},{10,1},{11,0},{16,27},{17,26... | collective-permute-start | bytes 491528 | tf_op jit(solution)/shard_map/ppermute | solution.py:312
  75.6 17.8 %copy-start.9 = (bf16[640,128]{1,0:T(8,128)(2,1)}, bf16[640,128]{1,0:T(8,128)(2,1)S(1)}, u32[]{:S(2)}) copy-start(bf16[640,128]{1,0:T(8,128)(2,1)S(1)} %collective-permute-done.10.rest_10_) | copy-start | bytes 491524
  75.7 17.1 %collective-permute-start.9 = (bf16[640,128]{1,0:T(8,128)(2,1)}, bf16[640,128]{1,0:T(8,128)(2,1)S(1)}, u32[]{:S(2)}, u32[]{:S(2)}) collective-permute-start(bf16[640,128]{1,0:T(8,128)(2,1)} %get-tuple-element.32), channel_id=1, source_target_pairs={{0,17},{1,16},{2,19},{3,18},{8,25},{9,24},{10,27},{11,26},{16,1},{... | collective-permute-start | bytes 491528 | tf_op jit(solution)/shard_map/ppermute | solution.py:312
  77.4 16.1 %copy-start.10 = (bf16[640,128]{1,0:T(8,128)(2,1)}, bf16[640,128]{1,0:T(8,128)(2,1)S(1)}, u32[]{:S(2)}) copy-start(bf16[640,128]{1,0:T(8,128)(2,1)S(1)} %collective-permute-done.11.rest_11_) | copy-start | bytes 491524
  77.4 15.3 %collective-permute-start.14 = (bf16[640,128]{1,0:T(8,128)(2,1)S(1)}, bf16[640,128]{1,0:T(8,128)(2,1)S(1)}, u32[]{:S(2)}, u32[]{:S(2)}) collective-permute-start(bf16[640,128]{1,0:T(8,128)(2,1)S(1)} %copy-done.19), channel_id=1, source_target_pairs={{0,26},{1,27},{2,24},{3,25},{8,18},{9,19},{10,16},{11,17},{16,10},... | collective-permute-start | bytes 491528 | tf_op jit(solution)/shard_map/ppermute | solution.py:312
  79.5 13.9 %copy-start.11 = (bf16[640,128]{1,0:T(8,128)(2,1)}, bf16[640,128]{1,0:T(8,128)(2,1)S(1)}, u32[]{:S(2)}) copy-start(bf16[640,128]{1,0:T(8,128)(2,1)S(1)} %collective-permute-done.12.rest_12_) | copy-start | bytes 491524
  79.5 13.2 %collective-permute-start.15 = (bf16[640,128]{1,0:T(8,128)(2,1)S(1)}, bf16[640,128]{1,0:T(8,128)(2,1)S(1)}, u32[]{:S(2)}, u32[]{:S(2)}) collective-permute-start(bf16[640,128]{1,0:T(8,128)(2,1)S(1)} %copy-done.18), channel_id=1, source_target_pairs={{0,27},{1,26},{2,25},{3,24},{8,19},{9,18},{10,17},{11,16},{16,11},... | collective-permute-start | bytes 491528 | tf_op jit(solution)/shard_map/ppermute | solution.py:312
  83.7 0.8 copy-start
  89.1 4.4 %copy-start.12 = (bf16[640,128]{1,0:T(8,128)(2,1)}, bf16[640,128]{1,0:T(8,128)(2,1)S(1)}, u32[]{:S(2)}) copy-start(bf16[640,128]{1,0:T(8,128)(2,1)S(1)} %collective-permute-done.13.rest_13_) | copy-start | bytes 491524
  89.1 4.4 %copy-start.13 = (bf16[640,128]{1,0:T(8,128)(2,1)}, bf16[640,128]{1,0:T(8,128)(2,1)S(1)}, u32[]{:S(2)}) copy-start(bf16[640,128]{1,0:T(8,128)(2,1)S(1)} %collective-permute-done.7.rest_7_) | copy-start | bytes 491524
  92.7 0.8 copy-start.14
  92.7 0.8 copy-start.15
  92.7 0.8 copy-start.16
  121.4 4.7 %collective-permute-start.16 = (f32[16,256]{1,0:T(8,128)S(1)}, f32[16,256]{1,0:T(8,128)S(1)}, u32[]{:S(2)}, u32[]{:S(2)}) collective-permute-start(f32[16,256]{1,0:T(8,128)S(1)} %slice.64), channel_id=1, source_target_pairs={{0,4},{4,0},{1,5},{5,1},{2,6},{6,2},{3,7},{7,3},{8,12},{12,8},{9,1... | collective-permute-start | bytes 49160 | tf_op jit(solution)/shard_map/ppermute | solution.py:346

commit v3 on v2

--- a/solution.py
+++ b/solution.py
@@ -101,10 +101,10 @@
             lax.fori_loop(0, 2 * per, child, 0)
             narrow(spare, out, slab)
 
-    shapes = [jax.ShapeDtypeStruct((slab, width), table.dtype)] * len(shifts)
+    shapes = [jax.ShapeDtypeStruct((slab, width), jnp.bfloat16)] * len(shifts)
     spare_rows = slab
     if past_half:
-        shapes = [jax.ShapeDtypeStruct((peers * 2 * past_half, width), table.dtype)] + shapes
+        shapes = [jax.ShapeDtypeStruct((peers * 2 * past_half, width), jnp.bfloat16)] + shapes
         spare_rows = max(slab, peers * 2 * past_half)
     return pl.pallas_call(
         kernel,
@@ -152,39 +152,49 @@
     slab, width = slabs[0].shape
     parts = len(slabs)
     hidden = w_second.shape[0]
-    longest = queries * children // 2 + children
+    total = queries * parts
+    batch = 8
     longest = rounded(queries * children + queries * 8, BLOCK)
     per_block = BLOCK // 128
     quick = 3
     group = 4
+    half = queries // 2
 
     def kernel(seg_ref, base_ref, rel_ref, past_ref, w1, b1, w2, b2, wo, *rest):
-        slab_refs, out_ref = rest[:parts], rest[parts]
-        wide, rows, pool, line, g0, g1, g2 = rest[parts + 1 :]
+        slab_refs, out_refs = rest[:parts], rest[parts : parts + 2]
+        wide, rows, pool, line, g0, g1, g2 = rest[parts + 2 :]
         for i, ref in enumerate(slab_refs):
             widen(ref, wide, slab, at=i * slab)
         spots = lax.broadcasted_iota(jnp.int32, (8, width), 0)
 
-        def segment(t, c):
-            src = seg_ref[t]
-            dst = seg_ref[queries * parts + t]
-            count = seg_ref[2 * queries * parts + t]
-            chunks = [wide[pl.ds(src + 8 * i, 8), :] for i in range(quick)]
-            for i, chunk in enumerate(chunks):
-                pltpu.store(rows.at[pl.ds(dst + 8 * i, 8), :], chunk, mask=spots < count - 8 * i)
-
-            def more(i, c):
-                pltpu.store(
-                    rows.at[pl.ds(dst + 8 * i, 8), :],
-                    wide[pl.ds(src + 8 * i, 8), :],
-                    mask=spots < count - 8 * i,
-                )
-                return c
-
-            lax.fori_loop(quick, (count + 7) // 8, more, 0)
+        def segment(g, c):
+            at = [g * batch + i for i in range(batch)]
+            src = [seg_ref[t] for t in at]
+            dst = [seg_ref[total + t] for t in at]
+            count = [seg_ref[2 * total + t] for t in at]
+            chunks = [[wide[pl.ds(s + 8 * i, 8), :] for i in range(quick)] for s in src]
+            for d, n, chunk in zip(dst, count, chunks):
+                for i, part in enumerate(chunk):
+                    pltpu.store(rows.at[pl.ds(d + 8 * i, 8), :], part, mask=spots < n - 8 * i)
+            most = count[0]
+            for n in count[1:]:
+                most = jnp.maximum(most, n)
+
+            @pl.when(most > 8 * quick)
+            def _():
+                for s, d, n in zip(src, dst, count):
+
+                    def more(i, c, s=s, d=d, n=n):
+                        pltpu.store(
+                            rows.at[pl.ds(d + 8 * i, 8), :], wide[pl.ds(s + 8 * i, 8), :], mask=spots < n - 8 * i
+                        )
+                        return c
+
+                    lax.fori_loop(quick, (n + 7) // 8, more, 0)
+
             return c
 
-        lax.fori_loop(0, queries * parts, segment, 0)
+        lax.fori_loop(0, total // batch, segment, 0)
 
         def attend(g, c):
             for i in range(group):
@@ -224,16 +234,17 @@
                 spot = rel_ref[q : q + 8, k : k + 128]
                 lane = spot & 127
                 took = [jnp.take_along_axis(ref[q : q + 8, :], lane, axis=1) for ref in (g0, g1, g2)]
-                out_ref[q : q + 8, k : k + 128] = jnp.where(
+                out_ref, at = out_refs[q // half], q % half
+                out_ref[at : at + 8, k : k + 128] = jnp.where(
                     spot < 128, took[0], jnp.where(spot < 256, took[1], took[2])
                 )
 
     wide_rows = parts * slab + 8 * quick
     return pl.pallas_call(
         kernel,
-        out_shape=jax.ShapeDtypeStruct((queries, children), jnp.float32),
+        out_shape=[jax.ShapeDtypeStruct((half, children), jnp.float32)] * 2,
         in_specs=[SMEM, SMEM] + [VMEM] * (7 + parts),
-        out_specs=VMEM,
+        out_specs=[VMEM] * 2,
         scratch_shapes=[
             pltpu.VMEM((wide_rows, width), jnp.float32),
             pltpu.VMEM((longest + children, width), jnp.float32),
@@ -251,7 +262,7 @@
         b_first.reshape(1, hidden),
         w_second,
         b_second.reshape(1, hidden),
-        jnp.broadcast_to(w_out[None, :], (8, hidden)),
+        w_out,
         *slabs,
     )
 
@@ -288,32 +299,35 @@
     asked = lax.all_to_all(wanted.reshape(peers, 1, stride), AXES, split_axis=0, concat_axis=0, tiled=True)
     asked = asked.reshape(peers * stride)
 
+    ids = jnp.concatenate([child_ids, past_owner.reshape(queries, history), past_rank.reshape(queries, history)], axis=1)
+    swap = [(0, 1), (1, 0)]
+    mate_ids = lax.ppermute(ids, "ah", swap)
     shifts = jnp.arange(near, dtype=jnp.int32)
     target = (here ^ shifts) if power else (here + shifts) % near
     lists = (target // al_n) * (2 * al_n) + target % al_n
     order = jnp.stack([lists + ah * al_n, lists + (1 - ah) * al_n], axis=1).reshape(2 * near) * stride
 
     pairs = [(i, (i ^ s) if power else (i + s) % near) for s in range(near) for i in range(near)]
-    steps = sorted(range(near), key=lambda s: (s == 0, -bin(s).count("1"), -s))
-    first_cut = max(1, near // 8)
-    second_cut = near // 2
-    waves = [steps[:first_cut], steps[first_cut:second_cut], steps[second_cut:]]
+    steps = sorted(range(1, near), key=lambda s: (-bin(s).count("1"), -s))
+    cuts = [0, 3 * near // 16, near // 2, near - 1]
+    waves = [steps[a:b] for a, b in zip(cuts, cuts[1:])] + [[0]]
     slabs = [None] * near
     for number, wave in enumerate(waves):
         outs = gather_slabs(
-            asked, order, node_table, wave, capacity, stride, past_half if number == 0 else 0, peers, al_n
+            asked, order, node_table, wave, capacity, stride, past_half if number == 1 else 0, peers, al_n
         )
-        if number == 0:
+        if number == 1:
             past_out, outs = outs[0], outs[1:]
             past_in = lax.all_to_all(
                 past_out.reshape(peers, 2 * past_half, width), AXES, split_axis=0, concat_axis=0, tiled=True
             ).reshape(peers * 2 * past_half, width)
+        if number == len(waves) - 1:
+            slabs[0] = outs[0]
+            break
         for shift, out in zip(wave, outs):
-            slabs[shift] = lax.ppermute(out, HALF, pairs[shift * near : (shift + 1) * near]) if shift else out
-
-    ids = jnp.concatenate([child_ids, past_owner.reshape(queries, history), past_rank.reshape(queries, history)], axis=1)
-    swap = [(0, 1), (1, 0)]
-    mate_ids = lax.ppermute(ids, "ah", swap)
+            slabs[shift] = lax.ppermute(out, HALF, pairs[shift * near : (shift + 1) * near])
+
+    ids, mate_ids, _ = lax.optimization_barrier((ids, mate_ids, slabs[0]))
     both = jnp.stack([ids, mate_ids])
     kids = both[:, :, :children]
     owner = kids // shard_rows
@@ -340,11 +354,14 @@
     own_past, own_rank = both[:, :, children : children + history], both[:, :, children + history :]
     past_slot = own_past * (2 * past_half) + jnp.arange(2, dtype=jnp.int32)[:, None, None] * past_half + own_rank
 
+    w_last = jnp.broadcast_to(w_out[None, :], (8, w_out.shape[0]))
+    mine = inside_half[0].astype(jnp.int32)
+
     lanes = rounded(history, 128)
     past = arrange_past(past_slot.reshape(-1), past_in, 2 * queries, history, lanes)
-    scores = score_rows(segments, bases, rel, slabs, past, w_first, b_first, w_second, b_second, w_out, history, lanes)
-    back = lax.ppermute(scores[queries:], "ah", swap)
-    return jnp.where(inside_half[0], scores[:queries], back)
+    own, lent = score_rows(segments, bases, rel, slabs, past, w_first, b_first, w_second, b_second, w_last, history, lanes)
+    back = lax.ppermute(lent, "ah", swap)
+    return jnp.where(mine > 0, own, back)
 
 
 def solution(mesh):

time: 128 us -> 120 us (0.938)
  Pallas kernels: 54.5 us -> 50 us
  waiting for transfers between devices: 23.9 us -> 20.1 us
  starting transfers between devices: 29.9 us -> 32 us
  other arithmetic: 7.81 us -> 6.42 us
    pallas_call x1, Pallas kernels: 27.1 us -> 19.9 us  [score_rows(): pl.pallas_call(kernel, out_shape=[jax.ShapeDtypeStruct((half, children),...]
    all_to_all x1, starting transfers between devices: 3.82 us -> 7.32 us  [body(): lax.all_to_all(wanted.reshape(peers, 1, stride), AXES, split_axis=0, conc...]
    ppermute x15, waiting for transfers between devices: 14.6 us -> 11.5 us  [body(): lax.ppermute(out, HALF, pairs[shift * near:(shift + 1) * near])]
    pallas_call x3 -> x4, Pallas kernels: 22.7 us -> 25.6 us  [gather_slabs(): pl.pallas_call(kernel, out_shape=shapes, in_specs=[SMEM, SMEM, VMEM], out...]
    all_to_all x1, waiting for transfers between devices: 5.53 us -> 3.63 us  [body(): lax.all_to_all(wanted.reshape(peers, 1, stride), AXES, split_axis=0, conc...]
    ppermute x1, starting transfers between devices: 4.07 us -> 2.68 us  [body(): mate_ids = lax.ppermute(ids, 'ah', swap)]
  transfers between devices with their start and end apart: 19 -> 19, of which waited for: 5 -> 9; matrix products, arithmetic and copies ran while one was open for 9% -> 5% of each run, Pallas kernels for 17% -> 25%
where the time goes in v3:
time: 120 us; the launch traced here: 119 us
  Pallas kernels  50 us (42%)
  starting transfers between devices  32 us (27%)
  waiting for transfers between devices  20.1 us (17%)
  local copies, waits for them, and re-layouts  7.65 us (6%)
  other arithmetic  6.42 us (5%)
  matrix products  2.67 us (2%)
    pallas_call x4, Pallas kernels, gather_slabs(): pl.pallas_call(kernel, out_shape=shapes, in_specs=[SMEM, SMEM, VMEM], out...  25.6 us
    pallas_call x1, Pallas kernels, score_rows(): pl.pallas_call(kernel, out_shape=[jax.ShapeDtypeStruct((half, children),...  19.9 us
    ppermute x15, starting transfers between devices, body(): lax.ppermute(out, HALF, pairs[shift * near:(shift + 1) * near])  19.3 us
    ppermute x15, waiting for transfers between devices, body(): lax.ppermute(out, HALF, pairs[shift * near:(shift + 1) * near])  11.5 us
    all_to_all x1, starting transfers between devices, body(): lax.all_to_all(wanted.reshape(peers, 1, stride), AXES, split_axis=0, conc...  7.32 us
    ppermute x1, waiting for transfers between devices, body(): back = lax.ppermute(lent, 'ah', swap)  5.01 us
    pallas_call x1, Pallas kernels, arrange_past(): pl.pallas_call(kernel, out_shape=jax.ShapeDtypeStruct((queries * lanes, w...  4.6 us
    all_to_all x1, waiting for transfers between devices, body(): lax.all_to_all(wanted.reshape(peers, 1, stride), AXES, split_axis=0, conc...  3.63 us
  transfers between devices with their start and end apart: 19, of which 9 were waited for; matrix products, arithmetic and copies ran while one was open for 5% of the time, Pallas kernels for 25%

profile of v3, /device:TPU:0, one launch (start us, length us, event | category | flops | bytes accessed | tf_op | source)
XLA Modules:
  0.0 119.4 jit_solution(5911986257350306311)
XLA Ops:
  0.0 0.8 reshape.487
  1.2 0.8 select_convert_fusion.1
  2.0 0.5 fusion.11
  2.5 0.7 reshape.490
  3.2 0.7 copy.17
  4.3 0.3 fusion.7
  4.7 1.4 %fusion = f32[64,320]{1,0:T(8,128)S(1)} fusion(s32[4096]{0:T(1024)S(1)} %convert_bitcast_fusion, bf16[4096,32]{0,1:T(8,128)(2,1)S(1)} %get-tuple-element.52, bf16[4096,32]{0,1:T(8,128)(2,1)S(1)} %get-tuple-element.51), kind=kOutput, calls=%fused_computation.1 | convolution fusion | flops 170131456 | bytes 622592 | tf_op jit(solution)/shard_map/io,is->os/dot_general | solution.py:42
  6.2 0.7 copy.15
  6.9 7.3 %all-to-all-start = ((s32[32,1,384]{2,1,0:T(1,128)}), s32[32,1,384]{2,1,0:T(1,128)S(1)}, u32[]{:S(2)}, u32[]{:S(2)}) async-start(s32[32,1,384]{2,1,0:T(1,128)} %copy.15), calls=%async_computation | async-start | bytes 98304 | tf_op jit(solution)/shard_map/all_to_all | solution.py:299
  14.4 2.7 %collective-permute-start = (s32[16,394]{1,0:T(8,128)S(1)}, s32[16,394]{1,0:T(8,128)S(1)}, u32[]{:S(2)}, u32[]{:S(2)}) collective-permute-start(s32[16,394]{1,0:T(8,128)S(1)} %pad_add_fusion), channel_id=1, source_target_pairs={{0,4},{4,0},{1,5},{5,1},{2,6},{6,2},{3,7},{7,3},{8,12},{12,8},{9,1... | collective-permute-start | bytes 75656 | tf_op jit(solution)/shard_map/ppermute | solution.py:304
  17.3 0.6 mul.115.order_ref
  17.9 3.6 %all-to-all-done = s32[32,1,384]{2,1,0:T(1,128)S(1)} async-done(((s32[32,1,384]{2,1,0:T(1,128)}), s32[32,1,384]{2,1,0:T(1,128)S(1)}, u32[]{:S(2)}, u32[]{:S(2)}) %all-to-all-start) | async-done | bytes 49184 | tf_op jit(solution)/shard_map/all_to_all | solution.py:299
  21.6 0.6 copy-done.1
  22.2 3.5 %gather_slabs.3.rest_0_ = bf16[640,128]{1,0:T(8,128)(2,1)} custom-call(s32[32]{0:T(128)} %mul.115.order_ref, s32[12288]{0:T(1024)} %bitcast.59, bf16[8192,128]{1,0:T(8,128)(2,1)} %table_ref.7), custom_call_target="tpu_custom_call" | custom-call | tf_op jit(solution)/shard_map/gather_slabs/pallas_call | solution.py:109
  25.7 8.6 %gather_past.1 = (bf16[2304,128]{1,0:T(8,128)(2,1)}, bf16[640,128]{1,0:T(8,128)(2,1)}, bf16[640,128]{1,0:T(8,128)(2,1)}, bf16[640,128]{1,0:T(8,128)(2,1)}, bf16[...) custom-call(s32[32]{0:T(128)} %mul.115.order_ref, s32[12288]{0:T(1024)} %bitcast.60, bf16[8192,128]{1,0:T(8,128)(2,1)} %table_ref.7), custom_call_target="tpu_custom_call" | custom-call | tf_op jit(solution)/shard_map/gather_past/pallas_call | solution.py:109
  34.3 2.6 %all-to-all-start.1 = ((bf16[32,72,128]{2,1,0:T(8,128)(2,1)}), bf16[32,72,128]{2,1,0:T(8,128)(2,1)S(1)}, u32[]{:S(2)}, u32[]{:S(2)}) async-start(bf16[32,72,128]{2,1,0:T(8,128)(2,1)} %bitcast.63), calls=%async_computation.1 | async-start | bytes 1179648 | tf_op jit(solution)/shard_map/all_to_all | solution.py:321
  37.8 0.5 slice.52
  38.5 8.2 %gather_slabs.4 = (bf16[640,128]{1,0:T(8,128)(2,1)}, bf16[640,128]{1,0:T(8,128)(2,1)}, bf16[640,128]{1,0:T(8,128)(2,1)}, bf16[640,128]{1,0:T(8,128)(2,1)}, bf16[...) custom-call(s32[32]{0:T(128)} %mul.115.order_ref, s32[12288]{0:T(1024)} %bitcast.61, ...), custom_call_target="tpu_custom_call" | custom-call | tf_op jit(solution)/shard_map/gather_slabs/pallas_call | solution.py:109
  46.7 5.2 %gather_slabs.5 = (bf16[640,128]{1,0:T(8,128)(2,1)}, bf16[640,128]{1,0:T(8,128)(2,1)}, bf16[640,128]{1,0:T(8,128)(2,1)}) custom-call(s32[32]{0:T(128)} %mul.115.order_ref, s32[12288]{0:T(1024)} %bitcast.62, bf16[8192,128]{1,0:T(8,128)(2,1)} %table_ref.7), custom_call_target="tpu_custom_call" | custom-call | tf_op jit(solution)/shard_map/gather_slabs/pallas_call | solution.py:109
  52.3 1.6 %collective-permute-start.1 = (bf16[640,128]{1,0:T(8,128)(2,1)}, bf16[640,128]{1,0:T(8,128)(2,1)S(1)}, u32[]{:S(2)}, u32[]{:S(2)}) collective-permute-start(bf16[640,128]{1,0:T(8,128)(2,1)} %get-tuple-element.28), channel_id=1, source_target_pairs={{0,1},{1,0},{2,3},{3,2},{8,9},{9,8},{10,11},{11,10},{16,17},{17,16... | collective-permute-start | bytes 491528 | tf_op jit(solution)/shard_map/ppermute | solution.py:328
  53.9 1.5 %collective-permute-start.2 = (bf16[640,128]{1,0:T(8,128)(2,1)S(1)}, bf16[640,128]{1,0:T(8,128)(2,1)S(1)}, u32[]{:S(2)}, u32[]{:S(2)}) collective-permute-start(bf16[640,128]{1,0:T(8,128)(2,1)S(1)} %copy-done.29), channel_id=1, source_target_pairs={{0,2},{1,3},{2,0},{3,1},{8,10},{9,11},{10,8},{11,9},{16,18},{17,19... | collective-permute-start | bytes 491528 | tf_op jit(solution)/shard_map/ppermute | solution.py:328
  55.4 0.3 collective-permute-start.3
  55.8 1.7 %collective-permute-start.5 = (bf16[640,128]{1,0:T(8,128)(2,1)S(1)}, bf16[640,128]{1,0:T(8,128)(2,1)S(1)}, u32[]{:S(2)}, u32[]{:S(2)}) collective-permute-start(bf16[640,128]{1,0:T(8,128)(2,1)S(1)} %copy-done.26), channel_id=1, source_target_pairs={{0,9},{1,8},{2,11},{3,10},{8,1},{9,0},{10,3},{11,2},{16,25},{17,24... | collective-permute-start | bytes 491528 | tf_op jit(solution)/shard_map/ppermute | solution.py:328
  57.5 0.3 fusion.6
  57.9 0.7 convert_add_fusion.rel_ref
  58.6 0.3 collective-permute-done.1.rest_1_
  58.9 1.0 collective-permute-start.6
  59.9 1.1 collective-permute-done.2.rest_2_
  61.0 1.5 %collective-permute-start.8 = (bf16[640,128]{1,0:T(8,128)(2,1)S(1)}, bf16[640,128]{1,0:T(8,128)(2,1)S(1)}, u32[]{:S(2)}, u32[]{:S(2)}) collective-permute-start(bf16[640,128]{1,0:T(8,128)(2,1)S(1)} %copy-done.25), channel_id=1, source_target_pairs={{0,16},{1,17},{2,18},{3,19},{8,24},{9,25},{10,26},{11,27},{16,0},{... | collective-permute-start | bytes 491528 | tf_op jit(solution)/shard_map/ppermute | solution.py:328
  62.5 1.1 collective-permute-done.3.rest_3_
  63.6 2.5 %collective-permute-start.10 = (bf16[640,128]{1,0:T(8,128)(2,1)S(1)}, bf16[640,128]{1,0:T(8,128)(2,1)S(1)}, u32[]{:S(2)}, u32[]{:S(2)}) collective-permute-start(bf16[640,128]{1,0:T(8,128)(2,1)S(1)} %copy-done.24), channel_id=1, source_target_pairs={{0,18},{1,19},{2,16},{3,17},{8,26},{9,27},{10,24},{11,25},{16,2},{... | collective-permute-start | bytes 491528 | tf_op jit(solution)/shard_map/ppermute | solution.py:328
  66.1 2.3 %collective-permute-start.11 = (bf16[640,128]{1,0:T(8,128)(2,1)S(1)}, bf16[640,128]{1,0:T(8,128)(2,1)S(1)}, u32[]{:S(2)}, u32[]{:S(2)}) collective-permute-start(bf16[640,128]{1,0:T(8,128)(2,1)S(1)} %copy-done.23), channel_id=1, source_target_pairs={{0,19},{1,18},{2,17},{3,16},{8,27},{9,26},{10,25},{11,24},{16,3},{... | collective-permute-start | bytes 491528 | tf_op jit(solution)/shard_map/ppermute | solution.py:328
  68.6 1.9 %collective-permute-start.7 = (bf16[640,128]{1,0:T(8,128)(2,1)S(1)}, bf16[640,128]{1,0:T(8,128)(2,1)S(1)}, u32[]{:S(2)}, u32[]{:S(2)}) collective-permute-start(bf16[640,128]{1,0:T(8,128)(2,1)S(1)} %copy-done.21), channel_id=1, source_target_pairs={{0,11},{1,10},{2,9},{3,8},{8,3},{9,2},{10,1},{11,0},{16,27},{17,26... | collective-permute-start | bytes 491528 | tf_op jit(solution)/shard_map/ppermute | solution.py:328
  70.4 2.4 %collective-permute-start.9 = (bf16[640,128]{1,0:T(8,128)(2,1)S(1)}, bf16[640,128]{1,0:T(8,128)(2,1)S(1)}, u32[]{:S(2)}, u32[]{:S(2)}) collective-permute-start(bf16[640,128]{1,0:T(8,128)(2,1)S(1)} %copy-done.20), channel_id=1, source_target_pairs={{0,17},{1,16},{2,19},{3,18},{8,25},{9,24},{10,27},{11,26},{16,1},{... | collective-permute-start | bytes 491528 | tf_op jit(solution)/shard_map/ppermute | solution.py:328
  72.8 0.2 collective-permute-done.10.rest_10_
  73.1 3.3 %collective-permute-done.11.rest_11_ = bf16[640,128]{1,0:T(8,128)(2,1)S(1)} collective-permute-done((bf16[640,128]{1,0:T(8,128)(2,1)S(1)}, bf16[640,128]{1,0:T(8,128)(2,1)S(1)}, u32[]{:S(2)}, u32[]{:S(2)}) %collective-permute-start.11) | collective-permute-done | bytes 163872 | tf_op jit(solution)/shard_map/ppermute | solution.py:328
  76.4 2.1 %collective-permute-done.12.rest_12_ = bf16[640,128]{1,0:T(8,128)(2,1)S(1)} collective-permute-done((bf16[640,128]{1,0:T(8,128)(2,1)S(1)}, bf16[640,128]{1,0:T(8,128)(2,1)S(1)}, u32[]{:S(2)}, u32[]{:S(2)}) %collective-permute-start.12) | collective-permute-done | bytes 163872 | tf_op jit(solution)/shard_map/ppermute | solution.py:328
  78.5 2.4 %collective-permute-start.15 = (bf16[640,128]{1,0:T(8,128)(2,1)}, bf16[640,128]{1,0:T(8,128)(2,1)S(1)}, u32[]{:S(2)}, u32[]{:S(2)}) collective-permute-start(bf16[640,128]{1,0:T(8,128)(2,1)} %get-tuple-element.42), channel_id=1, source_target_pairs={{0,27},{1,26},{2,25},{3,24},{8,19},{9,18},{10,17},{11,16},{16,11},... | collective-permute-start | bytes 491528 | tf_op jit(solution)/shard_map/ppermute | solution.py:328
  80.9 1.3 %pad_add_fusion.3.base_ref = s32[33]{0:T(128)} fusion(s32[1]{0:T(128)} %bitcast.14, s32[32]{0:T(128)S(1)} %get-tuple-element.46), kind=kLoop, calls=%fused_computation.176 | loop fusion | flops 33 | bytes 264 | tf_op jit(solution)/shard_map/concatenate | solution.py:353
  82.2 0.7 reshape.494.slot_ref
  82.9 0.6 pad_add_fusion.2.seg_ref
  83.5 0.8 copy-done
  84.3 4.6 %arrange_past.1.past_ref = bf16[4096,128]{1,0:T(8,128)(2,1)} custom-call(s32[2208]{0:T(1024)} %reshape.494.slot_ref, bf16[2304,128]{1,0:T(8,128)(2,1)} %bitcast.58), custom_call_target="tpu_custom_call" | custom-call | tf_op jit(solution)/shard_map/arrange_past/pallas_call | solution.py:140
  89.0 3.4 %collective-permute-done.13.rest_13_ = bf16[640,128]{1,0:T(8,128)(2,1)S(1)} collective-permute-done((bf16[640,128]{1,0:T(8,128)(2,1)}, bf16[640,128]{1,0:T(8,128)(2,1)S(1)}, u32[]{:S(2)}, u32[]{:S(2)}) %collective-permute-start.13) | collective-permute-done | bytes 163872 | tf_op jit(solution)/shard_map/ppermute | solution.py:328
  92.4 0.7 broadcast_in_dim.49.wo
  93.2 19.9 %score_rows.1 = (f32[16,256]{1,0:T(8,128)}, f32[16,256]{1,0:T(8,128)}) custom-call(s32[1536]{0:T(1024)} %pad_add_fusion.2.seg_ref, s32[33]{0:T(128)} %pad_add_fusion.3.base_ref, s32[32,256]{1,0:T(8,128)} %convert_add_fusion.rel_ref, bf16[4096,128]{1,0:T(8,128)(2,1)} %arrange_past.1.past_ref, bf16[256,512]{1,0:T(8,128)(2,1)} %w1.1, f32[1,512]{1,0:T(1,128)} %bitcast.74, ...), custom_call_target="tpu_custom_call" | custom-call | tf_op jit(solution)/shard_map/score_rows/pallas_call | solution.py:243
  113.1 5.0 %collective-permute-done.16 = f32[16,256]{1,0:T(8,128)S(1)} collective-permute-done((f32[16,256]{1,0:T(8,128)}, f32[16,256]{1,0:T(8,128)S(1)}, u32[]{:S(2)}, u32[]{:S(2)}) %collective-permute-start.16) | collective-permute-done | bytes 16416 | tf_op jit(solution)/shard_map/ppermute | solution.py:363
  118.1 1.3 %fusion.55 = f32[16,256]{1,0:T(8,128)} fusion(f32[16,256]{1,0:T(8,128)} %get-tuple-element.43, f32[16,256]{1,0:T(8,128)S(1)} %collective-permute-done.16, pred[2,16,256]{2,1,0:T(8,128)(4,1)S(1)} %get-tuple-element.48), kind=kLoop, calls=%fused_computation.120 | loop fusion | flops 12288 | bytes 53248 | tf_op jit(solution)/shard_map/jit(_where)/select_n | solution.py:364
  (119 shorter events, 2.9 us)
Async XLA Ops:
  4.6 9.7 %copy-start.18 = (s32[16,69]{1,0:T(8,128)S(1)}, s32[16,69]{1,0:T(8,128)}, u32[]{:S(2)}) copy-start(s32[16,69]{1,0:T(8,128)} %param.9) | copy-start | bytes 13252
  4.6 9.7 %copy-start.17 = (s32[16,256]{1,0:T(8,128)S(1)}, s32[16,256]{1,0:T(8,128)}, u32[]{:S(2)}) copy-start(s32[16,256]{1,0:T(8,128)} %param.8) | copy-start | bytes 49156
  6.9 14.7 %all-to-all-start = ((s32[32,1,384]{2,1,0:T(1,128)}), s32[32,1,384]{2,1,0:T(1,128)S(1)}, u32[]{:S(2)}, u32[]{:S(2)}) async-start(s32[32,1,384]{2,1,0:T(1,128)} %copy.15), calls=%async_computation | async-start | bytes 98304 | tf_op jit(solution)/shard_map/all_to_all | solution.py:299
  14.4 19.9 %collective-permute-start = (s32[16,394]{1,0:T(8,128)S(1)}, s32[16,394]{1,0:T(8,128)S(1)}, u32[]{:S(2)}, u32[]{:S(2)}) collective-permute-start(s32[16,394]{1,0:T(8,128)S(1)} %pad_add_fusion), channel_id=1, source_target_pairs={{0,4},{4,0},{1,5},{5,1},{2,6},{6,2},{3,7},{7,3},{8,12},{12,8},{9,1... | collective-permute-start | bytes 75656 | tf_op jit(solution)/shard_map/ppermute | solution.py:304
  34.3 49.2 %all-to-all-start.1 = ((bf16[32,72,128]{2,1,0:T(8,128)(2,1)}), bf16[32,72,128]{2,1,0:T(8,128)(2,1)S(1)}, u32[]{:S(2)}, u32[]{:S(2)}) async-start(bf16[32,72,128]{2,1,0:T(8,128)(2,1)} %bitcast.63), calls=%async_computation.1 | async-start | bytes 1179648 | tf_op jit(solution)/shard_map/all_to_all | solution.py:321
  46.7 7.2 %copy-start.29 = (bf16[640,128]{1,0:T(8,128)(2,1)S(1)}, bf16[640,128]{1,0:T(8,128)(2,1)}, u32[]{:S(2)}) copy-start(bf16[640,128]{1,0:T(8,128)(2,1)} %get-tuple-element.29) | copy-start | bytes 491524
  46.7 8.8 %copy-start.28 = (bf16[640,128]{1,0:T(8,128)(2,1)S(1)}, bf16[640,128]{1,0:T(8,128)(2,1)}, u32[]{:S(2)}) copy-start(bf16[640,128]{1,0:T(8,128)(2,1)} %get-tuple-element.30) | copy-start | bytes 491524
  46.7 9.1 %copy-start.27 = (bf16[640,128]{1,0:T(8,128)(2,1)S(1)}, bf16[640,128]{1,0:T(8,128)(2,1)}, u32[]{:S(2)}) copy-start(bf16[640,128]{1,0:T(8,128)(2,1)} %get-tuple-element.31) | copy-start | bytes 491524
  46.7 9.1 %copy-start.26 = (bf16[640,128]{1,0:T(8,128)(2,1)S(1)}, bf16[640,128]{1,0:T(8,128)(2,1)}, u32[]{:S(2)}) copy-start(bf16[640,128]{1,0:T(8,128)(2,1)} %get-tuple-element.32) | copy-start | bytes 491524
  46.7 14.3 %copy-start.25 = (bf16[640,128]{1,0:T(8,128)(2,1)S(1)}, bf16[640,128]{1,0:T(8,128)(2,1)}, u32[]{:S(2)}) copy-start(bf16[640,128]{1,0:T(8,128)(2,1)} %get-tuple-element.35) | copy-start | bytes 491524
  46.7 16.9 %copy-start.24 = (bf16[640,128]{1,0:T(8,128)(2,1)S(1)}, bf16[640,128]{1,0:T(8,128)(2,1)}, u32[]{:S(2)}) copy-start(bf16[640,128]{1,0:T(8,128)(2,1)} %get-tuple-element.37) | copy-start | bytes 491524
  46.7 19.4 %copy-start.23 = (bf16[640,128]{1,0:T(8,128)(2,1)S(1)}, bf16[640,128]{1,0:T(8,128)(2,1)}, u32[]{:S(2)}) copy-start(bf16[640,128]{1,0:T(8,128)(2,1)} %get-tuple-element.38) | copy-start | bytes 491524
  46.7 21.7 %copy-start.22 = (bf16[640,128]{1,0:T(8,128)(2,1)S(1)}, bf16[640,128]{1,0:T(8,128)(2,1)}, u32[]{:S(2)}) copy-start(bf16[640,128]{1,0:T(8,128)(2,1)} %get-tuple-element.39) | copy-start | bytes 491524
  46.7 21.8 %copy-start.21 = (bf16[640,128]{1,0:T(8,128)(2,1)S(1)}, bf16[640,128]{1,0:T(8,128)(2,1)}, u32[]{:S(2)}) copy-start(bf16[640,128]{1,0:T(8,128)(2,1)} %get-tuple-element.34) | copy-start | bytes 491524
  46.7 23.7 %copy-start.20 = (bf16[640,128]{1,0:T(8,128)(2,1)S(1)}, bf16[640,128]{1,0:T(8,128)(2,1)}, u32[]{:S(2)}) copy-start(bf16[640,128]{1,0:T(8,128)(2,1)} %get-tuple-element.36) | copy-start | bytes 491524
  46.7 45.6 %copy-start.19 = (bf16[512]{0:T(512)(128)(2,1)S(1)}, bf16[512]{0:T(512)(128)(2,1)}, u32[]{:S(2)}) copy-start(bf16[512]{0:T(512)(128)(2,1)} %param.15) | copy-start | bytes 3076
  52.3 6.6 %collective-permute-start.1 = (bf16[640,128]{1,0:T(8,128)(2,1)}, bf16[640,128]{1,0:T(8,128)(2,1)S(1)}, u32[]{:S(2)}, u32[]{:S(2)}) collective-permute-start(bf16[640,128]{1,0:T(8,128)(2,1)} %get-tuple-element.28), channel_id=1, source_target_pairs={{0,1},{1,0},{2,3},{3,2},{8,9},{9,8},{10,11},{11,10},{16,17},{17,16... | collective-permute-start | bytes 491528 | tf_op jit(solution)/shard_map/ppermute | solution.py:328
  53.9 7.1 %collective-permute-start.2 = (bf16[640,128]{1,0:T(8,128)(2,1)S(1)}, bf16[640,128]{1,0:T(8,128)(2,1)S(1)}, u32[]{:S(2)}, u32[]{:S(2)}) collective-permute-start(bf16[640,128]{1,0:T(8,128)(2,1)S(1)} %copy-done.29), channel_id=1, source_target_pairs={{0,2},{1,3},{2,0},{3,1},{8,10},{9,11},{10,8},{11,9},{16,18},{17,19... | collective-permute-start | bytes 491528 | tf_op jit(solution)/shard_map/ppermute | solution.py:328
  55.4 8.1 %collective-permute-start.3 = (bf16[640,128]{1,0:T(8,128)(2,1)S(1)}, bf16[640,128]{1,0:T(8,128)(2,1)S(1)}, u32[]{:S(2)}, u32[]{:S(2)}) collective-permute-start(bf16[640,128]{1,0:T(8,128)(2,1)S(1)} %copy-done.28), channel_id=1, source_target_pairs={{0,3},{1,2},{2,1},{3,0},{8,11},{9,10},{10,9},{11,8},{16,19},{17,18... | collective-permute-start | bytes 491528 | tf_op jit(solution)/shard_map/ppermute | solution.py:328
  55.8 10.3 %collective-permute-start.4 = (bf16[640,128]{1,0:T(8,128)(2,1)S(1)}, bf16[640,128]{1,0:T(8,128)(2,1)S(1)}, u32[]{:S(2)}, u32[]{:S(2)}) collective-permute-start(bf16[640,128]{1,0:T(8,128)(2,1)S(1)} %copy-done.27), channel_id=1, source_target_pairs={{0,8},{1,9},{2,10},{3,11},{8,0},{9,1},{10,2},{11,3},{16,24},{17,25... | collective-permute-start | bytes 491528 | tf_op jit(solution)/shard_map/ppermute | solution.py:328
  55.8 12.7 %collective-permute-start.5 = (bf16[640,128]{1,0:T(8,128)(2,1)S(1)}, bf16[640,128]{1,0:T(8,128)(2,1)S(1)}, u32[]{:S(2)}, u32[]{:S(2)}) collective-permute-start(bf16[640,128]{1,0:T(8,128)(2,1)S(1)} %copy-done.26), channel_id=1, source_target_pairs={{0,9},{1,8},{2,11},{3,10},{8,1},{9,0},{10,3},{11,2},{16,25},{17,24... | collective-permute-start | bytes 491528 | tf_op jit(solution)/shard_map/ppermute | solution.py:328
  58.9 34.2 %copy-start.2 = (bf16[640,128]{1,0:T(8,128)(2,1)}, bf16[640,128]{1,0:T(8,128)(2,1)S(1)}, u32[]{:S(2)}) copy-start(bf16[640,128]{1,0:T(8,128)(2,1)S(1)} %collective-permute-done.1.rest_1_) | copy-start | bytes 491524
  58.9 9.7 %collective-permute-start.6 = (bf16[640,128]{1,0:T(8,128)(2,1)}, bf16[640,128]{1,0:T(8,128)(2,1)S(1)}, u32[]{:S(2)}, u32[]{:S(2)}) collective-permute-start(bf16[640,128]{1,0:T(8,128)(2,1)} %get-tuple-element.33), channel_id=1, source_target_pairs={{0,10},{1,11},{2,8},{3,9},{8,2},{9,3},{10,0},{11,1},{16,26},{17,27... | collective-permute-start | bytes 491528 | tf_op jit(solution)/shard_map/ppermute | solution.py:328
  61.0 32.1 %copy-start.3 = (bf16[640,128]{1,0:T(8,128)(2,1)}, bf16[640,128]{1,0:T(8,128)(2,1)S(1)}, u32[]{:S(2)}) copy-start(bf16[640,128]{1,0:T(8,128)(2,1)S(1)} %collective-permute-done.2.rest_2_) | copy-start | bytes 491524
  61.0 9.5 %collective-permute-start.8 = (bf16[640,128]{1,0:T(8,128)(2,1)S(1)}, bf16[640,128]{1,0:T(8,128)(2,1)S(1)}, u32[]{:S(2)}, u32[]{:S(2)}) collective-permute-start(bf16[640,128]{1,0:T(8,128)(2,1)S(1)} %copy-done.25), channel_id=1, source_target_pairs={{0,16},{1,17},{2,18},{3,19},{8,24},{9,25},{10,26},{11,27},{16,0},{... | collective-permute-start | bytes 491528 | tf_op jit(solution)/shard_map/ppermute | solution.py:328
  63.6 29.5 %copy-start.4 = (bf16[640,128]{1,0:T(8,128)(2,1)}, bf16[640,128]{1,0:T(8,128)(2,1)S(1)}, u32[]{:S(2)}) copy-start(bf16[640,128]{1,0:T(8,128)(2,1)S(1)} %collective-permute-done.3.rest_3_) | copy-start | bytes 491524
  63.6 9.5 %collective-permute-start.10 = (bf16[640,128]{1,0:T(8,128)(2,1)S(1)}, bf16[640,128]{1,0:T(8,128)(2,1)S(1)}, u32[]{:S(2)}, u32[]{:S(2)}) collective-permute-start(bf16[640,128]{1,0:T(8,128)(2,1)S(1)} %copy-done.24), channel_id=1, source_target_pairs={{0,18},{1,19},{2,16},{3,17},{8,26},{9,27},{10,24},{11,25},{16,2},{... | collective-permute-start | bytes 491528 | tf_op jit(solution)/shard_map/ppermute | solution.py:328
  66.1 26.9 %copy-start.5 = (bf16[640,128]{1,0:T(8,128)(2,1)}, bf16[640,128]{1,0:T(8,128)(2,1)S(1)}, u32[]{:S(2)}) copy-start(bf16[640,128]{1,0:T(8,128)(2,1)S(1)} %collective-permute-done.4.rest_4_) | copy-start | bytes 491524
  66.1 10.3 %collective-permute-start.11 = (bf16[640,128]{1,0:T(8,128)(2,1)S(1)}, bf16[640,128]{1,0:T(8,128)(2,1)S(1)}, u32[]{:S(2)}, u32[]{:S(2)}) collective-permute-start(bf16[640,128]{1,0:T(8,128)(2,1)S(1)} %copy-done.23), channel_id=1, source_target_pairs={{0,19},{1,18},{2,17},{3,16},{8,27},{9,26},{10,25},{11,24},{16,3},{... | collective-permute-start | bytes 491528 | tf_op jit(solution)/shard_map/ppermute | solution.py:328
  68.4 24.6 %copy-start.6 = (bf16[640,128]{1,0:T(8,128)(2,1)}, bf16[640,128]{1,0:T(8,128)(2,1)S(1)}, u32[]{:S(2)}) copy-start(bf16[640,128]{1,0:T(8,128)(2,1)S(1)} %collective-permute-done.5.rest_5_) | copy-start | bytes 491524
  68.4 10.1 %collective-permute-start.12 = (bf16[640,128]{1,0:T(8,128)(2,1)S(1)}, bf16[640,128]{1,0:T(8,128)(2,1)S(1)}, u32[]{:S(2)}, u32[]{:S(2)}) collective-permute-start(bf16[640,128]{1,0:T(8,128)(2,1)S(1)} %copy-done.22), channel_id=1, source_target_pairs={{0,24},{1,25},{2,26},{3,27},{8,16},{9,17},{10,18},{11,19},{16,8},{... | collective-permute-start | bytes 491528 | tf_op jit(solution)/shard_map/ppermute | solution.py:328
  68.5 24.5 %copy-start.7 = (bf16[640,128]{1,0:T(8,128)(2,1)}, bf16[640,128]{1,0:T(8,128)(2,1)S(1)}, u32[]{:S(2)}) copy-start(bf16[640,128]{1,0:T(8,128)(2,1)S(1)} %collective-permute-done.6.rest_6_) | copy-start | bytes 491524
  68.6 20.4 %collective-permute-start.7 = (bf16[640,128]{1,0:T(8,128)(2,1)S(1)}, bf16[640,128]{1,0:T(8,128)(2,1)S(1)}, u32[]{:S(2)}, u32[]{:S(2)}) collective-permute-start(bf16[640,128]{1,0:T(8,128)(2,1)S(1)} %copy-done.21), channel_id=1, source_target_pairs={{0,11},{1,10},{2,9},{3,8},{8,3},{9,2},{10,1},{11,0},{16,27},{17,26... | collective-permute-start | bytes 491528 | tf_op jit(solution)/shard_map/ppermute | solution.py:328
  70.4 22.6 %copy-start.8 = (bf16[640,128]{1,0:T(8,128)(2,1)}, bf16[640,128]{1,0:T(8,128)(2,1)S(1)}, u32[]{:S(2)}) copy-start(bf16[640,128]{1,0:T(8,128)(2,1)S(1)} %collective-permute-done.8.rest_8_) | copy-start | bytes 491524
  70.4 18.5 %collective-permute-start.9 = (bf16[640,128]{1,0:T(8,128)(2,1)S(1)}, bf16[640,128]{1,0:T(8,128)(2,1)S(1)}, u32[]{:S(2)}, u32[]{:S(2)}) collective-permute-start(bf16[640,128]{1,0:T(8,128)(2,1)S(1)} %copy-done.20), channel_id=1, source_target_pairs={{0,17},{1,16},{2,19},{3,18},{8,25},{9,24},{10,27},{11,26},{16,1},{... | collective-permute-start | bytes 491528 | tf_op jit(solution)/shard_map/ppermute | solution.py:328
  73.1 20.0 %copy-start.9 = (bf16[640,128]{1,0:T(8,128)(2,1)}, bf16[640,128]{1,0:T(8,128)(2,1)S(1)}, u32[]{:S(2)}) copy-start(bf16[640,128]{1,0:T(8,128)(2,1)S(1)} %collective-permute-done.10.rest_10_) | copy-start | bytes 491524
  73.1 19.3 %collective-permute-start.13 = (bf16[640,128]{1,0:T(8,128)(2,1)}, bf16[640,128]{1,0:T(8,128)(2,1)S(1)}, u32[]{:S(2)}, u32[]{:S(2)}) collective-permute-start(bf16[640,128]{1,0:T(8,128)(2,1)} %get-tuple-element.40), channel_id=1, source_target_pairs={{0,25},{1,24},{2,27},{3,26},{8,17},{9,16},{10,19},{11,18},{16,9},{... | collective-permute-start | bytes 491528 | tf_op jit(solution)/shard_map/ppermute | solution.py:328
  76.4 16.7 %copy-start.10 = (bf16[640,128]{1,0:T(8,128)(2,1)}, bf16[640,128]{1,0:T(8,128)(2,1)S(1)}, u32[]{:S(2)}) copy-start(bf16[640,128]{1,0:T(8,128)(2,1)S(1)} %collective-permute-done.11.rest_11_) | copy-start | bytes 491524
  76.4 16.0 %collective-permute-start.14 = (bf16[640,128]{1,0:T(8,128)(2,1)}, bf16[640,128]{1,0:T(8,128)(2,1)S(1)}, u32[]{:S(2)}, u32[]{:S(2)}) collective-permute-start(bf16[640,128]{1,0:T(8,128)(2,1)} %get-tuple-element.41), channel_id=1, source_target_pairs={{0,26},{1,27},{2,24},{3,25},{8,18},{9,19},{10,16},{11,17},{16,10},... | collective-permute-start | bytes 491528 | tf_op jit(solution)/shard_map/ppermute | solution.py:328
  78.5 14.6 %copy-start.11 = (bf16[640,128]{1,0:T(8,128)(2,1)}, bf16[640,128]{1,0:T(8,128)(2,1)S(1)}, u32[]{:S(2)}) copy-start(bf16[640,128]{1,0:T(8,128)(2,1)S(1)} %collective-permute-done.12.rest_12_) | copy-start | bytes 491524
  78.5 13.8 %collective-permute-start.15 = (bf16[640,128]{1,0:T(8,128)(2,1)}, bf16[640,128]{1,0:T(8,128)(2,1)S(1)}, u32[]{:S(2)}, u32[]{:S(2)}) collective-permute-start(bf16[640,128]{1,0:T(8,128)(2,1)} %get-tuple-element.42), channel_id=1, source_target_pairs={{0,27},{1,26},{2,25},{3,24},{8,19},{9,18},{10,17},{11,16},{16,11},... | collective-permute-start | bytes 491528 | tf_op jit(solution)/shard_map/ppermute | solution.py:328
  83.5 0.8 copy-start
  88.9 4.2 %copy-start.12 = (bf16[640,128]{1,0:T(8,128)(2,1)}, bf16[640,128]{1,0:T(8,128)(2,1)S(1)}, u32[]{:S(2)}) copy-start(bf16[640,128]{1,0:T(8,128)(2,1)S(1)} %collective-permute-done.7.rest_7_) | copy-start | bytes 491524
  88.9 4.2 %copy-start.13 = (bf16[640,128]{1,0:T(8,128)(2,1)}, bf16[640,128]{1,0:T(8,128)(2,1)S(1)}, u32[]{:S(2)}) copy-start(bf16[640,128]{1,0:T(8,128)(2,1)S(1)} %collective-permute-done.9.rest_9_) | copy-start | bytes 491524
  92.3 0.8 copy-start.14
  92.3 0.8 copy-start.15
  92.3 0.8 copy-start.16
  113.0 5.1 %collective-permute-start.16 = (f32[16,256]{1,0:T(8,128)}, f32[16,256]{1,0:T(8,128)S(1)}, u32[]{:S(2)}, u32[]{:S(2)}) collective-permute-start(f32[16,256]{1,0:T(8,128)} %get-tuple-element.44), channel_id=1, source_target_pairs={{0,4},{4,0},{1,5},{5,1},{2,6},{6,2},{3,7},{7,3},{8,12},{12,8},{9,1... | collective-permute-start | bytes 49160 | tf_op jit(solution)/shard_map/ppermute | solution.py:363
  (1 other events, 0.6 us)

commit v4 on v3

v4 whole, which is shorter than its diff:
```python
import jax
import jax.numpy as jnp
from jax import lax
from jax.experimental import pallas as pl
from jax.experimental.pallas import tpu as pltpu
from jax.sharding import Mesh
from jax.sharding import PartitionSpec as P

AXES = ("pb", "ah", "al")
HALF = ("pb", "al")
BLOCK = 1024


def rounded(n, m):
    return -(-n // m) * m


def unroll_of(n, most=64):
    return max(u for u in range(1, most + 1) if n % u == 0)


VMEM = pl.BlockSpec(memory_space=pltpu.VMEM)
SMEM = pl.BlockSpec(memory_space=pltpu.SMEM)


def near_by(x):
    return pltpu.with_memory_space_constraint(x, pltpu.VMEM)


def widen(src, dst, rows, at=0, step=128):
    def go(i, c):
        dst[pl.ds(at + i * step, step), :] = src[pl.ds(i * step, step), :].astype(jnp.float32)
        return c

    step = unroll_of(rows // 8, step // 8) * 8
    lax.fori_loop(0, rows // step, go, 0)


def narrow(src, dst, rows, step=128):
    def go(i, c):
        dst[pl.ds(i * step, step), :] = src[pl.ds(i * step, step), :].astype(jnp.bfloat16)
        return c

    step = unroll_of(rows // 8, step // 8) * 8
    lax.fori_loop(0, rows // step, go, 0)


def split(ids, m):
    if m & (m - 1) == 0:
        return ids >> (m.bit_length() - 1), ids & (m - 1)
    return ids // m, ids % m


def iota(shape, axis):
    return lax.broadcasted_iota(jnp.int32, shape, axis)


def ones_where(mask):
    return jnp.where(mask, 1.0, 0.0).astype(jnp.bfloat16)


def exact_dot(a, b):
    return jnp.dot(a.astype(jnp.bfloat16), b.astype(jnp.bfloat16), preferred_element_type=jnp.float32)


def occurrences(keys, groups):
    rows, lanes = keys.shape
    hits = [keys == g for g in range(groups)]
    stack = jnp.concatenate([ones_where(hit) for hit in hits], axis=0)
    before = exact_dot(stack, ones_where(iota((lanes, lanes), 0) < iota((lanes, lanes), 1)))
    totals = exact_dot(stack, jnp.ones((lanes, 128), jnp.bfloat16))
    lane = iota((rows, 128), 1)
    counts = jnp.zeros((rows, 128), jnp.float32)
    for g in range(groups):
        counts = jnp.where(lane == g, totals[g * rows : (g + 1) * rows], counts)
    return hits, [before[g * rows : (g + 1) * rows] for g in range(groups)], counts


def places(hits, before, shifts):
    out = jnp.zeros(hits[0].shape, jnp.float32)
    for g, hit in enumerate(hits):
        out = jnp.where(hit, before[g] + shifts[:, g : g + 1], out)
    return out.astype(jnp.int32)


def build_lists(child_ids, history_ids, shard_rows, peers, capacity, past_half, stride):
    queries, children = child_ids.shape
    history = history_ids.shape[1]
    lanes = rounded(history, 128)
    digit_rows = rounded(2 * peers, 128)

    def kernel(kid_ref, past_ref, want_ref, ids_ref, pad, acc, spot_ref, digit_ref, *scratch):
        pad[...] = jnp.full(pad.shape, -1, jnp.int32)
        pad[:, :history] = past_ref[...]
        strict = ones_where(iota((queries, queries), 0) > iota((queries, queries), 1))
        for source, low, high, (owner_ref, rank_ref, off_ref) in (
            (kid_ref, 0, capacity, scratch[:3]),
            (pad, capacity, stride, scratch[3:]),
        ):
            owner, offset = split(source[...], shard_rows)
            hits, before, counts = occurrences(owner, peers)
            rank = places(hits, before, exact_dot(strict, counts))
            owner_ref[...] = owner
            rank_ref[...] = rank
            off_ref[...] = offset
            if low:
                ids_ref[:, children:] = owner * (2 * past_half) + rank
            else:
                ids_ref[:, :children] = source[...]
            size = source.shape[1]
            if digit_rows > 2 * peers:
                digit_ref[2 * peers :, :] = jnp.zeros((digit_rows - 2 * peers, digit_ref.shape[1]), jnp.bfloat16)

            def query(q, c, low=low, high=high, owner_ref=owner_ref, rank_ref=rank_ref, off_ref=off_ref, size=size):
                at = pl.ds(pl.multiple_of(q * size, size), size)
                hit = iota((peers, size), 0) == owner_ref[pl.ds(q, 1), :]
                offset = off_ref[pl.ds(q, 1), :].astype(jnp.float32)
                upper = jnp.floor(offset * (1.0 / 256.0))
                digit_ref[:peers, at] = jnp.where(hit, upper, 0.0).astype(jnp.bfloat16)
                digit_ref[peers : 2 * peers, at] = jnp.where(hit, offset - 256.0 * upper, 0.0).astype(jnp.bfloat16)
                spot_ref[: high - low, at] = ones_where(iota((high - low, size), 0) == rank_ref[pl.ds(q, 1), :])
                return c

            lax.fori_loop(0, queries, query, 0, unroll=2)
            acc[low:high, :] = lax.dot_general(
                spot_ref[: high - low, : queries * size],
                digit_ref[:, : queries * size],
                (((1,), (1,)), ((), ())),
                preferred_element_type=jnp.float32,
            )
        digits = acc[...].T.astype(jnp.int32)
        wanted = digits[:peers] * 256 + digits[peers : 2 * peers]
        for o in range(peers):
            want_ref[o, 0:1, :] = wanted[o : o + 1, :]

    return pl.pallas_call(
        kernel,
        out_shape=[
            jax.ShapeDtypeStruct((peers, 1, stride), jnp.int32),
            jax.ShapeDtypeStruct((queries, children + lanes), jnp.int32),
        ],
        in_specs=[VMEM, VMEM],
        out_specs=[VMEM, VMEM],
        scratch_shapes=[
            pltpu.VMEM((queries, lanes), jnp.int32),
            pltpu.VMEM((stride, digit_rows), jnp.float32),
            pltpu.VMEM((max(capacity, stride - capacity), queries * max(children, lanes)), jnp.bfloat16),
            pltpu.VMEM((digit_rows, queries * max(children, lanes)), jnp.bfloat16),
        ]
        + [pltpu.VMEM((queries, children), jnp.int32)] * 3
        + [pltpu.VMEM((queries, lanes), jnp.int32)] * 3,
        name="build_lists",
    )(child_ids, history_ids)


def plan_rows(here, ids, mate_ids, shard_rows, children, al_n, near, capacity, past_half):
    half = ids.shape[0]
    queries = 2 * half
    lanes = ids.shape[1] - children

    def kernel(here_ref, ids_ref, mate_ref, seg_ref, base_ref, rel_ref, slot_ref, mine_ref):
        at, side = here_ref[0], here_ref[1]
        kids = jnp.concatenate([ids_ref[:, :children], mate_ref[:, :children]], axis=0)
        owner, _ = split(kids, shard_rows)
        line, spot = split(owner, al_n)
        block, which_half = split(line, 2)
        local = block * al_n + spot
        part = (local ^ at) if near & (near - 1) == 0 else lax.rem(at - local + near, near)
        inside = which_half == side
        mine_ref[...] = inside[:half].astype(jnp.int32)
        hits, before, counts = occurrences(jnp.where(inside, part, near), near)
        row, col = iota((queries, queries), 0), iota((queries, queries), 1)
        lower = row > col
        starts = exact_dot(ones_where(lower & ((row < half) == (col < half))), counts).astype(jnp.int32)
        square = (128, 128)
        offsets = exact_dot(counts, ones_where(iota(square, 0) < iota(square, 1)))
        lengths = exact_dot(counts, jnp.ones(square, jnp.bfloat16)).astype(jnp.int32)
        lengths = (lengths + 7) & -8
        bases = exact_dot(ones_where(lower), lengths.astype(jnp.float32)).astype(jnp.int32)
        rel_ref[...] = places(hits, before, offsets + (bases & 127).astype(jnp.float32))
        mate_rows = iota((queries, 128), 0) >= half
        seg_ref[:queries] = (
            iota((queries, 128), 1) * (2 * capacity) + jnp.where(mate_rows, capacity, 0) + starts
        )
        seg_ref[queries : 2 * queries] = bases + offsets.astype(jnp.int32)
        seg_ref[2 * queries :] = counts.astype(jnp.int32)
        base_ref[:queries] = bases
        base_ref[queries:] = jnp.broadcast_to((bases + lengths)[queries - 1 :], (8, 128))
        slot_ref[:half] = ids_ref[:, children:]
        slot_ref[half:] = mate_ref[:, children:] + past_half

    shapes = [(3 * queries, 128), (queries + 8, 128), (queries, children), (queries, lanes), (half, children)]
    return pl.pallas_call(
        kernel,
        out_shape=[jax.ShapeDtypeStruct(shape, jnp.int32) for shape in shapes],
        in_specs=[SMEM, VMEM, VMEM],
        out_specs=[VMEM] * len(shapes),
        name="plan_rows",
    )(here, ids, near_by(mate_ids))


def gather_slabs(asked, here, table, shifts, capacity, stride, past_half, peers, al_n):
    width = table.shape[1]
    slab = 2 * capacity
    unroll = unroll_of(capacity)
    per = capacity // unroll

    def kernel(here_ref, asked_ref, table_ref, *rest):
        outs, wide, spare = rest[:-2], rest[-2], rest[-1]
        widen(table_ref, wide, table_ref.shape[0])
        if past_half:
            pasts, outs = outs[0], outs[1:]

            def past(d, c):
                at = d * stride + capacity
                rows = [wide[pl.ds(asked_ref[at + i], 1), :] for i in range(past_half)]
                mate = d + al_n * (1 - 2 * lax.rem(lax.div(d, al_n), 2))
                for i, row in enumerate(rows):
                    spare[pl.ds(d * 2 * past_half + i, 1), :] = row
                for i, row in enumerate(rows):
                    spare[pl.ds((mate * 2 + 1) * past_half + i, 1), :] = row
                return c

            lax.fori_loop(0, peers, past, 0)
            narrow(spare, pasts, peers * 2 * past_half)
        near = peers // 2
        at, side = here_ref[0], here_ref[1]
        for out, shift in zip(outs, shifts):
            target = (at ^ shift) if near & (near - 1) == 0 else lax.rem(at + shift, near)
            row = lax.div(target, al_n) * (2 * al_n) + lax.rem(target, al_n)
            own, mate = (row + side * al_n) * stride, (row + (1 - side) * al_n) * stride

            def child(t, c, own=own, mate=mate):
                at = jnp.where(t < per, own, mate - per * unroll) + t * unroll
                rows = [wide[pl.ds(asked_ref[at + i], 1), :] for i in range(unroll)]
                for i, row in enumerate(rows):
                    spare[pl.ds(t * unroll + i, 1), :] = row
                return c

            lax.fori_loop(0, 2 * per, child, 0)
            narrow(spare, out, slab)

    shapes = [jax.ShapeDtypeStruct((slab, width), jnp.bfloat16)] * len(shifts)
    spare_rows = slab
    if past_half:
        shapes = [jax.ShapeDtypeStruct((peers * 2 * past_half, width), jnp.bfloat16)] + shapes
        spare_rows = max(slab, peers * 2 * past_half)
    return pl.pallas_call(
        kernel,
        out_shape=shapes,
        in_specs=[SMEM, SMEM, VMEM],
        out_specs=[VMEM] * len(shapes),
        scratch_shapes=[
            pltpu.VMEM(table.shape, jnp.float32),
            pltpu.VMEM((spare_rows, width), jnp.float32),
        ],
        name="gather_past" if past_half else "gather_slabs",
    )(here, asked, table)


def arrange_past(slots, fetched, queries, history, lanes):
    rows, width = fetched.shape

    def kernel(slot_ref, in_ref, out_ref, wide, spare):
        widen(in_ref, wide, rows)
        spare[...] = jnp.zeros(spare.shape, jnp.float32)

        def one(q, c):
            for lo in range(0, history, 35):
                part = range(lo, min(lo + 35, history))
                vals = [wide[pl.ds(slot_ref[q, h], 1), :] for h in part]
                for h, val in zip(part, vals):
                    spare[pl.ds(h, 1), :] = val
            out_ref[pl.ds(pl.multiple_of(q * lanes, lanes), lanes), :] = spare[...].astype(jnp.bfloat16)
            return c

        lax.fori_loop(0, queries, one, 0)

    return pl.pallas_call(
        kernel,
        out_shape=jax.ShapeDtypeStruct((queries * lanes, width), fetched.dtype),
        in_specs=[SMEM, VMEM],
        out_specs=VMEM,
        scratch_shapes=[pltpu.VMEM((rows, width), jnp.float32), pltpu.VMEM((lanes, width), jnp.float32)],
        name="arrange_past",
    )(slots, near_by(fetched))


def score_rows(segments, bases, rel, slabs, past, w_first, b_first, w_second, b_second, w_out, history, lanes):
    queries, children = rel.shape
    slab, width = slabs[0].shape
    parts = len(slabs)
    hidden = w_second.shape[0]
    batch = min(parts, 16)
    longest = rounded(queries * children + queries * 8, BLOCK)
    per_block = BLOCK // 128
    quick = 3
    group = 16
    half = queries // 2

    def kernel(seg_ref, base_ref, rel_ref, past_ref, w1, b1, w2, b2, wo, *rest):
        slab_refs, out_refs = rest[:parts], rest[parts : parts + 2]
        wide, rows, pool, line, g0, g1, g2 = rest[parts + 2 :]
        for i, ref in enumerate(slab_refs):
            widen(ref, wide, slab, at=i * slab)
        spots = [lax.broadcasted_iota(jnp.int32, (8, width), 0) + 8 * i for i in range(quick)]

        def segment(q, c):
            for x in range(0, parts, batch):
                src, dst, count = ([seg_ref[n * queries + q, x + i] for i in range(batch)] for n in range(3))
                chunks = [[wide[pl.ds(s + 8 * i, 8), :] for i in range(quick)] for s in src]
                for d, n, chunk in zip(dst, count, chunks):
                    for i, part in enumerate(chunk):
                        pltpu.store(rows.at[pl.ds(d + 8 * i, 8), :], part, mask=spots[i] < n)
                most = count[0]
                for n in count[1:]:
                    most = jnp.maximum(most, n)

                @pl.when(most > 8 * quick)
                def _(src=src, dst=dst, count=count):
                    for s, d, n in zip(src, dst, count):

                        def more(i, c, s=s, d=d, n=n):
                            pltpu.store(
                                rows.at[pl.ds(d + 8 * i, 8), :], wide[pl.ds(s + 8 * i, 8), :], mask=spots[0] < n - 8 * i
                            )
                            return c

                        lax.fori_loop(quick, (n + 7) >> 3, more, 0)

            return c

        lax.fori_loop(0, queries, segment, 0)

        def attend(g, c):
            for i in range(group):
                q = g * group + i
                base = pl.multiple_of(base_ref[q, 0], 8)
                kids = rows[pl.ds(base, children), :].astype(jnp.bfloat16)
                own = past_ref[pl.ds(pl.multiple_of(q * lanes, lanes), lanes), :]
                logits = lax.dot_general(kids, own, (((1,), (1,)), ((), ())), preferred_element_type=jnp.float32)
                logits = logits * width ** (-0.5)
                share = (jax.nn.sigmoid(logits) * history ** (-0.5)).astype(jnp.bfloat16)
                pool[pl.ds(base, children), :] = jnp.dot(share, own, preferred_element_type=jnp.float32)
            return c

        lax.fori_loop(0, queries // group, attend, 0)

        last = jnp.broadcast_to(wo[...], (8, hidden))

        def dense(b, c):
            at = pl.multiple_of(b * BLOCK, BLOCK)
            kids = rows[pl.ds(at, BLOCK), :].astype(jnp.bfloat16)
            pooled = pool[pl.ds(at, BLOCK), :].astype(jnp.bfloat16)
            joined = jnp.concatenate([kids, pooled], axis=1)
            first = jnp.dot(joined, w1[...], preferred_element_type=jnp.float32) + b1[...]
            first = jnp.maximum(first, 0.0).astype(jnp.bfloat16)
            second = jnp.dot(first, w2[...], preferred_element_type=jnp.float32) + b2[...]
            second = jnp.maximum(second, 0.0).astype(jnp.bfloat16)
            out = lax.dot_general(last, second, (((1,), (1,)), ((), ())), preferred_element_type=jnp.float32)
            for i in range(per_block):
                line[pl.ds(b * per_block + i, 1), :] = out[0:1, i * 128 : (i + 1) * 128]
            return c

        lax.fori_loop(0, (base_ref[queries, 0] + BLOCK - 1) // BLOCK, dense, 0)
        for q in range(queries):
            at = base_ref[q, 0] // 128
            for i, ref in enumerate((g0, g1, g2)):
                ref[q : q + 1, :] = line[pl.ds(at + i, 1), :]
        for q in range(0, queries, 8):
            for k in range(0, children, 128):
                spot = rel_ref[q : q + 8, k : k + 128]
                lane = spot & 127
                took = [jnp.take_along_axis(ref[q : q + 8, :], lane, axis=1) for ref in (g0, g1, g2)]
                out_ref, at = out_refs[q // half], q % half
                out_ref[at : at + 8, k : k + 128] = jnp.where(
                    spot < 128, took[0], jnp.where(spot < 256, took[1], took[2])
                )

    wide_rows = parts * slab + 8 * quick
    return pl.pallas_call(
        kernel,
        out_shape=[jax.ShapeDtypeStruct((half, children), jnp.float32)] * 2,
        in_specs=[SMEM, SMEM] + [VMEM] * (7 + parts),
        out_specs=[VMEM] * 2,
        scratch_shapes=[
            pltpu.VMEM((wide_rows, width), jnp.float32),
            pltpu.VMEM((longest + children, width), jnp.float32),
            pltpu.VMEM((longest + children, width), jnp.float32),
            pltpu.VMEM((rounded(longest // 128 + 3, 8), 128), jnp.float32),
        ]
        + [pltpu.VMEM((queries, 128), jnp.float32)] * 3,
        name="score_rows",
    )(
        segments,
        bases,
        rel,
        past,
        w_first,
        b_first.reshape(1, hidden),
        w_second,
        b_second.reshape(1, hidden),
        w_out,
        *slabs,
    )


def body(child_ids, history_ids, node_table, w_first, b_first, w_second, b_second, w_out):
    queries, children = child_ids.shape
    history = history_ids.shape[1]
    shard_rows, width = node_table.shape
    pb_n, al_n = lax.axis_size("pb"), lax.axis_size("al")
    peers, near = 2 * pb_n * al_n, pb_n * al_n
    pb, ah, al = (lax.axis_index(a) for a in AXES)
    place = jnp.stack([pb * al_n + al, ah])
    capacity = 5 * queries * children // (2 * peers)
    past_cap = (queries * history + peers - 1) // peers
    past_half = rounded(past_cap, 4)
    stride = rounded(capacity + past_half, 128)
    power = near & (near - 1) == 0

    wanted, ids = build_lists(child_ids, history_ids, shard_rows, peers, capacity, past_half, stride)
    asked = lax.all_to_all(wanted, AXES, split_axis=0, concat_axis=0, tiled=True)
    asked = asked.reshape(peers * stride)

    swap = [(0, 1), (1, 0)]
    mate_ids = lax.ppermute(ids, "ah", swap)
    segments, bases, rel, past_slot, mine = plan_rows(
        place, ids, mate_ids, shard_rows, children, al_n, near, capacity, past_half
    )

    pairs = [(i, (i ^ s) if power else (i + s) % near) for s in range(near) for i in range(near)]
    steps = sorted(range(1, near), key=lambda s: (-bin(s).count("1"), -s))
    cuts = [0, 1 * near // 16, 5 * near // 16, 10 * near // 16, near - 1]
    waves = [steps[a:b] for a, b in zip(cuts, cuts[1:])]
    waves[-1] = waves[-1] + [0]
    slabs = [None] * near
    for number, wave in enumerate(waves):
        outs = gather_slabs(
            asked, place, node_table, wave, capacity, stride, past_half if number == 0 else 0, peers, al_n
        )
        if number == 0:
            past_out, outs = outs[0], outs[1:]
            past_in = lax.all_to_all(
                past_out.reshape(peers, 2 * past_half, width), AXES, split_axis=0, concat_axis=0, tiled=True
            ).reshape(peers * 2 * past_half, width)
        for shift, out in zip(wave, outs):
            slabs[shift] = lax.ppermute(out, HALF, pairs[shift * near : (shift + 1) * near]) if shift else out

    lanes = rounded(history, 128)
    past = arrange_past(past_slot, past_in, 2 * queries, history, lanes)
    own, lent = score_rows(segments, bases, rel, slabs, past, w_first, b_first, w_second, b_second, w_out.reshape(1, -1), history, lanes)
    back = lax.ppermute(lent, "ah", swap)
    return jnp.where(mine > 0, own, back)


def solution(mesh):
    pb_n, an_n = mesh.shape["pb"], mesh.shape["an"]
    fine = Mesh(mesh.devices.reshape(pb_n, 2, an_n // 2), AXES)
    rows = P(AXES, None)
    return jax.shard_map(
        body, mesh=fine, in_specs=(rows, rows, rows, P(), P(), P(), P(), P()), out_specs=rows, check_vma=False
    )
```

time: 120 us -> 107 us (0.89)
  local copies, waits for them, and re-layouts: 7.65 us -> 1.83 us
  other arithmetic: 6.42 us -> 1.91 us
  matrix products: 2.67 us -> 0 us
  starting transfers between devices: 32 us -> 30.2 us
  waiting for transfers between devices: 20.1 us -> 21.6 us
    pallas_call x0 -> x2, Pallas kernels: none -> 6.69 us  [the longest x1 4.61 us: build_lists(): pl.pallas_call(kernel, out_shape=[jax.ShapeDtypeStruct((peers, 1, stride)...]
    ppermute x15, waiting for transfers between devices: 11.5 us -> 5.71 us  [body(): lax.ppermute(out, HALF, pairs[shift * near:(shift + 1) * near])]
    ppermute x1, waiting for transfers between devices: 0.01 us -> 4.45 us  [body(): mate_ids = lax.ppermute(ids, 'ah', swap)]
    pallas_call x1, Pallas kernels: 19.9 us -> 15.8 us  [score_rows(): pl.pallas_call(kernel, out_shape=[jax.ShapeDtypeStruct((half, children),...]
    all_to_all x1, waiting for transfers between devices: 3.63 us -> 6.64 us  [body(): lax.all_to_all(wanted, AXES, split_axis=0, concat_axis=0, tiled=True)]
    dot_general x5 -> x0, matrix products: 2.67 us -> none  [the longest x2 1.85 us: place(): jnp.einsum('io,is->os', jnp.concatenate([high, low], axis=1), spot, prefe...]
    reshape x4 -> x1, local copies, waits for them, and re-layouts: 2.86 us -> 0.59 us  [body(): w_out.reshape(1, -1)]
    pallas_call x4, Pallas kernels: 25.6 us -> 23.5 us  [gather_slabs(): pl.pallas_call(kernel, out_shape=shapes, in_specs=[SMEM, SMEM, VMEM], out...]
  transfers between devices with their start and end apart: 19 -> 19, of which waited for: 9 -> 6; matrix products, arithmetic and copies ran while one was open for 5% -> 1% of each run, Pallas kernels for 25% -> 23%
where the time goes in v4:
time: 107 us; the launch traced here: 106 us
  Pallas kernels  50.4 us (47%)
  starting transfers between devices  30.2 us (28%)
  waiting for transfers between devices  21.6 us (20%)
  other arithmetic  1.91 us (2%)
  local copies, waits for them, and re-layouts  1.83 us (2%)
    pallas_call x4, Pallas kernels, gather_slabs(): pl.pallas_call(kernel, out_shape=shapes, in_specs=[SMEM, SMEM, VMEM], out...  23.5 us
    ppermute x15, starting transfers between devices, body(): lax.ppermute(out, HALF, pairs[shift * near:(shift + 1) * near])  17.5 us
    pallas_call x1, Pallas kernels, score_rows(): pl.pallas_call(kernel, out_shape=[jax.ShapeDtypeStruct((half, children),...  15.8 us
    all_to_all x1, starting transfers between devices, body(): lax.all_to_all(wanted, AXES, split_axis=0, concat_axis=0, tiled=True)  7.32 us
    all_to_all x1, waiting for transfers between devices, body(): lax.all_to_all(wanted, AXES, split_axis=0, concat_axis=0, tiled=True)  6.64 us
    ppermute x15, waiting for transfers between devices, body(): lax.ppermute(out, HALF, pairs[shift * near:(shift + 1) * near])  5.71 us
    ppermute x1, waiting for transfers between devices, body(): back = lax.ppermute(lent, 'ah', swap)  4.84 us
    pallas_call x1, Pallas kernels, build_lists(): pl.pallas_call(kernel, out_shape=[jax.ShapeDtypeStruct((peers, 1, stride)...  4.61 us
  transfers between devices with their start and end apart: 19, of which 6 were waited for; matrix products, arithmetic and copies ran while one was open for 1% of the time, Pallas kernels for 23%

profile of v4, /device:TPU:0, one launch (start us, length us, event | category | flops | bytes accessed | tf_op | source)
XLA Modules:
  0.0 106.3 jit_solution(1606090772321073594)
XLA Ops:
  0.0 4.6 %build_lists.1 = (s32[32,1,384]{2,1,0:T(1,128)}, s32[16,384]{1,0:T(8,128)}) custom-call(s32[16,256]{1,0:T(8,128)} %kid_ref.1, s32[16,69]{1,0:T(8,128)} %past_ref.1), custom_call_target="tpu_custom_call" | custom-call | tf_op jit(solution)/shard_map/build_lists/pallas_call | solution.py:136
  4.6 7.3 %all-to-all-start = ((s32[32,1,384]{2,1,0:T(1,128)}), s32[32,1,384]{2,1,0:T(1,128)S(1)}, u32[]{:S(2)}, u32[]{:S(2)}) async-start(s32[32,1,384]{2,1,0:T(1,128)} %get-tuple-element.37), calls=%async_computation | async-start | bytes 98304 | tf_op jit(solution)/shard_map/all_to_all | solution.py:423
  11.9 0.6 pad_add_fusion.here_ref
  12.5 6.6 %all-to-all-done = s32[32,1,384]{2,1,0:T(1,128)S(1)} async-done(((s32[32,1,384]{2,1,0:T(1,128)}), s32[32,1,384]{2,1,0:T(1,128)S(1)}, u32[]{:S(2)}, u32[]{:S(2)}) %all-to-all-start) | async-done | bytes 49184 | tf_op jit(solution)/shard_map/all_to_all | solution.py:423
  19.2 0.6 copy-done
  19.8 5.3 %gather_past.1 = (bf16[2304,128]{1,0:T(8,128)(2,1)}, bf16[640,128]{1,0:T(8,128)(2,1)}) custom-call(s32[2]{0:T(128)} %pad_add_fusion.here_ref, s32[12288]{0:T(1024)} %bitcast.8, bf16[8192,128]{1,0:T(8,128)(2,1)} %table_ref.7), custom_call_target="tpu_custom_call" | custom-call | tf_op jit(solution)/shard_map/gather_past/pallas_call | solution.py:248
  25.1 2.6 %all-to-all-start.1 = ((bf16[32,72,128]{2,1,0:T(8,128)(2,1)}), bf16[32,72,128]{2,1,0:T(8,128)(2,1)S(1)}, u32[]{:S(2)}, u32[]{:S(2)}) async-start(bf16[32,72,128]{2,1,0:T(8,128)(2,1)} %bitcast.12), calls=%async_computation.1 | async-start | bytes 1179648 | tf_op jit(solution)/shard_map/all_to_all | solution.py:444
  27.7 2.7 %collective-permute-start = (s32[16,384]{1,0:T(8,128)S(1)}, s32[16,384]{1,0:T(8,128)S(1)}, u32[]{:S(2)}, u32[]{:S(2)}) collective-permute-start(s32[16,384]{1,0:T(8,128)S(1)} %copy-done.16), channel_id=1, source_target_pairs={{0,4},{4,0},{1,5},{5,1},{2,6},{6,2},{3,7},{7,3},{8,12},{12,8},{9,1... | collective-permute-start | bytes 73736 | tf_op jit(solution)/shard_map/ppermute | solution.py:427
  30.4 6.7 %gather_slabs.3 = (bf16[640,128]{1,0:T(8,128)(2,1)}, bf16[640,128]{1,0:T(8,128)(2,1)}, bf16[640,128]{1,0:T(8,128)(2,1)}, bf16[640,128]{1,0:T(8,128)(2,1)}, bf16[...) custom-call(s32[2]{0:T(128)} %pad_add_fusion.here_ref, s32[12288]{0:T(1024)} %bitcast.9, bf16[8192,128]{1,0:T(8,128)(2,1)} %table_ref.7), custom_call_target="tpu_custom_call" | custom-call | tf_op jit(solution)/shard_map/gather_slabs/pallas_call | solution.py:248
  37.1 1.5 %collective-permute-start.1 = (bf16[640,128]{1,0:T(8,128)(2,1)}, bf16[640,128]{1,0:T(8,128)(2,1)S(1)}, u32[]{:S(2)}, u32[]{:S(2)}) collective-permute-start(bf16[640,128]{1,0:T(8,128)(2,1)} %get-tuple-element.40), channel_id=1, source_target_pairs={{0,1},{1,0},{2,3},{3,2},{8,9},{9,8},{10,11},{11,10},{16,17},{17,16... | collective-permute-start | bytes 491528 | tf_op jit(solution)/shard_map/ppermute | solution.py:448
  38.6 1.5 %collective-permute-start.2 = (bf16[640,128]{1,0:T(8,128)(2,1)}, bf16[640,128]{1,0:T(8,128)(2,1)S(1)}, u32[]{:S(2)}, u32[]{:S(2)}) collective-permute-start(bf16[640,128]{1,0:T(8,128)(2,1)} %get-tuple-element.41), channel_id=1, source_target_pairs={{0,2},{1,3},{2,0},{3,1},{8,10},{9,11},{10,8},{11,9},{16,18},{17,19... | collective-permute-start | bytes 491528 | tf_op jit(solution)/shard_map/ppermute | solution.py:448
  40.2 0.5 collective-permute-start.3
  40.6 0.0 collective-permute-start.4
  40.6 4.5 %collective-permute-done.mate_ref = s32[16,384]{1,0:T(8,128)S(1)} collective-permute-done((s32[16,384]{1,0:T(8,128)S(1)}, s32[16,384]{1,0:T(8,128)S(1)}, u32[]{:S(2)}, u32[]{:S(2)}) %collective-permute-start) | collective-permute-done | bytes 24608 | tf_op jit(solution)/shard_map/ppermute | solution.py:427
  45.1 1.5 %collective-permute-start.8 = (bf16[640,128]{1,0:T(8,128)(2,1)}, bf16[640,128]{1,0:T(8,128)(2,1)S(1)}, u32[]{:S(2)}, u32[]{:S(2)}) collective-permute-start(bf16[640,128]{1,0:T(8,128)(2,1)} %get-tuple-element.47), channel_id=1, source_target_pairs={{0,16},{1,17},{2,18},{3,19},{8,24},{9,25},{10,26},{11,27},{16,0},{... | collective-permute-start | bytes 491528 | tf_op jit(solution)/shard_map/ppermute | solution.py:448
  46.6 6.1 %gather_slabs.4 = (bf16[640,128]{1,0:T(8,128)(2,1)}, bf16[640,128]{1,0:T(8,128)(2,1)}, bf16[640,128]{1,0:T(8,128)(2,1)}, bf16[640,128]{1,0:T(8,128)(2,1)}, bf16[640,128]{1,0:T(8,128)(2,1)}) custom-call(s32[2]{0:T(128)} %pad_add_fusion.here_ref, s32[12288]{0:T(1024)} %bitcast.10, bf16[8192,128]{1,0:T(8,128)(2,1)} %table_ref.7), custom_call_target="tpu_custom_call" | custom-call | tf_op jit(solution)/shard_map/gather_slabs/pallas_call | solution.py:248
  52.7 0.0 collective-permute-done.1.rest_1_
  52.7 0.1 collective-permute-start.10
  52.8 0.1 collective-permute-start.12
  52.9 0.0 collective-permute-done.3.rest_3_
  52.9 1.7 %collective-permute-start.5 = (bf16[640,128]{1,0:T(8,128)(2,1)}, bf16[640,128]{1,0:T(8,128)(2,1)S(1)}, u32[]{:S(2)}, u32[]{:S(2)}) collective-permute-start(bf16[640,128]{1,0:T(8,128)(2,1)} %get-tuple-element.44), channel_id=1, source_target_pairs={{0,9},{1,8},{2,11},{3,10},{8,1},{9,0},{10,3},{11,2},{16,25},{17,24... | collective-permute-start | bytes 491528 | tf_op jit(solution)/shard_map/ppermute | solution.py:448
  54.6 1.5 %collective-permute-start.6 = (bf16[640,128]{1,0:T(8,128)(2,1)}, bf16[640,128]{1,0:T(8,128)(2,1)S(1)}, u32[]{:S(2)}, u32[]{:S(2)}) collective-permute-start(bf16[640,128]{1,0:T(8,128)(2,1)} %get-tuple-element.45), channel_id=1, source_target_pairs={{0,10},{1,11},{2,8},{3,9},{8,2},{9,3},{10,0},{11,1},{16,26},{17,27... | collective-permute-start | bytes 491528 | tf_op jit(solution)/shard_map/ppermute | solution.py:448
  56.1 1.5 %collective-permute-start.9 = (bf16[640,128]{1,0:T(8,128)(2,1)}, bf16[640,128]{1,0:T(8,128)(2,1)S(1)}, u32[]{:S(2)}, u32[]{:S(2)}) collective-permute-start(bf16[640,128]{1,0:T(8,128)(2,1)} %get-tuple-element.48), channel_id=1, source_target_pairs={{0,17},{1,16},{2,19},{3,18},{8,25},{9,24},{10,27},{11,26},{16,1},{... | collective-permute-start | bytes 491528 | tf_op jit(solution)/shard_map/ppermute | solution.py:448
  57.5 5.4 %gather_slabs.5 = (bf16[640,128]{1,0:T(8,128)(2,1)}, bf16[640,128]{1,0:T(8,128)(2,1)}, bf16[640,128]{1,0:T(8,128)(2,1)}, bf16[640,128]{1,0:T(8,128)(2,1)}) custom-call(s32[2]{0:T(128)} %pad_add_fusion.here_ref, s32[12288]{0:T(1024)} %bitcast.11, bf16[8192,128]{1,0:T(8,128)(2,1)} %table_ref.7), custom_call_target="tpu_custom_call" | custom-call | tf_op jit(solution)/shard_map/gather_slabs/pallas_call | solution.py:248
  62.9 2.4 %collective-permute-start.11 = (bf16[640,128]{1,0:T(8,128)(2,1)}, bf16[640,128]{1,0:T(8,128)(2,1)S(1)}, u32[]{:S(2)}, u32[]{:S(2)}) collective-permute-start(bf16[640,128]{1,0:T(8,128)(2,1)} %get-tuple-element.50), channel_id=1, source_target_pairs={{0,19},{1,18},{2,17},{3,16},{8,27},{9,26},{10,25},{11,24},{16,3},{... | collective-permute-start | bytes 491528 | tf_op jit(solution)/shard_map/ppermute | solution.py:448
  65.4 0.6 collective-permute-done.12.rest_12_
  66.0 1.2 %collective-permute-start.13 = (bf16[640,128]{1,0:T(8,128)(2,1)}, bf16[640,128]{1,0:T(8,128)(2,1)S(1)}, u32[]{:S(2)}, u32[]{:S(2)}) collective-permute-start(bf16[640,128]{1,0:T(8,128)(2,1)} %get-tuple-element.52), channel_id=1, source_target_pairs={{0,25},{1,24},{2,27},{3,26},{8,17},{9,16},{10,19},{11,18},{16,9},{... | collective-permute-start | bytes 491528 | tf_op jit(solution)/shard_map/ppermute | solution.py:448
  67.2 0.0 collective-permute-done.5.rest_5_
  67.2 0.8 collective-permute-start.14
  68.1 1.5 %collective-permute-start.7 = (bf16[640,128]{1,0:T(8,128)(2,1)}, bf16[640,128]{1,0:T(8,128)(2,1)S(1)}, u32[]{:S(2)}, u32[]{:S(2)}) collective-permute-start(bf16[640,128]{1,0:T(8,128)(2,1)} %get-tuple-element.46), channel_id=1, source_target_pairs={{0,11},{1,10},{2,9},{3,8},{8,3},{9,2},{10,1},{11,0},{16,27},{17,26... | collective-permute-start | bytes 491528 | tf_op jit(solution)/shard_map/ppermute | solution.py:448
  69.5 0.0 collective-permute-done.9.rest_9_
  69.5 1.8 %collective-permute-start.15 = (bf16[640,128]{1,0:T(8,128)(2,1)S(1)}, bf16[640,128]{1,0:T(8,128)(2,1)S(1)}, u32[]{:S(2)}, u32[]{:S(2)}) collective-permute-start(bf16[640,128]{1,0:T(8,128)(2,1)S(1)} %copy-done.19), channel_id=1, source_target_pairs={{0,27},{1,26},{2,25},{3,24},{8,19},{9,18},{10,17},{11,16},{16,11},... | collective-permute-start | bytes 491528 | tf_op jit(solution)/shard_map/ppermute | solution.py:448
  71.4 0.6 reshape.23.wo
  72.0 2.1 %plan_rows.1 = (s32[96,128]{1,0:T(8,128)}, s32[40,128]{1,0:T(8,128)}, s32[32,256]{1,0:T(8,128)}, s32[32,128]{1,0:T(8,128)}, s32[16,256]{1,0:T(8,128)}) custom-call(s32[2]{0:T(128)} %pad_add_fusion.here_ref, s32[16,384]{1,0:T(8,128)} %get-tuple-element.31.ids_ref, s32[16,384]{1,0:T(8,128)S(1)} %collective-permute-done.mate_ref), custom_call_target="tpu_custom_call" | custom-call | tf_op jit(solution)/shard_map/plan_rows/pallas_call | solution.py:193
  74.0 4.4 %arrange_past.1.past_ref = bf16[4096,128]{1,0:T(8,128)(2,1)} custom-call(s32[32,128]{1,0:T(8,128)} %get-tuple-element.36.slot_ref, bf16[2304,128]{1,0:T(8,128)(2,1)S(1)} %bitcast.7), custom_call_target="tpu_custom_call" | custom-call | tf_op jit(solution)/shard_map/arrange_past/pallas_call | solution.py:279
  78.5 0.0 collective-permute-done.11.rest_11_
  78.5 4.6 %collective-permute-done.13.rest_13_ = bf16[640,128]{1,0:T(8,128)(2,1)S(1)} collective-permute-done((bf16[640,128]{1,0:T(8,128)(2,1)}, bf16[640,128]{1,0:T(8,128)(2,1)S(1)}, u32[]{:S(2)}, u32[]{:S(2)}) %collective-permute-start.13) | collective-permute-done | bytes 163872 | tf_op jit(solution)/shard_map/ppermute | solution.py:448
  83.1 0.0 collective-permute-done.14.rest_14_
  83.1 0.0 collective-permute-done.7.rest_7_
  83.1 0.4 collective-permute-done.15.rest_15_
  83.7 0.1 copy-done.12
  83.7 0.1 copy-done.13
  83.8 0.0 copy-done.14
  83.9 0.3 copy-done.15
  84.2 15.8 %score_rows.1 = (f32[16,256]{1,0:T(8,128)}, f32[16,256]{1,0:T(8,128)}) custom-call(s32[96,128]{1,0:T(8,128)} %get-tuple-element.33.seg_ref, s32[40,128]{1,0:T(8,128)} %get-tuple-element.34.base_ref, s32[32,256]{1,0:T(8,128)} %get-tuple-element.35.rel_ref, bf16[4096,128]{1,0:T(8,128)(2,1)} %arrange_past.1.past_ref, bf16[256,512]{1,0:T(8,128)(2,1)} %w1.1, ...), custom_call_target="tpu_custom_call" | custom-call | tf_op jit(solution)/shard_map/score_rows/pallas_call | solution.py:381
  100.0 0.1 collective-permute-start.16
  100.1 4.8 %collective-permute-done.16 = f32[16,256]{1,0:T(8,128)S(1)} collective-permute-done((f32[16,256]{1,0:T(8,128)}, f32[16,256]{1,0:T(8,128)S(1)}, u32[]{:S(2)}, u32[]{:S(2)}) %collective-permute-start.16) | collective-permute-done | bytes 16416 | tf_op jit(solution)/shard_map/ppermute | solution.py:453
  104.9 1.3 %compare_select_fusion = f32[16,256]{1,0:T(8,128)} fusion(f32[16,256]{1,0:T(8,128)} %get-tuple-element.55, f32[16,256]{1,0:T(8,128)S(1)} %collective-permute-done.16, s32[16,256]{1,0:T(8,128)S(1)} %copy-done.17), kind=kLoop, calls=%fused_computation | loop fusion | flops 8192 | bytes 65536 | tf_op jit(solution)/shard_map/jit(_where)/select_n | solution.py:454
  (41 shorter events, 0.1 us)
Async XLA Ops:
  4.6 23.1 %copy-start.16 = (s32[16,384]{1,0:T(8,128)S(1)}, s32[16,384]{1,0:T(8,128)}, u32[]{:S(2)}) copy-start(s32[16,384]{1,0:T(8,128)} %get-tuple-element.31.ids_ref) | copy-start | bytes 73732
  4.6 14.6 %all-to-all-start = ((s32[32,1,384]{2,1,0:T(1,128)}), s32[32,1,384]{2,1,0:T(1,128)S(1)}, u32[]{:S(2)}, u32[]{:S(2)}) async-start(s32[32,1,384]{2,1,0:T(1,128)} %get-tuple-element.37), calls=%async_computation | async-start | bytes 98304 | tf_op jit(solution)/shard_map/all_to_all | solution.py:423
  19.2 0.6 copy-start
  25.1 49.0 %all-to-all-start.1 = ((bf16[32,72,128]{2,1,0:T(8,128)(2,1)}), bf16[32,72,128]{2,1,0:T(8,128)(2,1)S(1)}, u32[]{:S(2)}, u32[]{:S(2)}) async-start(bf16[32,72,128]{2,1,0:T(8,128)(2,1)} %bitcast.12), calls=%async_computation.1 | async-start | bytes 1179648 | tf_op jit(solution)/shard_map/all_to_all | solution.py:444
  27.7 17.4 %collective-permute-start = (s32[16,384]{1,0:T(8,128)S(1)}, s32[16,384]{1,0:T(8,128)S(1)}, u32[]{:S(2)}, u32[]{:S(2)}) collective-permute-start(s32[16,384]{1,0:T(8,128)S(1)} %copy-done.16), channel_id=1, source_target_pairs={{0,4},{4,0},{1,5},{5,1},{2,6},{6,2},{3,7},{7,3},{8,12},{12,8},{9,1... | collective-permute-start | bytes 73736 | tf_op jit(solution)/shard_map/ppermute | solution.py:427
  37.1 15.5 %collective-permute-start.1 = (bf16[640,128]{1,0:T(8,128)(2,1)}, bf16[640,128]{1,0:T(8,128)(2,1)S(1)}, u32[]{:S(2)}, u32[]{:S(2)}) collective-permute-start(bf16[640,128]{1,0:T(8,128)(2,1)} %get-tuple-element.40), channel_id=1, source_target_pairs={{0,1},{1,0},{2,3},{3,2},{8,9},{9,8},{10,11},{11,10},{16,17},{17,16... | collective-permute-start | bytes 491528 | tf_op jit(solution)/shard_map/ppermute | solution.py:448
  38.6 14.1 %collective-permute-start.2 = (bf16[640,128]{1,0:T(8,128)(2,1)}, bf16[640,128]{1,0:T(8,128)(2,1)S(1)}, u32[]{:S(2)}, u32[]{:S(2)}) collective-permute-start(bf16[640,128]{1,0:T(8,128)(2,1)} %get-tuple-element.41), channel_id=1, source_target_pairs={{0,2},{1,3},{2,0},{3,1},{8,10},{9,11},{10,8},{11,9},{16,18},{17,19... | collective-permute-start | bytes 491528 | tf_op jit(solution)/shard_map/ppermute | solution.py:448
  40.2 12.7 %collective-permute-start.3 = (bf16[640,128]{1,0:T(8,128)(2,1)}, bf16[640,128]{1,0:T(8,128)(2,1)S(1)}, u32[]{:S(2)}, u32[]{:S(2)}) collective-permute-start(bf16[640,128]{1,0:T(8,128)(2,1)} %get-tuple-element.42), channel_id=1, source_target_pairs={{0,3},{1,2},{2,1},{3,0},{8,11},{9,10},{10,9},{11,8},{16,19},{17,18... | collective-permute-start | bytes 491528 | tf_op jit(solution)/shard_map/ppermute | solution.py:448
  40.6 14.0 %collective-permute-start.4 = (bf16[640,128]{1,0:T(8,128)(2,1)}, bf16[640,128]{1,0:T(8,128)(2,1)S(1)}, u32[]{:S(2)}, u32[]{:S(2)}) collective-permute-start(bf16[640,128]{1,0:T(8,128)(2,1)} %get-tuple-element.43), channel_id=1, source_target_pairs={{0,8},{1,9},{2,10},{3,11},{8,0},{9,1},{10,2},{11,3},{16,24},{17,25... | collective-permute-start | bytes 491528 | tf_op jit(solution)/shard_map/ppermute | solution.py:448
  45.1 24.5 %copy-start.19 = (bf16[640,128]{1,0:T(8,128)(2,1)S(1)}, bf16[640,128]{1,0:T(8,128)(2,1)}, u32[]{:S(2)}) copy-start(bf16[640,128]{1,0:T(8,128)(2,1)} %get-tuple-element.54) | copy-start | bytes 491524
  45.1 26.3 %copy-start.18 = (bf16[512]{0:T(512)(128)(2,1)S(1)}, bf16[512]{0:T(512)(128)(2,1)}, u32[]{:S(2)}) copy-start(bf16[512]{0:T(512)(128)(2,1)} %param.15) | copy-start | bytes 3076
  45.1 11.0 %collective-permute-start.8 = (bf16[640,128]{1,0:T(8,128)(2,1)}, bf16[640,128]{1,0:T(8,128)(2,1)S(1)}, u32[]{:S(2)}, u32[]{:S(2)}) collective-permute-start(bf16[640,128]{1,0:T(8,128)(2,1)} %get-tuple-element.47), channel_id=1, source_target_pairs={{0,16},{1,17},{2,18},{3,19},{8,24},{9,25},{10,26},{11,27},{16,0},{... | collective-permute-start | bytes 491528 | tf_op jit(solution)/shard_map/ppermute | solution.py:448
  52.7 30.9 %copy-start.1 = (bf16[640,128]{1,0:T(8,128)(2,1)}, bf16[640,128]{1,0:T(8,128)(2,1)S(1)}, u32[]{:S(2)}) copy-start(bf16[640,128]{1,0:T(8,128)(2,1)S(1)} %collective-permute-done.1.rest_1_) | copy-start | bytes 491524
  52.7 10.3 %collective-permute-start.10 = (bf16[640,128]{1,0:T(8,128)(2,1)}, bf16[640,128]{1,0:T(8,128)(2,1)S(1)}, u32[]{:S(2)}, u32[]{:S(2)}) collective-permute-start(bf16[640,128]{1,0:T(8,128)(2,1)} %get-tuple-element.49), channel_id=1, source_target_pairs={{0,18},{1,19},{2,16},{3,17},{8,26},{9,27},{10,24},{11,25},{16,2},{... | collective-permute-start | bytes 491528 | tf_op jit(solution)/shard_map/ppermute | solution.py:448
  52.8 30.8 %copy-start.2 = (bf16[640,128]{1,0:T(8,128)(2,1)}, bf16[640,128]{1,0:T(8,128)(2,1)S(1)}, u32[]{:S(2)}) copy-start(bf16[640,128]{1,0:T(8,128)(2,1)S(1)} %collective-permute-done.2.rest_2_) | copy-start | bytes 491524
  52.8 13.2 %collective-permute-start.12 = (bf16[640,128]{1,0:T(8,128)(2,1)}, bf16[640,128]{1,0:T(8,128)(2,1)S(1)}, u32[]{:S(2)}, u32[]{:S(2)}) collective-permute-start(bf16[640,128]{1,0:T(8,128)(2,1)} %get-tuple-element.51), channel_id=1, source_target_pairs={{0,24},{1,25},{2,26},{3,27},{8,16},{9,17},{10,18},{11,19},{16,8},{... | collective-permute-start | bytes 491528 | tf_op jit(solution)/shard_map/ppermute | solution.py:448
  52.9 30.7 %copy-start.3 = (bf16[640,128]{1,0:T(8,128)(2,1)}, bf16[640,128]{1,0:T(8,128)(2,1)S(1)}, u32[]{:S(2)}) copy-start(bf16[640,128]{1,0:T(8,128)(2,1)S(1)} %collective-permute-done.3.rest_3_) | copy-start | bytes 491524
  52.9 14.3 %collective-permute-start.5 = (bf16[640,128]{1,0:T(8,128)(2,1)}, bf16[640,128]{1,0:T(8,128)(2,1)S(1)}, u32[]{:S(2)}, u32[]{:S(2)}) collective-permute-start(bf16[640,128]{1,0:T(8,128)(2,1)} %get-tuple-element.44), channel_id=1, source_target_pairs={{0,9},{1,8},{2,11},{3,10},{8,1},{9,0},{10,3},{11,2},{16,25},{17,24... | collective-permute-start | bytes 491528 | tf_op jit(solution)/shard_map/ppermute | solution.py:448
  54.6 29.0 %copy-start.4 = (bf16[640,128]{1,0:T(8,128)(2,1)}, bf16[640,128]{1,0:T(8,128)(2,1)S(1)}, u32[]{:S(2)}) copy-start(bf16[640,128]{1,0:T(8,128)(2,1)S(1)} %collective-permute-done.4.rest_4_) | copy-start | bytes 491524
  54.6 13.5 %collective-permute-start.6 = (bf16[640,128]{1,0:T(8,128)(2,1)}, bf16[640,128]{1,0:T(8,128)(2,1)S(1)}, u32[]{:S(2)}, u32[]{:S(2)}) collective-permute-start(bf16[640,128]{1,0:T(8,128)(2,1)} %get-tuple-element.45), channel_id=1, source_target_pairs={{0,10},{1,11},{2,8},{3,9},{8,2},{9,3},{10,0},{11,1},{16,26},{17,27... | collective-permute-start | bytes 491528 | tf_op jit(solution)/shard_map/ppermute | solution.py:448
  56.1 27.5 %copy-start.5 = (bf16[640,128]{1,0:T(8,128)(2,1)}, bf16[640,128]{1,0:T(8,128)(2,1)S(1)}, u32[]{:S(2)}) copy-start(bf16[640,128]{1,0:T(8,128)(2,1)S(1)} %collective-permute-done.8.rest_8_) | copy-start | bytes 491524
  56.1 13.5 %collective-permute-start.9 = (bf16[640,128]{1,0:T(8,128)(2,1)}, bf16[640,128]{1,0:T(8,128)(2,1)S(1)}, u32[]{:S(2)}, u32[]{:S(2)}) collective-permute-start(bf16[640,128]{1,0:T(8,128)(2,1)} %get-tuple-element.48), channel_id=1, source_target_pairs={{0,17},{1,16},{2,19},{3,18},{8,25},{9,24},{10,27},{11,26},{16,1},{... | collective-permute-start | bytes 491528 | tf_op jit(solution)/shard_map/ppermute | solution.py:448
  62.9 20.6 %copy-start.6 = (bf16[640,128]{1,0:T(8,128)(2,1)}, bf16[640,128]{1,0:T(8,128)(2,1)S(1)}, u32[]{:S(2)}) copy-start(bf16[640,128]{1,0:T(8,128)(2,1)S(1)} %collective-permute-done.10.rest_10_) | copy-start | bytes 491524
  62.9 15.5 %collective-permute-start.11 = (bf16[640,128]{1,0:T(8,128)(2,1)}, bf16[640,128]{1,0:T(8,128)(2,1)S(1)}, u32[]{:S(2)}, u32[]{:S(2)}) collective-permute-start(bf16[640,128]{1,0:T(8,128)(2,1)} %get-tuple-element.50), channel_id=1, source_target_pairs={{0,19},{1,18},{2,17},{3,16},{8,27},{9,26},{10,25},{11,24},{16,3},{... | collective-permute-start | bytes 491528 | tf_op jit(solution)/shard_map/ppermute | solution.py:448
  66.0 17.6 %copy-start.7 = (bf16[640,128]{1,0:T(8,128)(2,1)}, bf16[640,128]{1,0:T(8,128)(2,1)S(1)}, u32[]{:S(2)}) copy-start(bf16[640,128]{1,0:T(8,128)(2,1)S(1)} %collective-permute-done.12.rest_12_) | copy-start | bytes 491524
  66.0 17.1 %collective-permute-start.13 = (bf16[640,128]{1,0:T(8,128)(2,1)}, bf16[640,128]{1,0:T(8,128)(2,1)S(1)}, u32[]{:S(2)}, u32[]{:S(2)}) collective-permute-start(bf16[640,128]{1,0:T(8,128)(2,1)} %get-tuple-element.52), channel_id=1, source_target_pairs={{0,25},{1,24},{2,27},{3,26},{8,17},{9,16},{10,19},{11,18},{16,9},{... | collective-permute-start | bytes 491528 | tf_op jit(solution)/shard_map/ppermute | solution.py:448
  67.2 16.4 %copy-start.8 = (bf16[640,128]{1,0:T(8,128)(2,1)}, bf16[640,128]{1,0:T(8,128)(2,1)S(1)}, u32[]{:S(2)}) copy-start(bf16[640,128]{1,0:T(8,128)(2,1)S(1)} %collective-permute-done.5.rest_5_) | copy-start | bytes 491524
  67.2 15.9 %collective-permute-start.14 = (bf16[640,128]{1,0:T(8,128)(2,1)}, bf16[640,128]{1,0:T(8,128)(2,1)S(1)}, u32[]{:S(2)}, u32[]{:S(2)}) collective-permute-start(bf16[640,128]{1,0:T(8,128)(2,1)} %get-tuple-element.53), channel_id=1, source_target_pairs={{0,26},{1,27},{2,24},{3,25},{8,18},{9,19},{10,16},{11,17},{16,10},... | collective-permute-start | bytes 491528 | tf_op jit(solution)/shard_map/ppermute | solution.py:448
  68.1 15.6 %copy-start.9 = (bf16[640,128]{1,0:T(8,128)(2,1)}, bf16[640,128]{1,0:T(8,128)(2,1)S(1)}, u32[]{:S(2)}) copy-start(bf16[640,128]{1,0:T(8,128)(2,1)S(1)} %collective-permute-done.6.rest_6_) | copy-start | bytes 491524
  68.1 15.0 %collective-permute-start.7 = (bf16[640,128]{1,0:T(8,128)(2,1)}, bf16[640,128]{1,0:T(8,128)(2,1)S(1)}, u32[]{:S(2)}, u32[]{:S(2)}) collective-permute-start(bf16[640,128]{1,0:T(8,128)(2,1)} %get-tuple-element.46), channel_id=1, source_target_pairs={{0,11},{1,10},{2,9},{3,8},{8,3},{9,2},{10,1},{11,0},{16,27},{17,26... | collective-permute-start | bytes 491528 | tf_op jit(solution)/shard_map/ppermute | solution.py:448
  69.5 14.1 %copy-start.10 = (bf16[640,128]{1,0:T(8,128)(2,1)}, bf16[640,128]{1,0:T(8,128)(2,1)S(1)}, u32[]{:S(2)}) copy-start(bf16[640,128]{1,0:T(8,128)(2,1)S(1)} %collective-permute-done.9.rest_9_) | copy-start | bytes 491524
  69.5 14.0 %collective-permute-start.15 = (bf16[640,128]{1,0:T(8,128)(2,1)S(1)}, bf16[640,128]{1,0:T(8,128)(2,1)S(1)}, u32[]{:S(2)}, u32[]{:S(2)}) collective-permute-start(bf16[640,128]{1,0:T(8,128)(2,1)S(1)} %copy-done.19), channel_id=1, source_target_pairs={{0,27},{1,26},{2,25},{3,24},{8,19},{9,18},{10,17},{11,16},{16,11},... | collective-permute-start | bytes 491528 | tf_op jit(solution)/shard_map/ppermute | solution.py:448
  78.5 5.2 %copy-start.11 = (bf16[640,128]{1,0:T(8,128)(2,1)}, bf16[640,128]{1,0:T(8,128)(2,1)S(1)}, u32[]{:S(2)}) copy-start(bf16[640,128]{1,0:T(8,128)(2,1)S(1)} %collective-permute-done.11.rest_11_) | copy-start | bytes 491524
  83.1 0.7 copy-start.12
  83.1 0.7 copy-start.13
  83.1 0.8 copy-start.14
  83.6 0.7 copy-start.15
  84.2 20.7 %copy-start.17 = (s32[16,256]{1,0:T(8,128)S(1)}, s32[16,256]{1,0:T(8,128)}, u32[]{:S(2)}) copy-start(s32[16,256]{1,0:T(8,128)} %get-tuple-element.32) | copy-start | bytes 49156
  100.0 4.9 %collective-permute-start.16 = (f32[16,256]{1,0:T(8,128)}, f32[16,256]{1,0:T(8,128)S(1)}, u32[]{:S(2)}, u32[]{:S(2)}) collective-permute-start(f32[16,256]{1,0:T(8,128)} %get-tuple-element.56), channel_id=1, source_target_pairs={{0,4},{4,0},{1,5},{5,1},{2,6},{6,2},{3,7},{7,3},{8,12},{12,8},{9,1... | collective-permute-start | bytes 49160 | tf_op jit(solution)/shard_map/ppermute | solution.py:453

commit v5 on v4

--- a/solution.py
+++ b/solution.py
@@ -167,7 +167,7 @@
         local = block * al_n + spot
         part = (local ^ at) if near & (near - 1) == 0 else lax.rem(at - local + near, near)
         inside = which_half == side
-        mine_ref[...] = inside[:half].astype(jnp.int32)
+        mine_ref[...] = inside.astype(jnp.int32)
         hits, before, counts = occurrences(jnp.where(inside, part, near), near)
         row, col = iota((queries, queries), 0), iota((queries, queries), 1)
         lower = row > col
@@ -189,7 +189,7 @@
         slot_ref[:half] = ids_ref[:, children:]
         slot_ref[half:] = mate_ref[:, children:] + past_half
 
-    shapes = [(3 * queries, 128), (queries + 8, 128), (queries, children), (queries, lanes), (half, children)]
+    shapes = [(3 * queries, 128), (queries + 8, 128), (queries, children), (queries, lanes), (queries, children)]
     return pl.pallas_call(
         kernel,
         out_shape=[jax.ShapeDtypeStruct(shape, jnp.int32) for shape in shapes],
@@ -286,7 +286,7 @@
     )(slots, near_by(fetched))
 
 
-def score_rows(segments, bases, rel, slabs, past, w_first, b_first, w_second, b_second, w_out, history, lanes):
+def score_rows(segments, bases, rel, mine, slabs, past, w_first, b_first, w_second, b_second, w_out, history, lanes):
     queries, children = rel.shape
     slab, width = slabs[0].shape
     parts = len(slabs)
@@ -294,11 +294,11 @@
     batch = min(parts, 16)
     longest = rounded(queries * children + queries * 8, BLOCK)
     per_block = BLOCK // 128
-    quick = 3
+    quick = 4
     group = 16
     half = queries // 2
 
-    def kernel(seg_ref, base_ref, rel_ref, past_ref, w1, b1, w2, b2, wo, *rest):
+    def kernel(seg_ref, base_ref, rel_ref, mine_ref, past_ref, w1, b1, w2, b2, wo, *rest):
         slab_refs, out_refs = rest[:parts], rest[parts : parts + 2]
         wide, rows, pool, line, g0, g1, g2 = rest[parts + 2 :]
         for i, ref in enumerate(slab_refs):
@@ -373,15 +373,15 @@
                 lane = spot & 127
                 took = [jnp.take_along_axis(ref[q : q + 8, :], lane, axis=1) for ref in (g0, g1, g2)]
                 out_ref, at = out_refs[q // half], q % half
-                out_ref[at : at + 8, k : k + 128] = jnp.where(
-                    spot < 128, took[0], jnp.where(spot < 256, took[1], took[2])
-                )
+                found = jnp.where(spot < 128, took[0], jnp.where(spot < 256, took[1], took[2]))
+                here = mine_ref[q : q + 8, k : k + 128] > 0
+                out_ref[at : at + 8, k : k + 128] = jnp.where(here, found, 0.0)
 
     wide_rows = parts * slab + 8 * quick
     return pl.pallas_call(
         kernel,
         out_shape=[jax.ShapeDtypeStruct((half, children), jnp.float32)] * 2,
-        in_specs=[SMEM, SMEM] + [VMEM] * (7 + parts),
+        in_specs=[SMEM, SMEM] + [VMEM] * (8 + parts),
         out_specs=[VMEM] * 2,
         scratch_shapes=[
             pltpu.VMEM((wide_rows, width), jnp.float32),
@@ -395,6 +395,7 @@
         segments,
         bases,
         rel,
+        mine,
         past,
         w_first,
         b_first.reshape(1, hidden),
@@ -449,9 +450,10 @@
 
     lanes = rounded(history, 128)
     past = arrange_past(past_slot, past_in, 2 * queries, history, lanes)
-    own, lent = score_rows(segments, bases, rel, slabs, past, w_first, b_first, w_second, b_second, w_out.reshape(1, -1), history, lanes)
+    slabs = [near_by(x) if i in waves[-1] and i else x for i, x in enumerate(slabs)]
+    own, lent = score_rows(segments, bases, rel, mine, slabs, past, w_first, b_first, w_second, b_second, w_out.reshape(1, -1), history, lanes)
     back = lax.ppermute(lent, "ah", swap)
-    return jnp.where(mine > 0, own, back)
+    return own + back
 
 
 def solution(mesh):

time: 107 us -> 105 us (0.981)
  Pallas kernels: 50.4 us -> 48.7 us
    pallas_call x1, Pallas kernels: 15.8 us -> 14.1 us  [score_rows(): pl.pallas_call(kernel, out_shape=[jax.ShapeDtypeStruct((half, children),...]
    select_n x1 -> x0, other arithmetic: 1.33 us -> none  [body(): return jnp.where(mine > 0, own, back)]
    add x0 -> x1, other arithmetic: none -> 1.33 us  [body(): return own + back]
  transfers between devices with their start and end apart: 19 -> 19, of which waited for: 6 -> 6; matrix products, arithmetic and copies ran while one was open for 1% -> 1% of each run, Pallas kernels for 23% -> 24%
where the time goes in v5:
time: 105 us; the launch traced here: 104 us
  Pallas kernels  48.7 us (46%)
  starting transfers between devices  30.2 us (29%)
  waiting for transfers between devices  21.6 us (21%)
  other arithmetic  1.99 us (2%)
  local copies, waits for them, and re-layouts  1.86 us (2%)
    pallas_call x4, Pallas kernels, gather_slabs(): pl.pallas_call(kernel, out_shape=shapes, in_specs=[SMEM, SMEM, VMEM], out...  23.5 us
    ppermute x15, starting transfers between devices, body(): lax.ppermute(out, HALF, pairs[shift * near:(shift + 1) * near])  17.5 us
    pallas_call x1, Pallas kernels, score_rows(): pl.pallas_call(kernel, out_shape=[jax.ShapeDtypeStruct((half, children),...  14.1 us
    all_to_all x1, starting transfers between devices, body(): lax.all_to_all(wanted, AXES, split_axis=0, concat_axis=0, tiled=True)  7.32 us
    all_to_all x1, waiting for transfers between devices, body(): lax.all_to_all(wanted, AXES, split_axis=0, concat_axis=0, tiled=True)  6.56 us
    ppermute x15, waiting for transfers between devices, body(): lax.ppermute(out, HALF, pairs[shift * near:(shift + 1) * near])  5.75 us
    ppermute x1, waiting for transfers between devices, body(): back = lax.ppermute(lent, 'ah', swap)  4.84 us
    pallas_call x1, Pallas kernels, build_lists(): pl.pallas_call(kernel, out_shape=[jax.ShapeDtypeStruct((peers, 1, stride)...  4.6 us
  transfers between devices with their start and end apart: 19, of which 6 were waited for; matrix products, arithmetic and copies ran while one was open for 1% of the time, Pallas kernels for 24%

profile of v5, /device:TPU:0, one launch (start us, length us, event | category | flops | bytes accessed | tf_op | source)
XLA Modules:
  0.0 104.4 jit_solution(16296045523362694321)
XLA Ops:
  0.0 4.6 %build_lists.1 = (s32[32,1,384]{2,1,0:T(1,128)}, s32[16,384]{1,0:T(8,128)}) custom-call(s32[16,256]{1,0:T(8,128)} %kid_ref.1, s32[16,69]{1,0:T(8,128)} %past_ref.1), custom_call_target="tpu_custom_call" | custom-call | tf_op jit(solution)/shard_map/build_lists/pallas_call | solution.py:136
  4.6 7.3 %all-to-all-start = ((s32[32,1,384]{2,1,0:T(1,128)}), s32[32,1,384]{2,1,0:T(1,128)S(1)}, u32[]{:S(2)}, u32[]{:S(2)}) async-start(s32[32,1,384]{2,1,0:T(1,128)} %get-tuple-element.37), calls=%async_computation | async-start | bytes 98304 | tf_op jit(solution)/shard_map/all_to_all | solution.py:424
  11.9 0.7 pad_add_fusion.here_ref
  12.6 6.6 %all-to-all-done = s32[32,1,384]{2,1,0:T(1,128)S(1)} async-done(((s32[32,1,384]{2,1,0:T(1,128)}), s32[32,1,384]{2,1,0:T(1,128)S(1)}, u32[]{:S(2)}, u32[]{:S(2)}) %all-to-all-start) | async-done | bytes 49184 | tf_op jit(solution)/shard_map/all_to_all | solution.py:424
  19.2 0.6 copy-done
  19.8 5.2 %gather_past.1 = (bf16[2304,128]{1,0:T(8,128)(2,1)}, bf16[640,128]{1,0:T(8,128)(2,1)}) custom-call(s32[2]{0:T(128)} %pad_add_fusion.here_ref, s32[12288]{0:T(1024)} %bitcast.8, bf16[8192,128]{1,0:T(8,128)(2,1)} %table_ref.7), custom_call_target="tpu_custom_call" | custom-call | tf_op jit(solution)/shard_map/gather_past/pallas_call | solution.py:248
  25.0 2.6 %all-to-all-start.1 = ((bf16[32,72,128]{2,1,0:T(8,128)(2,1)}), bf16[32,72,128]{2,1,0:T(8,128)(2,1)S(1)}, u32[]{:S(2)}, u32[]{:S(2)}) async-start(bf16[32,72,128]{2,1,0:T(8,128)(2,1)} %bitcast.12), calls=%async_computation.1 | async-start | bytes 1179648 | tf_op jit(solution)/shard_map/all_to_all | solution.py:445
  27.7 2.7 %collective-permute-start = (s32[16,384]{1,0:T(8,128)S(1)}, s32[16,384]{1,0:T(8,128)S(1)}, u32[]{:S(2)}, u32[]{:S(2)}) collective-permute-start(s32[16,384]{1,0:T(8,128)S(1)} %copy-done.11), channel_id=1, source_target_pairs={{0,4},{4,0},{1,5},{5,1},{2,6},{6,2},{3,7},{7,3},{8,12},{12,8},{9,1... | collective-permute-start | bytes 73736 | tf_op jit(solution)/shard_map/ppermute | solution.py:428
  30.4 6.7 %gather_slabs.3 = (bf16[640,128]{1,0:T(8,128)(2,1)}, bf16[640,128]{1,0:T(8,128)(2,1)}, bf16[640,128]{1,0:T(8,128)(2,1)}, bf16[640,128]{1,0:T(8,128)(2,1)}, bf16[...) custom-call(s32[2]{0:T(128)} %pad_add_fusion.here_ref, s32[12288]{0:T(1024)} %bitcast.9, bf16[8192,128]{1,0:T(8,128)(2,1)} %table_ref.7), custom_call_target="tpu_custom_call" | custom-call | tf_op jit(solution)/shard_map/gather_slabs/pallas_call | solution.py:248
  37.1 1.5 %collective-permute-start.1 = (bf16[640,128]{1,0:T(8,128)(2,1)}, bf16[640,128]{1,0:T(8,128)(2,1)S(1)}, u32[]{:S(2)}, u32[]{:S(2)}) collective-permute-start(bf16[640,128]{1,0:T(8,128)(2,1)} %get-tuple-element.40), channel_id=1, source_target_pairs={{0,1},{1,0},{2,3},{3,2},{8,9},{9,8},{10,11},{11,10},{16,17},{17,16... | collective-permute-start | bytes 491528 | tf_op jit(solution)/shard_map/ppermute | solution.py:449
  38.6 1.5 %collective-permute-start.2 = (bf16[640,128]{1,0:T(8,128)(2,1)}, bf16[640,128]{1,0:T(8,128)(2,1)S(1)}, u32[]{:S(2)}, u32[]{:S(2)}) collective-permute-start(bf16[640,128]{1,0:T(8,128)(2,1)} %get-tuple-element.41), channel_id=1, source_target_pairs={{0,2},{1,3},{2,0},{3,1},{8,10},{9,11},{10,8},{11,9},{16,18},{17,19... | collective-permute-start | bytes 491528 | tf_op jit(solution)/shard_map/ppermute | solution.py:449
  40.1 0.5 collective-permute-start.3
  40.6 0.0 collective-permute-start.4
  40.6 4.5 %collective-permute-done.mate_ref = s32[16,384]{1,0:T(8,128)S(1)} collective-permute-done((s32[16,384]{1,0:T(8,128)S(1)}, s32[16,384]{1,0:T(8,128)S(1)}, u32[]{:S(2)}, u32[]{:S(2)}) %collective-permute-start) | collective-permute-done | bytes 24608 | tf_op jit(solution)/shard_map/ppermute | solution.py:428
  45.1 1.5 %collective-permute-start.8 = (bf16[640,128]{1,0:T(8,128)(2,1)}, bf16[640,128]{1,0:T(8,128)(2,1)S(1)}, u32[]{:S(2)}, u32[]{:S(2)}) collective-permute-start(bf16[640,128]{1,0:T(8,128)(2,1)} %get-tuple-element.47), channel_id=1, source_target_pairs={{0,16},{1,17},{2,18},{3,19},{8,24},{9,25},{10,26},{11,27},{16,0},{... | collective-permute-start | bytes 491528 | tf_op jit(solution)/shard_map/ppermute | solution.py:449
  46.6 6.1 %gather_slabs.4 = (bf16[640,128]{1,0:T(8,128)(2,1)}, bf16[640,128]{1,0:T(8,128)(2,1)}, bf16[640,128]{1,0:T(8,128)(2,1)}, bf16[640,128]{1,0:T(8,128)(2,1)}, bf16[640,128]{1,0:T(8,128)(2,1)}) custom-call(s32[2]{0:T(128)} %pad_add_fusion.here_ref, s32[12288]{0:T(1024)} %bitcast.10, bf16[8192,128]{1,0:T(8,128)(2,1)} %table_ref.7), custom_call_target="tpu_custom_call" | custom-call | tf_op jit(solution)/shard_map/gather_slabs/pallas_call | solution.py:248
  52.7 0.0 collective-permute-done.1.rest_1_
  52.7 0.0 collective-permute-start.10
  52.7 0.0 collective-permute-done.2.rest_2_
  52.7 0.1 collective-permute-start.12
  52.8 0.0 collective-permute-done.3.rest_3_
  52.8 1.7 %collective-permute-start.5 = (bf16[640,128]{1,0:T(8,128)(2,1)}, bf16[640,128]{1,0:T(8,128)(2,1)S(1)}, u32[]{:S(2)}, u32[]{:S(2)}) collective-permute-start(bf16[640,128]{1,0:T(8,128)(2,1)} %get-tuple-element.44), channel_id=1, source_target_pairs={{0,9},{1,8},{2,11},{3,10},{8,1},{9,0},{10,3},{11,2},{16,25},{17,24... | collective-permute-start | bytes 491528 | tf_op jit(solution)/shard_map/ppermute | solution.py:449
  54.5 0.0 collective-permute-done.4.rest_4_
  54.5 1.5 %collective-permute-start.6 = (bf16[640,128]{1,0:T(8,128)(2,1)}, bf16[640,128]{1,0:T(8,128)(2,1)S(1)}, u32[]{:S(2)}, u32[]{:S(2)}) collective-permute-start(bf16[640,128]{1,0:T(8,128)(2,1)} %get-tuple-element.45), channel_id=1, source_target_pairs={{0,10},{1,11},{2,8},{3,9},{8,2},{9,3},{10,0},{11,1},{16,26},{17,27... | collective-permute-start | bytes 491528 | tf_op jit(solution)/shard_map/ppermute | solution.py:449
  56.0 1.5 %collective-permute-start.9 = (bf16[640,128]{1,0:T(8,128)(2,1)}, bf16[640,128]{1,0:T(8,128)(2,1)S(1)}, u32[]{:S(2)}, u32[]{:S(2)}) collective-permute-start(bf16[640,128]{1,0:T(8,128)(2,1)} %get-tuple-element.48), channel_id=1, source_target_pairs={{0,17},{1,16},{2,19},{3,18},{8,25},{9,24},{10,27},{11,26},{16,1},{... | collective-permute-start | bytes 491528 | tf_op jit(solution)/shard_map/ppermute | solution.py:449
  57.4 5.4 %gather_slabs.5 = (bf16[640,128]{1,0:T(8,128)(2,1)}, bf16[640,128]{1,0:T(8,128)(2,1)}, bf16[640,128]{1,0:T(8,128)(2,1)}, bf16[640,128]{1,0:T(8,128)(2,1)}) custom-call(s32[2]{0:T(128)} %pad_add_fusion.here_ref, s32[12288]{0:T(1024)} %bitcast.11, bf16[8192,128]{1,0:T(8,128)(2,1)} %table_ref.7), custom_call_target="tpu_custom_call" | custom-call | tf_op jit(solution)/shard_map/gather_slabs/pallas_call | solution.py:248
  62.9 0.0 collective-permute-done.10.rest_10_
  62.9 2.4 %collective-permute-start.11 = (bf16[640,128]{1,0:T(8,128)(2,1)}, bf16[640,128]{1,0:T(8,128)(2,1)S(1)}, u32[]{:S(2)}, u32[]{:S(2)}) collective-permute-start(bf16[640,128]{1,0:T(8,128)(2,1)} %get-tuple-element.50), channel_id=1, source_target_pairs={{0,19},{1,18},{2,17},{3,16},{8,27},{9,26},{10,25},{11,24},{16,3},{... | collective-permute-start | bytes 491528 | tf_op jit(solution)/shard_map/ppermute | solution.py:449
  65.3 0.6 collective-permute-done.12.rest_12_
  65.9 1.2 %collective-permute-start.13 = (bf16[640,128]{1,0:T(8,128)(2,1)}, bf16[640,128]{1,0:T(8,128)(2,1)S(1)}, u32[]{:S(2)}, u32[]{:S(2)}) collective-permute-start(bf16[640,128]{1,0:T(8,128)(2,1)} %get-tuple-element.52), channel_id=1, source_target_pairs={{0,25},{1,24},{2,27},{3,26},{8,17},{9,16},{10,19},{11,18},{16,9},{... | collective-permute-start | bytes 491528 | tf_op jit(solution)/shard_map/ppermute | solution.py:449
  67.1 0.0 collective-permute-done.5.rest_5_
  67.1 0.8 collective-permute-start.14
  68.0 1.5 %collective-permute-start.7 = (bf16[640,128]{1,0:T(8,128)(2,1)}, bf16[640,128]{1,0:T(8,128)(2,1)S(1)}, u32[]{:S(2)}, u32[]{:S(2)}) collective-permute-start(bf16[640,128]{1,0:T(8,128)(2,1)} %get-tuple-element.46), channel_id=1, source_target_pairs={{0,11},{1,10},{2,9},{3,8},{8,3},{9,2},{10,1},{11,0},{16,27},{17,26... | collective-permute-start | bytes 491528 | tf_op jit(solution)/shard_map/ppermute | solution.py:449
  69.4 1.8 %collective-permute-start.15 = (bf16[640,128]{1,0:T(8,128)(2,1)S(1)}, bf16[640,128]{1,0:T(8,128)(2,1)S(1)}, u32[]{:S(2)}, u32[]{:S(2)}) collective-permute-start(bf16[640,128]{1,0:T(8,128)(2,1)S(1)} %copy-done.13), channel_id=1, source_target_pairs={{0,27},{1,26},{2,25},{3,24},{8,19},{9,18},{10,17},{11,16},{16,11},... | collective-permute-start | bytes 491528 | tf_op jit(solution)/shard_map/ppermute | solution.py:449
  71.3 0.6 reshape.23.wo
  71.9 2.1 %plan_rows.1 = (s32[96,128]{1,0:T(8,128)}, s32[40,128]{1,0:T(8,128)}, s32[32,256]{1,0:T(8,128)}, s32[32,128]{1,0:T(8,128)}, s32[32,256]{1,0:T(8,128)}) custom-call(s32[2]{0:T(128)} %pad_add_fusion.here_ref, s32[16,384]{1,0:T(8,128)} %get-tuple-element.31.ids_ref, s32[16,384]{1,0:T(8,128)S(1)} %collective-permute-done.mate_ref), custom_call_target="tpu_custom_call" | custom-call | tf_op jit(solution)/shard_map/plan_rows/pallas_call | solution.py:193
  73.9 4.4 %arrange_past.1.past_ref = bf16[4096,128]{1,0:T(8,128)(2,1)} custom-call(s32[32,128]{1,0:T(8,128)} %get-tuple-element.36.slot_ref, bf16[2304,128]{1,0:T(8,128)(2,1)S(1)} %bitcast.7), custom_call_target="tpu_custom_call" | custom-call | tf_op jit(solution)/shard_map/arrange_past/pallas_call | solution.py:279
  78.4 4.6 %collective-permute-done.13.rest_13_ = bf16[640,128]{1,0:T(8,128)(2,1)S(1)} collective-permute-done((bf16[640,128]{1,0:T(8,128)(2,1)}, bf16[640,128]{1,0:T(8,128)(2,1)S(1)}, u32[]{:S(2)}, u32[]{:S(2)}) %collective-permute-start.13) | collective-permute-done | bytes 163872 | tf_op jit(solution)/shard_map/ppermute | solution.py:449
  83.0 0.0 collective-permute-done.7.rest_7_
  83.0 0.5 collective-permute-done.15.rest_15_
  83.5 0.1 copy-done.7
  83.7 0.1 copy-done.8
  83.7 0.1 copy-done.9
  83.8 0.3 copy-done.10
  84.1 14.1 %score_rows.1 = (f32[16,256]{1,0:T(8,128)}, f32[16,256]{1,0:T(8,128)}) custom-call(s32[96,128]{1,0:T(8,128)} %get-tuple-element.32.seg_ref, s32[40,128]{1,0:T(8,128)} %get-tuple-element.33.base_ref, s32[32,256]{1,0:T(8,128)} %get-tuple-element.34.rel_ref, s32[32,256]{1,0:T(8,128)} %get-tuple-element.35.mine_ref, bf16[4096,128]{1,0:T(8,128)(2,1)} %arrange_past.1.past_ref, ...), custom_call_target="tpu_custom_call" | custom-call | tf_op jit(solution)/shard_map/score_rows/pallas_call | solution.py:381
  98.2 0.0 collective-permute-start.16
  98.3 4.8 %collective-permute-done.16 = f32[16,256]{1,0:T(8,128)S(1)} collective-permute-done((f32[16,256]{1,0:T(8,128)}, f32[16,256]{1,0:T(8,128)S(1)}, u32[]{:S(2)}, u32[]{:S(2)}) %collective-permute-start.16) | collective-permute-done | bytes 16416 | tf_op jit(solution)/shard_map/ppermute | solution.py:455
  103.1 1.3 %add.7 = f32[16,256]{1,0:T(8,128)} add(f32[16,256]{1,0:T(8,128)} %get-tuple-element.55, f32[16,256]{1,0:T(8,128)S(1)} %collective-permute-done.16) | non-fusion elementwise | flops 4096 | bytes 49152 | tf_op jit(solution)/shard_map/add | solution.py:456
  (29 shorter events, 0.1 us)
Async XLA Ops:
  4.6 23.0 %copy-start.11 = (s32[16,384]{1,0:T(8,128)S(1)}, s32[16,384]{1,0:T(8,128)}, u32[]{:S(2)}) copy-start(s32[16,384]{1,0:T(8,128)} %get-tuple-element.31.ids_ref) | copy-start | bytes 73732
  4.6 14.6 %all-to-all-start = ((s32[32,1,384]{2,1,0:T(1,128)}), s32[32,1,384]{2,1,0:T(1,128)S(1)}, u32[]{:S(2)}, u32[]{:S(2)}) async-start(s32[32,1,384]{2,1,0:T(1,128)} %get-tuple-element.37), calls=%async_computation | async-start | bytes 98304 | tf_op jit(solution)/shard_map/all_to_all | solution.py:424
  19.2 0.6 copy-start
  25.0 48.9 %all-to-all-start.1 = ((bf16[32,72,128]{2,1,0:T(8,128)(2,1)}), bf16[32,72,128]{2,1,0:T(8,128)(2,1)S(1)}, u32[]{:S(2)}, u32[]{:S(2)}) async-start(bf16[32,72,128]{2,1,0:T(8,128)(2,1)} %bitcast.12), calls=%async_computation.1 | async-start | bytes 1179648 | tf_op jit(solution)/shard_map/all_to_all | solution.py:445
  27.7 17.4 %collective-permute-start = (s32[16,384]{1,0:T(8,128)S(1)}, s32[16,384]{1,0:T(8,128)S(1)}, u32[]{:S(2)}, u32[]{:S(2)}) collective-permute-start(s32[16,384]{1,0:T(8,128)S(1)} %copy-done.11), channel_id=1, source_target_pairs={{0,4},{4,0},{1,5},{5,1},{2,6},{6,2},{3,7},{7,3},{8,12},{12,8},{9,1... | collective-permute-start | bytes 73736 | tf_op jit(solution)/shard_map/ppermute | solution.py:428
  37.1 15.5 %collective-permute-start.1 = (bf16[640,128]{1,0:T(8,128)(2,1)}, bf16[640,128]{1,0:T(8,128)(2,1)S(1)}, u32[]{:S(2)}, u32[]{:S(2)}) collective-permute-start(bf16[640,128]{1,0:T(8,128)(2,1)} %get-tuple-element.40), channel_id=1, source_target_pairs={{0,1},{1,0},{2,3},{3,2},{8,9},{9,8},{10,11},{11,10},{16,17},{17,16... | collective-permute-start | bytes 491528 | tf_op jit(solution)/shard_map/ppermute | solution.py:449
  38.6 14.1 %collective-permute-start.2 = (bf16[640,128]{1,0:T(8,128)(2,1)}, bf16[640,128]{1,0:T(8,128)(2,1)S(1)}, u32[]{:S(2)}, u32[]{:S(2)}) collective-permute-start(bf16[640,128]{1,0:T(8,128)(2,1)} %get-tuple-element.41), channel_id=1, source_target_pairs={{0,2},{1,3},{2,0},{3,1},{8,10},{9,11},{10,8},{11,9},{16,18},{17,19... | collective-permute-start | bytes 491528 | tf_op jit(solution)/shard_map/ppermute | solution.py:449
  40.1 12.6 %collective-permute-start.3 = (bf16[640,128]{1,0:T(8,128)(2,1)}, bf16[640,128]{1,0:T(8,128)(2,1)S(1)}, u32[]{:S(2)}, u32[]{:S(2)}) collective-permute-start(bf16[640,128]{1,0:T(8,128)(2,1)} %get-tuple-element.42), channel_id=1, source_target_pairs={{0,3},{1,2},{2,1},{3,0},{8,11},{9,10},{10,9},{11,8},{16,19},{17,18... | collective-permute-start | bytes 491528 | tf_op jit(solution)/shard_map/ppermute | solution.py:449
  40.6 13.9 %collective-permute-start.4 = (bf16[640,128]{1,0:T(8,128)(2,1)}, bf16[640,128]{1,0:T(8,128)(2,1)S(1)}, u32[]{:S(2)}, u32[]{:S(2)}) collective-permute-start(bf16[640,128]{1,0:T(8,128)(2,1)} %get-tuple-element.43), channel_id=1, source_target_pairs={{0,8},{1,9},{2,10},{3,11},{8,0},{9,1},{10,2},{11,3},{16,24},{17,25... | collective-permute-start | bytes 491528 | tf_op jit(solution)/shard_map/ppermute | solution.py:449
  45.1 24.4 %copy-start.13 = (bf16[640,128]{1,0:T(8,128)(2,1)S(1)}, bf16[640,128]{1,0:T(8,128)(2,1)}, u32[]{:S(2)}) copy-start(bf16[640,128]{1,0:T(8,128)(2,1)} %get-tuple-element.54) | copy-start | bytes 491524
  45.1 26.2 %copy-start.12 = (bf16[512]{0:T(512)(128)(2,1)S(1)}, bf16[512]{0:T(512)(128)(2,1)}, u32[]{:S(2)}) copy-start(bf16[512]{0:T(512)(128)(2,1)} %param.15) | copy-start | bytes 3076
  45.1 10.9 %collective-permute-start.8 = (bf16[640,128]{1,0:T(8,128)(2,1)}, bf16[640,128]{1,0:T(8,128)(2,1)S(1)}, u32[]{:S(2)}, u32[]{:S(2)}) collective-permute-start(bf16[640,128]{1,0:T(8,128)(2,1)} %get-tuple-element.47), channel_id=1, source_target_pairs={{0,16},{1,17},{2,18},{3,19},{8,24},{9,25},{10,26},{11,27},{16,0},{... | collective-permute-start | bytes 491528 | tf_op jit(solution)/shard_map/ppermute | solution.py:449
  52.7 10.2 %collective-permute-start.10 = (bf16[640,128]{1,0:T(8,128)(2,1)}, bf16[640,128]{1,0:T(8,128)(2,1)S(1)}, u32[]{:S(2)}, u32[]{:S(2)}) collective-permute-start(bf16[640,128]{1,0:T(8,128)(2,1)} %get-tuple-element.49), channel_id=1, source_target_pairs={{0,18},{1,19},{2,16},{3,17},{8,26},{9,27},{10,24},{11,25},{16,2},{... | collective-permute-start | bytes 491528 | tf_op jit(solution)/shard_map/ppermute | solution.py:449
  52.7 13.2 %collective-permute-start.12 = (bf16[640,128]{1,0:T(8,128)(2,1)}, bf16[640,128]{1,0:T(8,128)(2,1)S(1)}, u32[]{:S(2)}, u32[]{:S(2)}) collective-permute-start(bf16[640,128]{1,0:T(8,128)(2,1)} %get-tuple-element.51), channel_id=1, source_target_pairs={{0,24},{1,25},{2,26},{3,27},{8,16},{9,17},{10,18},{11,19},{16,8},{... | collective-permute-start | bytes 491528 | tf_op jit(solution)/shard_map/ppermute | solution.py:449
  52.8 14.4 %collective-permute-start.5 = (bf16[640,128]{1,0:T(8,128)(2,1)}, bf16[640,128]{1,0:T(8,128)(2,1)S(1)}, u32[]{:S(2)}, u32[]{:S(2)}) collective-permute-start(bf16[640,128]{1,0:T(8,128)(2,1)} %get-tuple-element.44), channel_id=1, source_target_pairs={{0,9},{1,8},{2,11},{3,10},{8,1},{9,0},{10,3},{11,2},{16,25},{17,24... | collective-permute-start | bytes 491528 | tf_op jit(solution)/shard_map/ppermute | solution.py:449
  54.5 13.5 %collective-permute-start.6 = (bf16[640,128]{1,0:T(8,128)(2,1)}, bf16[640,128]{1,0:T(8,128)(2,1)S(1)}, u32[]{:S(2)}, u32[]{:S(2)}) collective-permute-start(bf16[640,128]{1,0:T(8,128)(2,1)} %get-tuple-element.45), channel_id=1, source_target_pairs={{0,10},{1,11},{2,8},{3,9},{8,2},{9,3},{10,0},{11,1},{16,26},{17,27... | collective-permute-start | bytes 491528 | tf_op jit(solution)/shard_map/ppermute | solution.py:449
  56.0 13.5 %collective-permute-start.9 = (bf16[640,128]{1,0:T(8,128)(2,1)}, bf16[640,128]{1,0:T(8,128)(2,1)S(1)}, u32[]{:S(2)}, u32[]{:S(2)}) collective-permute-start(bf16[640,128]{1,0:T(8,128)(2,1)} %get-tuple-element.48), channel_id=1, source_target_pairs={{0,17},{1,16},{2,19},{3,18},{8,25},{9,24},{10,27},{11,26},{16,1},{... | collective-permute-start | bytes 491528 | tf_op jit(solution)/shard_map/ppermute | solution.py:449
  62.9 20.6 %copy-start.1 = (bf16[640,128]{1,0:T(8,128)(2,1)}, bf16[640,128]{1,0:T(8,128)(2,1)S(1)}, u32[]{:S(2)}) copy-start(bf16[640,128]{1,0:T(8,128)(2,1)S(1)} %collective-permute-done.10.rest_10_) | copy-start | bytes 491524
  62.9 15.5 %collective-permute-start.11 = (bf16[640,128]{1,0:T(8,128)(2,1)}, bf16[640,128]{1,0:T(8,128)(2,1)S(1)}, u32[]{:S(2)}, u32[]{:S(2)}) collective-permute-start(bf16[640,128]{1,0:T(8,128)(2,1)} %get-tuple-element.50), channel_id=1, source_target_pairs={{0,19},{1,18},{2,17},{3,16},{8,27},{9,26},{10,25},{11,24},{16,3},{... | collective-permute-start | bytes 491528 | tf_op jit(solution)/shard_map/ppermute | solution.py:449
  65.9 17.6 %copy-start.2 = (bf16[640,128]{1,0:T(8,128)(2,1)}, bf16[640,128]{1,0:T(8,128)(2,1)S(1)}, u32[]{:S(2)}) copy-start(bf16[640,128]{1,0:T(8,128)(2,1)S(1)} %collective-permute-done.12.rest_12_) | copy-start | bytes 491524
  65.9 17.1 %collective-permute-start.13 = (bf16[640,128]{1,0:T(8,128)(2,1)}, bf16[640,128]{1,0:T(8,128)(2,1)S(1)}, u32[]{:S(2)}, u32[]{:S(2)}) collective-permute-start(bf16[640,128]{1,0:T(8,128)(2,1)} %get-tuple-element.52), channel_id=1, source_target_pairs={{0,25},{1,24},{2,27},{3,26},{8,17},{9,16},{10,19},{11,18},{16,9},{... | collective-permute-start | bytes 491528 | tf_op jit(solution)/shard_map/ppermute | solution.py:449
  67.1 16.4 %copy-start.3 = (bf16[640,128]{1,0:T(8,128)(2,1)}, bf16[640,128]{1,0:T(8,128)(2,1)S(1)}, u32[]{:S(2)}) copy-start(bf16[640,128]{1,0:T(8,128)(2,1)S(1)} %collective-permute-done.5.rest_5_) | copy-start | bytes 491524
  67.1 15.9 %collective-permute-start.14 = (bf16[640,128]{1,0:T(8,128)(2,1)}, bf16[640,128]{1,0:T(8,128)(2,1)S(1)}, u32[]{:S(2)}, u32[]{:S(2)}) collective-permute-start(bf16[640,128]{1,0:T(8,128)(2,1)} %get-tuple-element.53), channel_id=1, source_target_pairs={{0,26},{1,27},{2,24},{3,25},{8,18},{9,19},{10,16},{11,17},{16,10},... | collective-permute-start | bytes 491528 | tf_op jit(solution)/shard_map/ppermute | solution.py:449
  68.0 15.5 %copy-start.4 = (bf16[640,128]{1,0:T(8,128)(2,1)}, bf16[640,128]{1,0:T(8,128)(2,1)S(1)}, u32[]{:S(2)}) copy-start(bf16[640,128]{1,0:T(8,128)(2,1)S(1)} %collective-permute-done.6.rest_6_) | copy-start | bytes 491524
  68.0 15.0 %collective-permute-start.7 = (bf16[640,128]{1,0:T(8,128)(2,1)}, bf16[640,128]{1,0:T(8,128)(2,1)S(1)}, u32[]{:S(2)}, u32[]{:S(2)}) collective-permute-start(bf16[640,128]{1,0:T(8,128)(2,1)} %get-tuple-element.46), channel_id=1, source_target_pairs={{0,11},{1,10},{2,9},{3,8},{8,3},{9,2},{10,1},{11,0},{16,27},{17,26... | collective-permute-start | bytes 491528 | tf_op jit(solution)/shard_map/ppermute | solution.py:449
  69.4 14.1 %copy-start.5 = (bf16[640,128]{1,0:T(8,128)(2,1)}, bf16[640,128]{1,0:T(8,128)(2,1)S(1)}, u32[]{:S(2)}) copy-start(bf16[640,128]{1,0:T(8,128)(2,1)S(1)} %collective-permute-done.9.rest_9_) | copy-start | bytes 491524
  69.4 14.1 %collective-permute-start.15 = (bf16[640,128]{1,0:T(8,128)(2,1)S(1)}, bf16[640,128]{1,0:T(8,128)(2,1)S(1)}, u32[]{:S(2)}, u32[]{:S(2)}) collective-permute-start(bf16[640,128]{1,0:T(8,128)(2,1)S(1)} %copy-done.13), channel_id=1, source_target_pairs={{0,27},{1,26},{2,25},{3,24},{8,19},{9,18},{10,17},{11,16},{16,11},... | collective-permute-start | bytes 491528 | tf_op jit(solution)/shard_map/ppermute | solution.py:449
  78.4 5.2 %copy-start.6 = (bf16[640,128]{1,0:T(8,128)(2,1)}, bf16[640,128]{1,0:T(8,128)(2,1)S(1)}, u32[]{:S(2)}) copy-start(bf16[640,128]{1,0:T(8,128)(2,1)S(1)} %collective-permute-done.11.rest_11_) | copy-start | bytes 491524
  83.0 0.7 copy-start.7
  83.0 0.7 copy-start.8
  83.0 0.8 copy-start.9
  83.5 0.7 copy-start.10
  98.2 4.9 %collective-permute-start.16 = (f32[16,256]{1,0:T(8,128)}, f32[16,256]{1,0:T(8,128)S(1)}, u32[]{:S(2)}, u32[]{:S(2)}) collective-permute-start(f32[16,256]{1,0:T(8,128)} %get-tuple-element.56), channel_id=1, source_target_pairs={{0,4},{4,0},{1,5},{5,1},{2,6},{6,2},{3,7},{7,3},{8,12},{12,8},{9,1... | collective-permute-start | bytes 49160 | tf_op jit(solution)/shard_map/ppermute | solution.py:455

commit v6 on v5

--- a/solution.py
+++ b/solution.py
@@ -8,7 +8,7 @@
 
 AXES = ("pb", "ah", "al")
 HALF = ("pb", "al")
-BLOCK = 1024
+BLOCK = 1280
 
 
 def rounded(n, m):
@@ -278,7 +278,7 @@
 
     return pl.pallas_call(
         kernel,
-        out_shape=jax.ShapeDtypeStruct((queries * lanes, width), fetched.dtype),
+        out_shape=pltpu.VMEM((queries * lanes, width), fetched.dtype),
         in_specs=[SMEM, VMEM],
         out_specs=VMEM,
         scratch_shapes=[pltpu.VMEM((rows, width), jnp.float32), pltpu.VMEM((lanes, width), jnp.float32)],
@@ -295,7 +295,7 @@
     longest = rounded(queries * children + queries * 8, BLOCK)
     per_block = BLOCK // 128
     quick = 4
-    group = 16
+    group = 32
     half = queries // 2
 
     def kernel(seg_ref, base_ref, rel_ref, mine_ref, past_ref, w1, b1, w2, b2, wo, *rest):
@@ -339,8 +339,8 @@
                 kids = rows[pl.ds(base, children), :].astype(jnp.bfloat16)
                 own = past_ref[pl.ds(pl.multiple_of(q * lanes, lanes), lanes), :]
                 logits = lax.dot_general(kids, own, (((1,), (1,)), ((), ())), preferred_element_type=jnp.float32)
-                logits = logits * width ** (-0.5)
-                share = (jax.nn.sigmoid(logits) * history ** (-0.5)).astype(jnp.bfloat16)
+                half_share = 0.5 * history ** (-0.5)
+                share = (half_share + half_share * jnp.tanh(logits * (0.5 * width ** (-0.5)))).astype(jnp.bfloat16)
                 pool[pl.ds(base, children), :] = jnp.dot(share, own, preferred_element_type=jnp.float32)
             return c
 
@@ -396,7 +396,7 @@
         bases,
         rel,
         mine,
-        past,
+        near_by(past),
         w_first,
         b_first.reshape(1, hidden),
         w_second,

time: 105 us -> 104 us (level)
  Pallas kernels: 48.7 us -> 47.3 us
  waiting for transfers between devices: 21.6 us -> 22.8 us
    ppermute x15, waiting for transfers between devices: 5.75 us -> 6.97 us  [body(): lax.ppermute(out, HALF, pairs[shift * near:(shift + 1) * near])]
  transfers between devices with their start and end apart: 19 -> 19, of which waited for: 6 -> 6; matrix products, arithmetic and copies ran while one was open for 1% -> 1% of each run, Pallas kernels for 24% -> 23%
where the time goes in v6:
time: 104 us
  Pallas kernels  47.3 us (45%)
  starting transfers between devices  30.1 us (29%)
  waiting for transfers between devices  22.8 us (22%)
  other arithmetic  1.92 us (2%)
  local copies, waits for them, and re-layouts  1.24 us (1%)
    pallas_call x4, Pallas kernels, gather_slabs(): pl.pallas_call(kernel, out_shape=shapes, in_specs=[SMEM, SMEM, VMEM], out...  23.6 us
    ppermute x15, starting transfers between devices, body(): lax.ppermute(out, HALF, pairs[shift * near:(shift + 1) * near])  17.4 us
    pallas_call x1, Pallas kernels, score_rows(): pl.pallas_call(kernel, out_shape=[jax.ShapeDtypeStruct((half, children),...  13.6 us
    all_to_all x1, starting transfers between devices, body(): lax.all_to_all(wanted, AXES, split_axis=0, concat_axis=0, tiled=True)  7.32 us
    ppermute x15, waiting for transfers between devices, body(): lax.ppermute(out, HALF, pairs[shift * near:(shift + 1) * near])  6.97 us
    all_to_all x1, waiting for transfers between devices, body(): lax.all_to_all(wanted, AXES, split_axis=0, concat_axis=0, tiled=True)  6.63 us
    ppermute x1, waiting for transfers between devices, body(): back = lax.ppermute(lent, 'ah', swap)  4.84 us
    pallas_call x1, Pallas kernels, build_lists(): pl.pallas_call(kernel, out_shape=[jax.ShapeDtypeStruct((peers, 1, stride)...  4.61 us
  transfers between devices with their start and end apart: 19, of which 6 were waited for; matrix products, arithmetic and copies ran while one was open for 1% of the time, Pallas kernels for 23%

profile of v6, /device:TPU:0, one launch (start us, length us, event | category | flops | bytes accessed | tf_op | source)
XLA Modules:
  0.0 103.6 jit_solution(9199280669688379639)
XLA Ops:
  0.0 4.6 %build_lists.1 = (s32[32,1,384]{2,1,0:T(1,128)}, s32[16,384]{1,0:T(8,128)}) custom-call(s32[16,256]{1,0:T(8,128)} %kid_ref.1, s32[16,69]{1,0:T(8,128)} %past_ref.1), custom_call_target="tpu_custom_call" | custom-call | tf_op jit(solution)/shard_map/build_lists/pallas_call | solution.py:136
  4.6 7.3 %all-to-all-start = ((s32[32,1,384]{2,1,0:T(1,128)}), s32[32,1,384]{2,1,0:T(1,128)S(1)}, u32[]{:S(2)}, u32[]{:S(2)}) async-start(s32[32,1,384]{2,1,0:T(1,128)} %get-tuple-element.37), calls=%async_computation | async-start | bytes 98304 | tf_op jit(solution)/shard_map/all_to_all | solution.py:424
  11.9 0.6 pad_add_fusion.here_ref
  12.5 6.6 %all-to-all-done = s32[32,1,384]{2,1,0:T(1,128)S(1)} async-done(((s32[32,1,384]{2,1,0:T(1,128)}), s32[32,1,384]{2,1,0:T(1,128)S(1)}, u32[]{:S(2)}, u32[]{:S(2)}) %all-to-all-start) | async-done | bytes 49184 | tf_op jit(solution)/shard_map/all_to_all | solution.py:424
  19.2 0.6 copy-done
  19.8 5.3 %gather_past.1 = (bf16[2304,128]{1,0:T(8,128)(2,1)}, bf16[640,128]{1,0:T(8,128)(2,1)}) custom-call(s32[2]{0:T(128)} %pad_add_fusion.here_ref, s32[12288]{0:T(1024)} %bitcast.8, bf16[8192,128]{1,0:T(8,128)(2,1)} %table_ref.7), custom_call_target="tpu_custom_call" | custom-call | tf_op jit(solution)/shard_map/gather_past/pallas_call | solution.py:248
  25.0 2.6 %all-to-all-start.1 = ((bf16[32,72,128]{2,1,0:T(8,128)(2,1)}), bf16[32,72,128]{2,1,0:T(8,128)(2,1)S(1)}, u32[]{:S(2)}, u32[]{:S(2)}) async-start(bf16[32,72,128]{2,1,0:T(8,128)(2,1)} %bitcast.12), calls=%async_computation.1 | async-start | bytes 1179648 | tf_op jit(solution)/shard_map/all_to_all | solution.py:445
  27.7 2.7 %collective-permute-start = (s32[16,384]{1,0:T(8,128)S(1)}, s32[16,384]{1,0:T(8,128)S(1)}, u32[]{:S(2)}, u32[]{:S(2)}) collective-permute-start(s32[16,384]{1,0:T(8,128)S(1)} %copy-done.7), channel_id=1, source_target_pairs={{0,4},{4,0},{1,5},{5,1},{2,6},{6,2},{3,7},{7,3},{8,12},{12,8},{9,1... | collective-permute-start | bytes 73736 | tf_op jit(solution)/shard_map/ppermute | solution.py:428
  30.4 6.8 %gather_slabs.3 = (bf16[640,128]{1,0:T(8,128)(2,1)}, bf16[640,128]{1,0:T(8,128)(2,1)}, bf16[640,128]{1,0:T(8,128)(2,1)}, bf16[640,128]{1,0:T(8,128)(2,1)}, bf16[...) custom-call(s32[2]{0:T(128)} %pad_add_fusion.here_ref, s32[12288]{0:T(1024)} %bitcast.9, bf16[8192,128]{1,0:T(8,128)(2,1)} %table_ref.7), custom_call_target="tpu_custom_call" | custom-call | tf_op jit(solution)/shard_map/gather_slabs/pallas_call | solution.py:248
  37.2 1.5 %collective-permute-start.1 = (bf16[640,128]{1,0:T(8,128)(2,1)}, bf16[640,128]{1,0:T(8,128)(2,1)S(1)}, u32[]{:S(2)}, u32[]{:S(2)}) collective-permute-start(bf16[640,128]{1,0:T(8,128)(2,1)} %get-tuple-element.40), channel_id=1, source_target_pairs={{0,1},{1,0},{2,3},{3,2},{8,9},{9,8},{10,11},{11,10},{16,17},{17,16... | collective-permute-start | bytes 491528 | tf_op jit(solution)/shard_map/ppermute | solution.py:449
  38.7 1.5 %collective-permute-start.2 = (bf16[640,128]{1,0:T(8,128)(2,1)}, bf16[640,128]{1,0:T(8,128)(2,1)S(1)}, u32[]{:S(2)}, u32[]{:S(2)}) collective-permute-start(bf16[640,128]{1,0:T(8,128)(2,1)} %get-tuple-element.41), channel_id=1, source_target_pairs={{0,2},{1,3},{2,0},{3,1},{8,10},{9,11},{10,8},{11,9},{16,18},{17,19... | collective-permute-start | bytes 491528 | tf_op jit(solution)/shard_map/ppermute | solution.py:449
  40.2 0.5 collective-permute-start.3
  40.7 0.0 collective-permute-start.4
  40.7 4.4 %collective-permute-done.mate_ref = s32[16,384]{1,0:T(8,128)S(1)} collective-permute-done((s32[16,384]{1,0:T(8,128)S(1)}, s32[16,384]{1,0:T(8,128)S(1)}, u32[]{:S(2)}, u32[]{:S(2)}) %collective-permute-start) | collective-permute-done | bytes 24608 | tf_op jit(solution)/shard_map/ppermute | solution.py:428
  45.1 1.5 %collective-permute-start.8 = (bf16[640,128]{1,0:T(8,128)(2,1)}, bf16[640,128]{1,0:T(8,128)(2,1)S(1)}, u32[]{:S(2)}, u32[]{:S(2)}) collective-permute-start(bf16[640,128]{1,0:T(8,128)(2,1)} %get-tuple-element.47), channel_id=1, source_target_pairs={{0,16},{1,17},{2,18},{3,19},{8,24},{9,25},{10,26},{11,27},{16,0},{... | collective-permute-start | bytes 491528 | tf_op jit(solution)/shard_map/ppermute | solution.py:449
  46.6 6.1 %gather_slabs.4 = (bf16[640,128]{1,0:T(8,128)(2,1)}, bf16[640,128]{1,0:T(8,128)(2,1)}, bf16[640,128]{1,0:T(8,128)(2,1)}, bf16[640,128]{1,0:T(8,128)(2,1)}, bf16[640,128]{1,0:T(8,128)(2,1)}) custom-call(s32[2]{0:T(128)} %pad_add_fusion.here_ref, s32[12288]{0:T(1024)} %bitcast.10, bf16[8192,128]{1,0:T(8,128)(2,1)} %table_ref.7), custom_call_target="tpu_custom_call" | custom-call | tf_op jit(solution)/shard_map/gather_slabs/pallas_call | solution.py:248
  52.7 0.0 collective-permute-done.1.rest_1_
  52.7 0.0 collective-permute-start.10
  52.7 0.0 collective-permute-done.2.rest_2_
  52.7 0.1 collective-permute-start.12
  52.8 0.0 collective-permute-done.3.rest_3_
  52.8 1.7 %collective-permute-start.5 = (bf16[640,128]{1,0:T(8,128)(2,1)}, bf16[640,128]{1,0:T(8,128)(2,1)S(1)}, u32[]{:S(2)}, u32[]{:S(2)}) collective-permute-start(bf16[640,128]{1,0:T(8,128)(2,1)} %get-tuple-element.44), channel_id=1, source_target_pairs={{0,9},{1,8},{2,11},{3,10},{8,1},{9,0},{10,3},{11,2},{16,25},{17,24... | collective-permute-start | bytes 491528 | tf_op jit(solution)/shard_map/ppermute | solution.py:449
  54.5 0.0 collective-permute-done.4.rest_4_
  54.5 1.5 %collective-permute-start.6 = (bf16[640,128]{1,0:T(8,128)(2,1)}, bf16[640,128]{1,0:T(8,128)(2,1)S(1)}, u32[]{:S(2)}, u32[]{:S(2)}) collective-permute-start(bf16[640,128]{1,0:T(8,128)(2,1)} %get-tuple-element.45), channel_id=1, source_target_pairs={{0,10},{1,11},{2,8},{3,9},{8,2},{9,3},{10,0},{11,1},{16,26},{17,27... | collective-permute-start | bytes 491528 | tf_op jit(solution)/shard_map/ppermute | solution.py:449
  56.0 0.0 collective-permute-done.8.rest_8_
  56.0 1.5 %collective-permute-start.9 = (bf16[640,128]{1,0:T(8,128)(2,1)}, bf16[640,128]{1,0:T(8,128)(2,1)S(1)}, u32[]{:S(2)}, u32[]{:S(2)}) collective-permute-start(bf16[640,128]{1,0:T(8,128)(2,1)} %get-tuple-element.48), channel_id=1, source_target_pairs={{0,17},{1,16},{2,19},{3,18},{8,25},{9,24},{10,27},{11,26},{16,1},{... | collective-permute-start | bytes 491528 | tf_op jit(solution)/shard_map/ppermute | solution.py:449
  57.4 5.4 %gather_slabs.5 = (bf16[640,128]{1,0:T(8,128)(2,1)}, bf16[640,128]{1,0:T(8,128)(2,1)}, bf16[640,128]{1,0:T(8,128)(2,1)}, bf16[640,128]{1,0:T(8,128)(2,1)}) custom-call(s32[2]{0:T(128)} %pad_add_fusion.here_ref, s32[12288]{0:T(1024)} %bitcast.11, bf16[8192,128]{1,0:T(8,128)(2,1)} %table_ref.7), custom_call_target="tpu_custom_call" | custom-call | tf_op jit(solution)/shard_map/gather_slabs/pallas_call | solution.py:248
  62.9 0.0 collective-permute-done.10.rest_10_
  62.9 2.4 %collective-permute-start.11 = (bf16[640,128]{1,0:T(8,128)(2,1)}, bf16[640,128]{1,0:T(8,128)(2,1)S(1)}, u32[]{:S(2)}, u32[]{:S(2)}) collective-permute-start(bf16[640,128]{1,0:T(8,128)(2,1)} %get-tuple-element.50), channel_id=1, source_target_pairs={{0,19},{1,18},{2,17},{3,16},{8,27},{9,26},{10,25},{11,24},{16,3},{... | collective-permute-start | bytes 491528 | tf_op jit(solution)/shard_map/ppermute | solution.py:449
  65.3 0.6 collective-permute-done.12.rest_12_
  66.0 1.2 %collective-permute-start.13 = (bf16[640,128]{1,0:T(8,128)(2,1)}, bf16[640,128]{1,0:T(8,128)(2,1)}, u32[]{:S(2)}, u32[]{:S(2)}) collective-permute-start(bf16[640,128]{1,0:T(8,128)(2,1)} %get-tuple-element.52), channel_id=1, source_target_pairs={{0,25},{1,24},{2,27},{3,26},{8,17},{9,16},{10,19},{11,18},{16,9},{... | collective-permute-start | bytes 491528 | tf_op jit(solution)/shard_map/ppermute | solution.py:449
  67.1 0.9 collective-permute-start.14
  68.0 0.0 collective-permute-done.6.rest_6_
  68.0 1.5 %collective-permute-start.7 = (bf16[640,128]{1,0:T(8,128)(2,1)}, bf16[640,128]{1,0:T(8,128)(2,1)}, u32[]{:S(2)}, u32[]{:S(2)}) collective-permute-start(bf16[640,128]{1,0:T(8,128)(2,1)} %get-tuple-element.46), channel_id=1, source_target_pairs={{0,11},{1,10},{2,9},{3,8},{8,3},{9,2},{10,1},{11,0},{16,27},{17,26... | collective-permute-start | bytes 491528 | tf_op jit(solution)/shard_map/ppermute | solution.py:449
  69.4 0.0 collective-permute-done.9.rest_9_
  69.5 1.8 %collective-permute-start.15 = (bf16[640,128]{1,0:T(8,128)(2,1)}, bf16[640,128]{1,0:T(8,128)(2,1)}, u32[]{:S(2)}, u32[]{:S(2)}) collective-permute-start(bf16[640,128]{1,0:T(8,128)(2,1)} %get-tuple-element.54), channel_id=1, source_target_pairs={{0,27},{1,26},{2,25},{3,24},{8,19},{9,18},{10,17},{11,16},{16,11},... | collective-permute-start | bytes 491528 | tf_op jit(solution)/shard_map/ppermute | solution.py:449
  71.2 0.6 reshape.23.wo
  71.8 2.1 %plan_rows.1 = (s32[96,128]{1,0:T(8,128)}, s32[40,128]{1,0:T(8,128)}, s32[32,256]{1,0:T(8,128)}, s32[32,128]{1,0:T(8,128)}, s32[32,256]{1,0:T(8,128)}) custom-call(s32[2]{0:T(128)} %pad_add_fusion.here_ref, s32[16,384]{1,0:T(8,128)} %get-tuple-element.31.ids_ref, s32[16,384]{1,0:T(8,128)S(1)} %collective-permute-done.mate_ref), custom_call_target="tpu_custom_call" | custom-call | tf_op jit(solution)/shard_map/plan_rows/pallas_call | solution.py:193
  73.9 0.0 all-to-all-done.1
  73.9 3.4 %arrange_past.1.past_ref = bf16[4096,128]{1,0:T(8,128)(2,1)S(1)} custom-call(s32[32,128]{1,0:T(8,128)} %get-tuple-element.36.slot_ref, bf16[2304,128]{1,0:T(8,128)(2,1)S(1)} %bitcast.7), custom_call_target="tpu_custom_call" | custom-call | tf_op jit(solution)/shard_map/arrange_past/pallas_call | solution.py:279
  77.4 5.7 %collective-permute-done.13.rest_13_ = bf16[640,128]{1,0:T(8,128)(2,1)} collective-permute-done((bf16[640,128]{1,0:T(8,128)(2,1)}, bf16[640,128]{1,0:T(8,128)(2,1)}, u32[]{:S(2)}, u32[]{:S(2)}) %collective-permute-start.13) | collective-permute-done | bytes 163872 | tf_op jit(solution)/shard_map/ppermute | solution.py:449
  83.0 0.0 collective-permute-done.14.rest_14_
  83.0 0.0 collective-permute-done.7.rest_7_
  83.0 0.6 collective-permute-done.15.rest_15_
  83.7 13.6 %score_rows.1 = (f32[16,256]{1,0:T(8,128)}, f32[16,256]{1,0:T(8,128)}) custom-call(s32[96,128]{1,0:T(8,128)} %get-tuple-element.32.seg_ref, s32[40,128]{1,0:T(8,128)} %get-tuple-element.33.base_ref, s32[32,256]{1,0:T(8,128)} %get-tuple-element.34.rel_ref, s32[32,256]{1,0:T(8,128)} %get-tuple-element.35.mine_ref, bf16[4096,128]{1,0:T(8,128)(2,1)S(1)} %arrange_past.1.past_ref, ...), custom_call_target="tpu_custom_call" | custom-call | tf_op jit(solution)/shard_map/score_rows/pallas_call | solution.py:381
  97.3 0.0 collective-permute-start.16
  97.4 4.8 %collective-permute-done.16 = f32[16,256]{1,0:T(8,128)S(1)} collective-permute-done((f32[16,256]{1,0:T(8,128)}, f32[16,256]{1,0:T(8,128)S(1)}, u32[]{:S(2)}, u32[]{:S(2)}) %collective-permute-start.16) | collective-permute-done | bytes 16416 | tf_op jit(solution)/shard_map/ppermute | solution.py:455
  102.2 1.3 %add.7 = f32[16,256]{1,0:T(8,128)} add(f32[16,256]{1,0:T(8,128)} %get-tuple-element.55, f32[16,256]{1,0:T(8,128)S(1)} %collective-permute-done.16) | non-fusion elementwise | flops 4096 | bytes 49152 | tf_op jit(solution)/shard_map/add | solution.py:456
  (19 shorter events, 0.0 us)
Async XLA Ops:
  4.6 23.1 %copy-start.7 = (s32[16,384]{1,0:T(8,128)S(1)}, s32[16,384]{1,0:T(8,128)}, u32[]{:S(2)}) copy-start(s32[16,384]{1,0:T(8,128)} %get-tuple-element.31.ids_ref) | copy-start | bytes 73732
  4.6 14.6 %all-to-all-start = ((s32[32,1,384]{2,1,0:T(1,128)}), s32[32,1,384]{2,1,0:T(1,128)S(1)}, u32[]{:S(2)}, u32[]{:S(2)}) async-start(s32[32,1,384]{2,1,0:T(1,128)} %get-tuple-element.37), calls=%async_computation | async-start | bytes 98304 | tf_op jit(solution)/shard_map/all_to_all | solution.py:424
  19.2 0.6 copy-start
  25.0 48.9 %all-to-all-start.1 = ((bf16[32,72,128]{2,1,0:T(8,128)(2,1)}), bf16[32,72,128]{2,1,0:T(8,128)(2,1)S(1)}, u32[]{:S(2)}, u32[]{:S(2)}) async-start(bf16[32,72,128]{2,1,0:T(8,128)(2,1)} %bitcast.12), calls=%async_computation.1 | async-start | bytes 1179648 | tf_op jit(solution)/shard_map/all_to_all | solution.py:445
  27.7 17.4 %collective-permute-start = (s32[16,384]{1,0:T(8,128)S(1)}, s32[16,384]{1,0:T(8,128)S(1)}, u32[]{:S(2)}, u32[]{:S(2)}) collective-permute-start(s32[16,384]{1,0:T(8,128)S(1)} %copy-done.7), channel_id=1, source_target_pairs={{0,4},{4,0},{1,5},{5,1},{2,6},{6,2},{3,7},{7,3},{8,12},{12,8},{9,1... | collective-permute-start | bytes 73736 | tf_op jit(solution)/shard_map/ppermute | solution.py:428
  37.2 15.5 %collective-permute-start.1 = (bf16[640,128]{1,0:T(8,128)(2,1)}, bf16[640,128]{1,0:T(8,128)(2,1)S(1)}, u32[]{:S(2)}, u32[]{:S(2)}) collective-permute-start(bf16[640,128]{1,0:T(8,128)(2,1)} %get-tuple-element.40), channel_id=1, source_target_pairs={{0,1},{1,0},{2,3},{3,2},{8,9},{9,8},{10,11},{11,10},{16,17},{17,16... | collective-permute-start | bytes 491528 | tf_op jit(solution)/shard_map/ppermute | solution.py:449
  38.7 14.0 %collective-permute-start.2 = (bf16[640,128]{1,0:T(8,128)(2,1)}, bf16[640,128]{1,0:T(8,128)(2,1)S(1)}, u32[]{:S(2)}, u32[]{:S(2)}) collective-permute-start(bf16[640,128]{1,0:T(8,128)(2,1)} %get-tuple-element.41), channel_id=1, source_target_pairs={{0,2},{1,3},{2,0},{3,1},{8,10},{9,11},{10,8},{11,9},{16,18},{17,19... | collective-permute-start | bytes 491528 | tf_op jit(solution)/shard_map/ppermute | solution.py:449
  40.2 12.6 %collective-permute-start.3 = (bf16[640,128]{1,0:T(8,128)(2,1)}, bf16[640,128]{1,0:T(8,128)(2,1)S(1)}, u32[]{:S(2)}, u32[]{:S(2)}) collective-permute-start(bf16[640,128]{1,0:T(8,128)(2,1)} %get-tuple-element.42), channel_id=1, source_target_pairs={{0,3},{1,2},{2,1},{3,0},{8,11},{9,10},{10,9},{11,8},{16,19},{17,18... | collective-permute-start | bytes 491528 | tf_op jit(solution)/shard_map/ppermute | solution.py:449
  40.7 13.8 %collective-permute-start.4 = (bf16[640,128]{1,0:T(8,128)(2,1)}, bf16[640,128]{1,0:T(8,128)(2,1)S(1)}, u32[]{:S(2)}, u32[]{:S(2)}) collective-permute-start(bf16[640,128]{1,0:T(8,128)(2,1)} %get-tuple-element.43), channel_id=1, source_target_pairs={{0,8},{1,9},{2,10},{3,11},{8,0},{9,1},{10,2},{11,3},{16,24},{17,25... | collective-permute-start | bytes 491528 | tf_op jit(solution)/shard_map/ppermute | solution.py:449
  45.1 26.2 %copy-start.8 = (bf16[512]{0:T(512)(128)(2,1)S(1)}, bf16[512]{0:T(512)(128)(2,1)}, u32[]{:S(2)}) copy-start(bf16[512]{0:T(512)(128)(2,1)} %param.15) | copy-start | bytes 3076
  45.1 10.9 %collective-permute-start.8 = (bf16[640,128]{1,0:T(8,128)(2,1)}, bf16[640,128]{1,0:T(8,128)(2,1)S(1)}, u32[]{:S(2)}, u32[]{:S(2)}) collective-permute-start(bf16[640,128]{1,0:T(8,128)(2,1)} %get-tuple-element.47), channel_id=1, source_target_pairs={{0,16},{1,17},{2,18},{3,19},{8,24},{9,25},{10,26},{11,27},{16,0},{... | collective-permute-start | bytes 491528 | tf_op jit(solution)/shard_map/ppermute | solution.py:449
  52.7 10.2 %collective-permute-start.10 = (bf16[640,128]{1,0:T(8,128)(2,1)}, bf16[640,128]{1,0:T(8,128)(2,1)S(1)}, u32[]{:S(2)}, u32[]{:S(2)}) collective-permute-start(bf16[640,128]{1,0:T(8,128)(2,1)} %get-tuple-element.49), channel_id=1, source_target_pairs={{0,18},{1,19},{2,16},{3,17},{8,26},{9,27},{10,24},{11,25},{16,2},{... | collective-permute-start | bytes 491528 | tf_op jit(solution)/shard_map/ppermute | solution.py:449
  52.7 13.2 %collective-permute-start.12 = (bf16[640,128]{1,0:T(8,128)(2,1)}, bf16[640,128]{1,0:T(8,128)(2,1)S(1)}, u32[]{:S(2)}, u32[]{:S(2)}) collective-permute-start(bf16[640,128]{1,0:T(8,128)(2,1)} %get-tuple-element.51), channel_id=1, source_target_pairs={{0,24},{1,25},{2,26},{3,27},{8,16},{9,17},{10,18},{11,19},{16,8},{... | collective-permute-start | bytes 491528 | tf_op jit(solution)/shard_map/ppermute | solution.py:449
  52.8 14.3 %collective-permute-start.5 = (bf16[640,128]{1,0:T(8,128)(2,1)}, bf16[640,128]{1,0:T(8,128)(2,1)S(1)}, u32[]{:S(2)}, u32[]{:S(2)}) collective-permute-start(bf16[640,128]{1,0:T(8,128)(2,1)} %get-tuple-element.44), channel_id=1, source_target_pairs={{0,9},{1,8},{2,11},{3,10},{8,1},{9,0},{10,3},{11,2},{16,25},{17,24... | collective-permute-start | bytes 491528 | tf_op jit(solution)/shard_map/ppermute | solution.py:449
  54.5 13.5 %collective-permute-start.6 = (bf16[640,128]{1,0:T(8,128)(2,1)}, bf16[640,128]{1,0:T(8,128)(2,1)S(1)}, u32[]{:S(2)}, u32[]{:S(2)}) collective-permute-start(bf16[640,128]{1,0:T(8,128)(2,1)} %get-tuple-element.45), channel_id=1, source_target_pairs={{0,10},{1,11},{2,8},{3,9},{8,2},{9,3},{10,0},{11,1},{16,26},{17,27... | collective-permute-start | bytes 491528 | tf_op jit(solution)/shard_map/ppermute | solution.py:449
  56.0 13.5 %collective-permute-start.9 = (bf16[640,128]{1,0:T(8,128)(2,1)}, bf16[640,128]{1,0:T(8,128)(2,1)S(1)}, u32[]{:S(2)}, u32[]{:S(2)}) collective-permute-start(bf16[640,128]{1,0:T(8,128)(2,1)} %get-tuple-element.48), channel_id=1, source_target_pairs={{0,17},{1,16},{2,19},{3,18},{8,25},{9,24},{10,27},{11,26},{16,1},{... | collective-permute-start | bytes 491528 | tf_op jit(solution)/shard_map/ppermute | solution.py:449
  62.9 20.8 %copy-start.1 = (bf16[640,128]{1,0:T(8,128)(2,1)}, bf16[640,128]{1,0:T(8,128)(2,1)S(1)}, u32[]{:S(2)}) copy-start(bf16[640,128]{1,0:T(8,128)(2,1)S(1)} %collective-permute-done.10.rest_10_) | copy-start | bytes 491524
  62.9 14.5 %collective-permute-start.11 = (bf16[640,128]{1,0:T(8,128)(2,1)}, bf16[640,128]{1,0:T(8,128)(2,1)S(1)}, u32[]{:S(2)}, u32[]{:S(2)}) collective-permute-start(bf16[640,128]{1,0:T(8,128)(2,1)} %get-tuple-element.50), channel_id=1, source_target_pairs={{0,19},{1,18},{2,17},{3,16},{8,27},{9,26},{10,25},{11,24},{16,3},{... | collective-permute-start | bytes 491528 | tf_op jit(solution)/shard_map/ppermute | solution.py:449
  66.0 17.7 %copy-start.2 = (bf16[640,128]{1,0:T(8,128)(2,1)}, bf16[640,128]{1,0:T(8,128)(2,1)S(1)}, u32[]{:S(2)}) copy-start(bf16[640,128]{1,0:T(8,128)(2,1)S(1)} %collective-permute-done.12.rest_12_) | copy-start | bytes 491524
  66.0 17.1 %collective-permute-start.13 = (bf16[640,128]{1,0:T(8,128)(2,1)}, bf16[640,128]{1,0:T(8,128)(2,1)}, u32[]{:S(2)}, u32[]{:S(2)}) collective-permute-start(bf16[640,128]{1,0:T(8,128)(2,1)} %get-tuple-element.52), channel_id=1, source_target_pairs={{0,25},{1,24},{2,27},{3,26},{8,17},{9,16},{10,19},{11,18},{16,9},{... | collective-permute-start | bytes 491528 | tf_op jit(solution)/shard_map/ppermute | solution.py:449
  67.1 16.6 %copy-start.3 = (bf16[640,128]{1,0:T(8,128)(2,1)}, bf16[640,128]{1,0:T(8,128)(2,1)S(1)}, u32[]{:S(2)}) copy-start(bf16[640,128]{1,0:T(8,128)(2,1)S(1)} %collective-permute-done.5.rest_5_) | copy-start | bytes 491524
  67.1 15.9 %collective-permute-start.14 = (bf16[640,128]{1,0:T(8,128)(2,1)}, bf16[640,128]{1,0:T(8,128)(2,1)}, u32[]{:S(2)}, u32[]{:S(2)}) collective-permute-start(bf16[640,128]{1,0:T(8,128)(2,1)} %get-tuple-element.53), channel_id=1, source_target_pairs={{0,26},{1,27},{2,24},{3,25},{8,18},{9,19},{10,16},{11,17},{16,10},... | collective-permute-start | bytes 491528 | tf_op jit(solution)/shard_map/ppermute | solution.py:449
  68.0 15.7 %copy-start.4 = (bf16[640,128]{1,0:T(8,128)(2,1)}, bf16[640,128]{1,0:T(8,128)(2,1)S(1)}, u32[]{:S(2)}) copy-start(bf16[640,128]{1,0:T(8,128)(2,1)S(1)} %collective-permute-done.6.rest_6_) | copy-start | bytes 491524
  68.0 15.0 %collective-permute-start.7 = (bf16[640,128]{1,0:T(8,128)(2,1)}, bf16[640,128]{1,0:T(8,128)(2,1)}, u32[]{:S(2)}, u32[]{:S(2)}) collective-permute-start(bf16[640,128]{1,0:T(8,128)(2,1)} %get-tuple-element.46), channel_id=1, source_target_pairs={{0,11},{1,10},{2,9},{3,8},{8,3},{9,2},{10,1},{11,0},{16,27},{17,26... | collective-permute-start | bytes 491528 | tf_op jit(solution)/shard_map/ppermute | solution.py:449
  69.4 14.2 %copy-start.5 = (bf16[640,128]{1,0:T(8,128)(2,1)}, bf16[640,128]{1,0:T(8,128)(2,1)S(1)}, u32[]{:S(2)}) copy-start(bf16[640,128]{1,0:T(8,128)(2,1)S(1)} %collective-permute-done.9.rest_9_) | copy-start | bytes 491524
  69.5 14.2 %collective-permute-start.15 = (bf16[640,128]{1,0:T(8,128)(2,1)}, bf16[640,128]{1,0:T(8,128)(2,1)}, u32[]{:S(2)}, u32[]{:S(2)}) collective-permute-start(bf16[640,128]{1,0:T(8,128)(2,1)} %get-tuple-element.54), channel_id=1, source_target_pairs={{0,27},{1,26},{2,25},{3,24},{8,19},{9,18},{10,17},{11,16},{16,11},... | collective-permute-start | bytes 491528 | tf_op jit(solution)/shard_map/ppermute | solution.py:449
  77.3 6.4 %copy-start.6 = (bf16[640,128]{1,0:T(8,128)(2,1)}, bf16[640,128]{1,0:T(8,128)(2,1)S(1)}, u32[]{:S(2)}) copy-start(bf16[640,128]{1,0:T(8,128)(2,1)S(1)} %collective-permute-done.11.rest_11_) | copy-start | bytes 491524
  97.3 4.9 %collective-permute-start.16 = (f32[16,256]{1,0:T(8,128)}, f32[16,256]{1,0:T(8,128)S(1)}, u32[]{:S(2)}, u32[]{:S(2)}) collective-permute-start(f32[16,256]{1,0:T(8,128)} %get-tuple-element.56), channel_id=1, source_target_pairs={{0,4},{4,0},{1,5},{5,1},{2,6},{6,2},{3,7},{7,3},{8,12},{12,8},{9,1... | collective-permute-start | bytes 49160 | tf_op jit(solution)/shard_map/ppermute | solution.py:455
